TPU v7x, 8 devices: a whole 2x2x1 slice. The times are simulated.
8 devices in a mesh: dp: 1 (over z), tp: 8 (over y, x, core).
Axes of the slice: x: 2, y: 2, z: 1, core: 2. Of those that a mesh axis runs over, the one named last changes fastest.
Arguments:
- tokens: bfloat16 [4, 4096, 1152], P('dp', 'tp')
- ln1_gain: float32 [1152], replicated
- ln1_bias: float32 [1152], replicated
- w_qkv: bfloat16 [1152, 3, 16, 72], P(None, None, 'tp')
- b_qkv: float32 [3, 16, 72], P(None, 'tp')
- w_out: bfloat16 [16, 72, 1152], P('tp')
- b_out: float32 [1152], replicated
- ln2_gain: float32 [1152], replicated
- ln2_bias: float32 [1152], replicated
- w_up: bfloat16 [1152, 4304], P(None, 'tp')
- b_up: float32 [4304], P('tp')
- w_down: bfloat16 [4304, 1152], P('tp')
- b_down: float32 [1152], replicated
- lnf_gain: float32 [1152], replicated
- lnf_bias: float32 [1152], replicated
- probe_vec: bfloat16 [1152], replicated
- map_wq: bfloat16 [1152, 16, 72], replicated
- map_bq: float32 [16, 72], replicated
- map_wkv: bfloat16 [1152, 2, 16, 72], replicated
- map_bkv: float32 [2, 16, 72], replicated
- map_wo: bfloat16 [16, 72, 1152], replicated
- map_bo: float32 [1152], replicated
- map_ln_gain: float32 [1152], replicated
- map_ln_bias: float32 [1152], replicated
- map_w_up: bfloat16 [1152, 4304], replicated
- map_b_up: float32 [4304], replicated
- map_w_down: bfloat16 [4304, 1152], replicated
- map_b_down: float32 [1152], replicated
Outputs:
- output: bfloat16 [4, 1152], P('dp')
All inputs are finite; a program needn't handle non-finite values.
Results may differ from a plain program's by a relative error of at most 0.0105538.
Values are sent between devices in bfloat16 or wider.
A program may use at most 1 GiB of HBM per device.

v0:
```python
import jax
import jax.numpy as jnp
from jax import lax
from jax.sharding import PartitionSpec as P

LN_EPS = 1e-6


def layer_norm(values, gain_vec, bias_vec):
    centered = values - jnp.mean(values, axis=-1, keepdims=True)
    variance = jnp.mean(centered * centered, axis=-1, keepdims=True)
    return centered * lax.rsqrt(variance + LN_EPS) * gain_vec + bias_vec


def project(activations, weight, bias_arr):
    return (jnp.einsum('bnd,dhe->bnhe', activations, weight, preferred_element_type=jnp.float32) + bias_arr).astype(jnp.bfloat16)


def block_attention(query_blk, keys_all, vals_all):
    score_scale = query_blk.shape[-1] ** -0.5
    scores = jnp.einsum('bqhe,bkhe->bhqk', query_blk, keys_all, preferred_element_type=jnp.float32) * score_scale
    weights = jnp.exp(scores - jnp.max(scores, axis=-1, keepdims=True))
    weight_sum = jnp.sum(weights, axis=-1)
    mixed_vals = jnp.einsum('bhqk,bkhe->bqhe', weights.astype(jnp.bfloat16), vals_all, preferred_element_type=jnp.float32)
    return (mixed_vals / jnp.transpose(weight_sum, (0, 2, 1))[..., None]).astype(jnp.bfloat16)


def full_attention(queries, keys_all, vals_all, n_blocks):
    block_len = queries.shape[1] // n_blocks

    def one_block(block_idx):
        query_blk = lax.dynamic_slice_in_dim(queries, block_idx * block_len, block_len, axis=1)
        return block_attention(query_blk, keys_all, vals_all)

    stacked = lax.map(one_block, jnp.arange(n_blocks))
    return jnp.moveaxis(stacked, 0, 1).reshape(queries.shape)


def probe_attention(probe_q, keys_all, vals_all):
    score_scale = probe_q.shape[-1] ** -0.5
    scores = jnp.einsum('he,bnhe->bhn', probe_q, keys_all, preferred_element_type=jnp.float32) * score_scale
    weights = jnp.exp(scores - jnp.max(scores, axis=-1, keepdims=True))
    weight_sum = jnp.sum(weights, axis=-1)
    mixed_vals = jnp.einsum('bhn,bnhe->bhe', weights.astype(jnp.bfloat16), vals_all, preferred_element_type=jnp.float32)
    return (mixed_vals / weight_sum[..., None]).astype(jnp.bfloat16)


def map_tail(pooled_heads, map_wo, map_bo, map_ln_gain, map_ln_bias, map_w_up, map_b_up, map_w_down, map_b_down):
    attn_vec = jnp.einsum('bhe,hed->bd', pooled_heads, map_wo, preferred_element_type=jnp.float32) + map_bo
    map_hidden = layer_norm(attn_vec, map_ln_gain, map_ln_bias).astype(jnp.bfloat16)
    map_act = jax.nn.gelu(jnp.dot(map_hidden, map_w_up, preferred_element_type=jnp.float32) + map_b_up, approximate=True).astype(jnp.bfloat16)
    return (attn_vec + jnp.dot(map_act, map_w_down, preferred_element_type=jnp.float32) + map_b_down).astype(jnp.bfloat16)


def solution(mesh):
    tp_size = mesh.shape['tp']
    in_specs = (P('dp', 'tp', None), P(), P(), P(None, None, 'tp', None), P(None, 'tp', None), P('tp', None, None), P(), P(), P(), P(None, 'tp'), P('tp'), P('tp', None)) + (P(),) * 16

    def local_program(tokens, ln1_gain, ln1_bias, w_qkv, b_qkv, w_out, b_out, ln2_gain, ln2_bias, w_up, b_up, w_down, b_down, lnf_gain, lnf_bias, probe_vec, map_wq, map_bq, map_wkv, map_bkv, map_wo, map_bo, map_ln_gain, map_ln_bias, map_w_up, map_b_up, map_w_down, map_b_down):
        hidden = layer_norm(tokens.astype(jnp.float32), ln1_gain, ln1_bias).astype(jnp.bfloat16)
        hidden_all = lax.all_gather(hidden, 'tp', axis=1, tiled=True)
        queries = project(hidden_all, w_qkv[:, 0], b_qkv[0])
        keys_all = project(hidden_all, w_qkv[:, 1], b_qkv[1])
        vals_all = project(hidden_all, w_qkv[:, 2], b_qkv[2])
        attended = full_attention(queries, keys_all, vals_all, tp_size)
        attn_part = jnp.einsum('bnhe,hed->bnd', attended, w_out, preferred_element_type=jnp.float32).astype(jnp.bfloat16)
        attn_local = lax.psum_scatter(attn_part, 'tp', scatter_dimension=1, tiled=True)
        resid_one = (tokens.astype(jnp.float32) + attn_local.astype(jnp.float32) + b_out).astype(jnp.bfloat16)
        hidden_two = layer_norm(resid_one.astype(jnp.float32), ln2_gain, ln2_bias).astype(jnp.bfloat16)
        hidden_two_all = lax.all_gather(hidden_two, 'tp', axis=1, tiled=True)
        pre_act = jnp.einsum('bnd,df->bnf', hidden_two_all, w_up, preferred_element_type=jnp.float32) + b_up
        activated = jax.nn.gelu(pre_act, approximate=True).astype(jnp.bfloat16)
        mlp_part = jnp.einsum('bnf,fd->bnd', activated, w_down, preferred_element_type=jnp.float32).astype(jnp.bfloat16)
        mlp_local = lax.psum_scatter(mlp_part, 'tp', scatter_dimension=1, tiled=True)
        resid_two = (resid_one.astype(jnp.float32) + mlp_local.astype(jnp.float32) + b_down).astype(jnp.bfloat16)
        encoded = layer_norm(resid_two.astype(jnp.float32), lnf_gain, lnf_bias).astype(jnp.bfloat16)
        probe_q = (jnp.einsum('d,dhe->he', probe_vec, map_wq, preferred_element_type=jnp.float32) + map_bq).astype(jnp.bfloat16)
        kv_local = (jnp.einsum('bnd,dthe->bnthe', encoded, map_wkv, preferred_element_type=jnp.float32) + map_bkv).astype(jnp.bfloat16)
        kv_all = lax.all_gather(kv_local, 'tp', axis=1, tiled=True)
        pooled_heads = probe_attention(probe_q, kv_all[:, :, 0], kv_all[:, :, 1])
        return map_tail(pooled_heads, map_wo, map_bo, map_ln_gain, map_ln_bias, map_w_up, map_b_up, map_w_down, map_b_down)

    return jax.shard_map(local_program, mesh=mesh, in_specs=in_specs, out_specs=P('dp', None), check_vma=False)
```

profile of v0, /device:TPU:0, one launch (start us, length us, event | category | flops | bytes accessed | tf_op | source)
XLA Modules:
  0.0 2006.6 jit_solution(9992669389403088518)
XLA Ops:
  17.3 176.3 %all-gather.4.cloned.1.call-done = bf16[4,4096,1152]{2,1,0:T(8,128)(2,1)} async-done(((bf16[4,512,1152]{2,1,0:T(8,128)(2,1)}), bf16[4,4096,1152]{2,1,0:T(8,128)(2,1)}) %all-gather.4.cloned.1.call-update) | async-done | bytes 37748752 | tf_op jit(solution)/shard_map/all_gather | solution.py:61
  258.4 597.2 %while.10 = (s32[]{:T(128)}, bf16[8,4,512,2,72]{2,4,3,1,0:T(8,128)(2,1)}, s32[8]{0:T(128)S(1)}, bf16[4,4096,2,72]{1,3,2,0:T(8,128)(2,1)}, bf16[4,4096,2,72]{1,3,...) while((s32[]{:T(128)}, ...), condition=%wide.region_5.6_spmd, body=%wide.region_2.5_spmd.sunk | while | flops 4966637568 | bytes 212026016 | solution.py:35
  259.9 26.4 %multiply_reduce_fusion.3 = (f32[4,2,512]{2,1,0:T(2,128)S(1)}, f32[4,2,512,4096]{3,2,1,0:T(8,128)}) fusion(bf16[4,4096,2,72]{1,3,2,0:T(8,128)(2,1)} %get-tuple-element.128, bf16[4,4096,2,72]{1,3,2,0:T(8,128)(2,1)} %get-tuple-element.127, s32[]{:T(128)S(6)} %select_n.4), kind=kOutput, calls=%fused_computation.1.clone.1 | convolution fusion | flops 2449469440 | bytes 72433664 | tf_op jit(solution)/shard_map/while/body/eval_jaxpr/bqhe,bkhe->bhqk/dot_general | solution.py:21
  307.5 25.7 %fusion.171 = bf16[8,4,512,2,72]{2,4,3,1,0:T(8,128)(2,1)} fusion(bf16[8,4,512,2,72]{2,4,3,1,0:T(8,128)(2,1)} %get-tuple-element.115, s32[]{:T(128)} %get-tuple-element.114, bf16[4,4096,2,72]{1,3,2,0:T(8,128)(2,1)} %get-tuple-element.129, f32[4,2,512,4096]{3,2,1,0:T(8,128)} %get-tuple-element.102, f32[4,2,512]{2,1,0:T(2,128)S(1)} %get-tuple-element.103, ...), kind=kOutput, calls=%fused_computation.9.clone.1 | convolution fusion | flops 2466840576 | bytes 72450560 | tf_op jit(solution)/shard_map/while/body/eval_jaxpr/bhqk,bkhe->bqhe/dot_general | solution.py:24
  334.5 26.4 %multiply_reduce_fusion.3 = (f32[4,2,512]{2,1,0:T(2,128)S(1)}, f32[4,2,512,4096]{3,2,1,0:T(8,128)}) fusion(bf16[4,4096,2,72]{1,3,2,0:T(8,128)(2,1)} %get-tuple-element.128, bf16[4,4096,2,72]{1,3,2,0:T(8,128)(2,1)} %get-tuple-element.127, s32[]{:T(128)S(6)} %select_n.4), kind=kOutput, calls=%fused_computation.1.clone.1 | convolution fusion | flops 2449469440 | bytes 72433664 | tf_op jit(solution)/shard_map/while/body/eval_jaxpr/bqhe,bkhe->bhqk/dot_general | solution.py:21
  382.1 25.8 %fusion.171 = bf16[8,4,512,2,72]{2,4,3,1,0:T(8,128)(2,1)} fusion(bf16[8,4,512,2,72]{2,4,3,1,0:T(8,128)(2,1)} %get-tuple-element.115, s32[]{:T(128)} %get-tuple-element.114, bf16[4,4096,2,72]{1,3,2,0:T(8,128)(2,1)} %get-tuple-element.129, f32[4,2,512,4096]{3,2,1,0:T(8,128)} %get-tuple-element.102, f32[4,2,512]{2,1,0:T(2,128)S(1)} %get-tuple-element.103, ...), kind=kOutput, calls=%fused_computation.9.clone.1 | convolution fusion | flops 2466840576 | bytes 72450560 | tf_op jit(solution)/shard_map/while/body/eval_jaxpr/bhqk,bkhe->bqhe/dot_general | solution.py:24
  409.1 26.4 %multiply_reduce_fusion.3 = (f32[4,2,512]{2,1,0:T(2,128)S(1)}, f32[4,2,512,4096]{3,2,1,0:T(8,128)}) fusion(bf16[4,4096,2,72]{1,3,2,0:T(8,128)(2,1)} %get-tuple-element.128, bf16[4,4096,2,72]{1,3,2,0:T(8,128)(2,1)} %get-tuple-element.127, s32[]{:T(128)S(6)} %select_n.4), kind=kOutput, calls=%fused_computation.1.clone.1 | convolution fusion | flops 2449469440 | bytes 72433664 | tf_op jit(solution)/shard_map/while/body/eval_jaxpr/bqhe,bkhe->bhqk/dot_general | solution.py:21
  456.8 25.7 %fusion.171 = bf16[8,4,512,2,72]{2,4,3,1,0:T(8,128)(2,1)} fusion(bf16[8,4,512,2,72]{2,4,3,1,0:T(8,128)(2,1)} %get-tuple-element.115, s32[]{:T(128)} %get-tuple-element.114, bf16[4,4096,2,72]{1,3,2,0:T(8,128)(2,1)} %get-tuple-element.129, f32[4,2,512,4096]{3,2,1,0:T(8,128)} %get-tuple-element.102, f32[4,2,512]{2,1,0:T(2,128)S(1)} %get-tuple-element.103, ...), kind=kOutput, calls=%fused_computation.9.clone.1 | convolution fusion | flops 2466840576 | bytes 72450560 | tf_op jit(solution)/shard_map/while/body/eval_jaxpr/bhqk,bkhe->bqhe/dot_general | solution.py:24
  483.7 26.4 %multiply_reduce_fusion.3 = (f32[4,2,512]{2,1,0:T(2,128)S(1)}, f32[4,2,512,4096]{3,2,1,0:T(8,128)}) fusion(bf16[4,4096,2,72]{1,3,2,0:T(8,128)(2,1)} %get-tuple-element.128, bf16[4,4096,2,72]{1,3,2,0:T(8,128)(2,1)} %get-tuple-element.127, s32[]{:T(128)S(6)} %select_n.4), kind=kOutput, calls=%fused_computation.1.clone.1 | convolution fusion | flops 2449469440 | bytes 72433664 | tf_op jit(solution)/shard_map/while/body/eval_jaxpr/bqhe,bkhe->bhqk/dot_general | solution.py:21
  531.4 25.7 %fusion.171 = bf16[8,4,512,2,72]{2,4,3,1,0:T(8,128)(2,1)} fusion(bf16[8,4,512,2,72]{2,4,3,1,0:T(8,128)(2,1)} %get-tuple-element.115, s32[]{:T(128)} %get-tuple-element.114, bf16[4,4096,2,72]{1,3,2,0:T(8,128)(2,1)} %get-tuple-element.129, f32[4,2,512,4096]{3,2,1,0:T(8,128)} %get-tuple-element.102, f32[4,2,512]{2,1,0:T(2,128)S(1)} %get-tuple-element.103, ...), kind=kOutput, calls=%fused_computation.9.clone.1 | convolution fusion | flops 2466840576 | bytes 72450560 | tf_op jit(solution)/shard_map/while/body/eval_jaxpr/bhqk,bkhe->bqhe/dot_general | solution.py:24
  558.4 26.4 %multiply_reduce_fusion.3 = (f32[4,2,512]{2,1,0:T(2,128)S(1)}, f32[4,2,512,4096]{3,2,1,0:T(8,128)}) fusion(bf16[4,4096,2,72]{1,3,2,0:T(8,128)(2,1)} %get-tuple-element.128, bf16[4,4096,2,72]{1,3,2,0:T(8,128)(2,1)} %get-tuple-element.127, s32[]{:T(128)S(6)} %select_n.4), kind=kOutput, calls=%fused_computation.1.clone.1 | convolution fusion | flops 2449469440 | bytes 72433664 | tf_op jit(solution)/shard_map/while/body/eval_jaxpr/bqhe,bkhe->bhqk/dot_general | solution.py:21
  606.0 25.8 %fusion.171 = bf16[8,4,512,2,72]{2,4,3,1,0:T(8,128)(2,1)} fusion(bf16[8,4,512,2,72]{2,4,3,1,0:T(8,128)(2,1)} %get-tuple-element.115, s32[]{:T(128)} %get-tuple-element.114, bf16[4,4096,2,72]{1,3,2,0:T(8,128)(2,1)} %get-tuple-element.129, f32[4,2,512,4096]{3,2,1,0:T(8,128)} %get-tuple-element.102, f32[4,2,512]{2,1,0:T(2,128)S(1)} %get-tuple-element.103, ...), kind=kOutput, calls=%fused_computation.9.clone.1 | convolution fusion | flops 2466840576 | bytes 72450560 | tf_op jit(solution)/shard_map/while/body/eval_jaxpr/bhqk,bkhe->bqhe/dot_general | solution.py:24
  633.0 26.4 %multiply_reduce_fusion.3 = (f32[4,2,512]{2,1,0:T(2,128)S(1)}, f32[4,2,512,4096]{3,2,1,0:T(8,128)}) fusion(bf16[4,4096,2,72]{1,3,2,0:T(8,128)(2,1)} %get-tuple-element.128, bf16[4,4096,2,72]{1,3,2,0:T(8,128)(2,1)} %get-tuple-element.127, s32[]{:T(128)S(6)} %select_n.4), kind=kOutput, calls=%fused_computation.1.clone.1 | convolution fusion | flops 2449469440 | bytes 72433664 | tf_op jit(solution)/shard_map/while/body/eval_jaxpr/bqhe,bkhe->bhqk/dot_general | solution.py:21
  680.7 25.7 %fusion.171 = bf16[8,4,512,2,72]{2,4,3,1,0:T(8,128)(2,1)} fusion(bf16[8,4,512,2,72]{2,4,3,1,0:T(8,128)(2,1)} %get-tuple-element.115, s32[]{:T(128)} %get-tuple-element.114, bf16[4,4096,2,72]{1,3,2,0:T(8,128)(2,1)} %get-tuple-element.129, f32[4,2,512,4096]{3,2,1,0:T(8,128)} %get-tuple-element.102, f32[4,2,512]{2,1,0:T(2,128)S(1)} %get-tuple-element.103, ...), kind=kOutput, calls=%fused_computation.9.clone.1 | convolution fusion | flops 2466840576 | bytes 72450560 | tf_op jit(solution)/shard_map/while/body/eval_jaxpr/bhqk,bkhe->bqhe/dot_general | solution.py:24
  707.6 26.4 %multiply_reduce_fusion.3 = (f32[4,2,512]{2,1,0:T(2,128)S(1)}, f32[4,2,512,4096]{3,2,1,0:T(8,128)}) fusion(bf16[4,4096,2,72]{1,3,2,0:T(8,128)(2,1)} %get-tuple-element.128, bf16[4,4096,2,72]{1,3,2,0:T(8,128)(2,1)} %get-tuple-element.127, s32[]{:T(128)S(6)} %select_n.4), kind=kOutput, calls=%fused_computation.1.clone.1 | convolution fusion | flops 2449469440 | bytes 72433664 | tf_op jit(solution)/shard_map/while/body/eval_jaxpr/bqhe,bkhe->bhqk/dot_general | solution.py:21
  755.3 25.7 %fusion.171 = bf16[8,4,512,2,72]{2,4,3,1,0:T(8,128)(2,1)} fusion(bf16[8,4,512,2,72]{2,4,3,1,0:T(8,128)(2,1)} %get-tuple-element.115, s32[]{:T(128)} %get-tuple-element.114, bf16[4,4096,2,72]{1,3,2,0:T(8,128)(2,1)} %get-tuple-element.129, f32[4,2,512,4096]{3,2,1,0:T(8,128)} %get-tuple-element.102, f32[4,2,512]{2,1,0:T(2,128)S(1)} %get-tuple-element.103, ...), kind=kOutput, calls=%fused_computation.9.clone.1 | convolution fusion | flops 2466840576 | bytes 72450560 | tf_op jit(solution)/shard_map/while/body/eval_jaxpr/bhqk,bkhe->bqhe/dot_general | solution.py:24
  782.3 26.4 %multiply_reduce_fusion.3 = (f32[4,2,512]{2,1,0:T(2,128)S(1)}, f32[4,2,512,4096]{3,2,1,0:T(8,128)}) fusion(bf16[4,4096,2,72]{1,3,2,0:T(8,128)(2,1)} %get-tuple-element.128, bf16[4,4096,2,72]{1,3,2,0:T(8,128)(2,1)} %get-tuple-element.127, s32[]{:T(128)S(6)} %select_n.4), kind=kOutput, calls=%fused_computation.1.clone.1 | convolution fusion | flops 2449469440 | bytes 72433664 | tf_op jit(solution)/shard_map/while/body/eval_jaxpr/bqhe,bkhe->bhqk/dot_general | solution.py:21
  829.9 25.7 %fusion.171 = bf16[8,4,512,2,72]{2,4,3,1,0:T(8,128)(2,1)} fusion(bf16[8,4,512,2,72]{2,4,3,1,0:T(8,128)(2,1)} %get-tuple-element.115, s32[]{:T(128)} %get-tuple-element.114, bf16[4,4096,2,72]{1,3,2,0:T(8,128)(2,1)} %get-tuple-element.129, f32[4,2,512,4096]{3,2,1,0:T(8,128)} %get-tuple-element.102, f32[4,2,512]{2,1,0:T(2,128)S(1)} %get-tuple-element.103, ...), kind=kOutput, calls=%fused_computation.9.clone.1 | convolution fusion | flops 2466840576 | bytes 72450560 | tf_op jit(solution)/shard_map/while/body/eval_jaxpr/bhqk,bkhe->bqhe/dot_general | solution.py:24
  882.4 216.1 %reduce-scatter.3.cloned.1.call-done = bf16[4,512,1152]{2,1,0:T(8,128)(2,1)} async-done(((bf16[4,4096,1152]{2,1,0:T(8,128)(2,1)}), bf16[4,512,1152]{2,1,0:T(8,128)(2,1)}) %reduce-scatter.3.cloned.1.call-update) | async-done | bytes 4718608 | tf_op jit(solution)/shard_map/reduce_scatter | solution.py:67
  1109.5 173.6 %all-gather.6.cloned.1.call-done = bf16[4,4096,1152]{2,1,0:T(8,128)(2,1)} async-done(((bf16[4,512,1152]{2,1,0:T(8,128)(2,1)}), bf16[4,4096,1152]{2,1,0:T(8,128)(2,1)}) %all-gather.6.cloned.1.call-update) | async-done | bytes 37748752 | tf_op jit(solution)/shard_map/all_gather | solution.py:70
  1283.1 36.1 %fusion.160 = bf16[4,4096,538]{1,2,0:T(8,128)(2,1)} fusion(bf16[4,4096,1152]{2,1,0:T(8,128)(2,1)} %all-gather.6.cloned.1.call-done, f32[538]{0:T(1024)S(1)} %copy-done.22, bf16[1152,538]{0,1:T(8,128)(2,1)} %param.39), kind=kOutput, calls=%fused_computation.36.clone.clone.1 | convolution fusion | flops 20396965888 | bytes 56619624 | tf_op jit(solution)/shard_map/bnd,df->bnf/dot_general | solution.py:71
  1319.2 43.7 %convolution_convert_fusion = bf16[4,4096,1152]{2,1,0:T(8,128)(2,1)} fusion(bf16[538,1152]{1,0:T(8,128)(2,1)S(1)} %copy-done.18, bf16[4,4096,538]{1,2,0:T(8,128)(2,1)} %fusion.160), kind=kOutput, calls=%fused_computation.16 | convolution fusion | flops 20327694336 | bytes 56617472 | tf_op jit(solution)/shard_map/bnf,fd->bnd/dot_general | solution.py:73
  1363.0 216.3 %reduce-scatter.5.cloned.1.call-done = bf16[4,512,1152]{2,1,0:T(8,128)(2,1)} async-done(((bf16[4,4096,1152]{2,1,0:T(8,128)(2,1)}), bf16[4,512,1152]{2,1,0:T(8,128)(2,1)}) %reduce-scatter.5.cloned.1.call-update) | async-done | bytes 4718608 | tf_op jit(solution)/shard_map/reduce_scatter | solution.py:74
  1608.7 345.3 %all-gather.8.cloned.1.call-done = bf16[4,4096,2,16,72]{1,4,3,2,0:T(8,128)(2,1)} async-done(((bf16[4,512,2,16,72]{1,4,3,2,0:T(8,128)(2,1)}), bf16[4,4096,2,16,72]{1,4,3,2,0:T(8,128)(2,1)}) %all-gather.8.cloned.1.call-update) | async-done | bytes 75497488 | tf_op jit(solution)/shard_map/all_gather | solution.py:79
  (108 shorter events, 363.3 us)
Async XLA Ops:
  6.5 1981.0 %copy-start = (bf16[16,72,1152]{2,1,0:T(8,128)(2,1)S(1)}, bf16[16,72,1152]{2,1,0:T(8,128)(2,1)}, u32[]{:S(2)}) copy-start(bf16[16,72,1152]{2,1,0:T(8,128)(2,1)} %param.50) | copy-start | bytes 7962628
  6.5 7.1 copy-start.6
  6.5 7.1 copy-start.5
  6.5 187.0 %all-gather.4.cloned.1.call-start = ((), (), s32[]{:S(2)}) async-start(), calls=%async_computation.2 | async-start | bytes 42467328 | tf_op jit(solution)/shard_map/all_gather | solution.py:61
  6.5 7.1 copy-start.1
  9.8 7.5 copy-start.17
  17.0 1081.4 %reduce-scatter.3.cloned.1.call-start = ((), (), s32[]{:S(2)}) async-start(), calls=%async_computation.3 | async-start | bytes 42467328 | tf_op jit(solution)/shard_map/reduce_scatter | solution.py:67
  881.8 216.6 %copy-start.7 = (f32[1152]{0:T(1024)S(1)}, f32[1152]{0:T(1024)}, u32[]{:S(2)}) copy-start(f32[1152]{0:T(1024)} %param.36) | copy-start | bytes 13828
  881.9 224.2 %copy-start.8 = (f32[1152]{0:T(1024)S(1)}, f32[1152]{0:T(1024)}, u32[]{:S(2)}) copy-start(f32[1152]{0:T(1024)} %param.38) | copy-start | bytes 13828
  881.9 224.2 %copy-start.9 = (f32[1152]{0:T(1024)S(1)}, f32[1152]{0:T(1024)}, u32[]{:S(2)}) copy-start(f32[1152]{0:T(1024)} %param.37) | copy-start | bytes 13828
  881.9 401.2 %all-gather.6.cloned.1.call-start = ((), (), s32[]{:S(2)}) async-start(), calls=%async_computation.4 | async-start | bytes 42467328 | tf_op jit(solution)/shard_map/all_gather | solution.py:70
  1104.0 179.1 %copy-start.22 = (f32[538]{0:T(1024)S(1)}, f32[538]{0:T(1024)}, u32[]{:S(2)}) copy-start(f32[538]{0:T(1024)} %param.40) | copy-start | bytes 6460
  1109.4 470.0 %reduce-scatter.5.cloned.1.call-start = ((), (), s32[]{:S(2)}) async-start(), calls=%async_computation.5 | async-start | bytes 42467328 | tf_op jit(solution)/shard_map/reduce_scatter | solution.py:74
  1283.1 36.1 %copy-start.18 = (bf16[538,1152]{1,0:T(8,128)(2,1)S(1)}, bf16[538,1152]{1,0:T(8,128)(2,1)}, u32[]{:S(2)}) copy-start(bf16[538,1152]{1,0:T(8,128)(2,1)} %param.41) | copy-start | bytes 3718660
  1362.9 216.4 %copy-start.10 = (f32[1152]{0:T(1024)S(1)}, f32[1152]{0:T(1024)}, u32[]{:S(2)}) copy-start(f32[1152]{0:T(1024)} %param.42) | copy-start | bytes 13828
  1363.0 223.4 %copy-start.19 = (f32[2,16,72]{2,1,0:T(8,128)S(1)}, f32[2,16,72]{2,1,0:T(8,128)}, u32[]{:S(2)}) copy-start(f32[2,16,72]{2,1,0:T(8,128)} %param.49) | copy-start | bytes 27652
  1363.0 223.4 %copy-start.20 = (f32[1152]{0:T(1024)S(1)}, f32[1152]{0:T(1024)}, u32[]{:S(2)}) copy-start(f32[1152]{0:T(1024)} %param.44) | copy-start | bytes 13828
  1363.0 223.4 %copy-start.21 = (f32[1152]{0:T(1024)S(1)}, f32[1152]{0:T(1024)}, u32[]{:S(2)}) copy-start(f32[1152]{0:T(1024)} %param.43) | copy-start | bytes 13828
  1363.0 590.9 %all-gather.8.cloned.1.call-start = ((), (), s32[]{:S(2)}) async-start(), calls=%async_computation.6 | async-start | bytes 84934656 | tf_op jit(solution)/shard_map/all_gather | solution.py:79
  1971.7 15.8 copy-start.11
  1971.7 16.9 copy-start.4
  1971.7 16.9 copy-start.12
  1971.7 16.9 copy-start.13
  1971.7 16.9 copy-start.14
  (4 other events, 11.6 us)
Sparse Core Ops, SparseCore 0:
  17.1 176.3 all-gather.3
  882.0 216.3 reduce-scatter.2
  1109.5 173.5 all-gather.5
  1363.1 216.2 reduce-scatter.4
  1605.2 348.6 all-gather.7
where the time goes:
time: 2010 us
  waiting for transfers between devices  1130 us (56%)
  matrix products  647 us (32%)
  other arithmetic  201 us (10%)
    all_gather x1, waiting for transfers between devices, local_program(): kv_all = lax.all_gather(kv_local, 'tp', axis=1, tiled=True)  345 us
    reduce_scatter x1, waiting for transfers between devices, local_program(): lax.psum_scatter(mlp_part, 'tp', scatter_dimension=1, tiled=True)  216 us
    reduce_scatter x1, waiting for transfers between devices, local_program(): lax.psum_scatter(attn_part, 'tp', scatter_dimension=1, tiled=True)  216 us
    dot_general x8, matrix products, block_attention(): jnp.einsum('bqhe,bkhe->bhqk', query_blk, keys_all, preferred_element_type...  211 us
    dot_general x8, matrix products, block_attention(): jnp.einsum('bhqk,bkhe->bqhe', weights.astype(jnp.bfloat16), vals_all, pre...  206 us
    all_gather x1, waiting for transfers between devices, local_program(): hidden_all = lax.all_gather(hidden, 'tp', axis=1, tiled=True)  176 us
    all_gather x1, waiting for transfers between devices, local_program(): hidden_two_all = lax.all_gather(hidden_two, 'tp', axis=1, tiled=True)  174 us
    reduce_sum x8, other arithmetic, block_attention(): weight_sum = jnp.sum(weights, axis=-1)  170 us
  transfers between devices with their start and end apart: 5, of which 5 were waited for; matrix products, arithmetic and copies ran while one was open for 0% of the time, Pallas kernels for 0%

commit v1 on v0

v1 whole, which is shorter than its diff:
```python
import functools

import jax
import jax.numpy as jnp
from jax import lax
from jax.experimental import pallas as pl
from jax.experimental.pallas import tpu as pltpu
from jax.sharding import PartitionSpec as P

LN_EPS = 1e-6
LOG2E = 1.4426950408889634
LANES = 128


def layer_norm(values, gain_vec, bias_vec):
    centered = values - jnp.mean(values, axis=-1, keepdims=True)
    variance = jnp.mean(centered * centered, axis=-1, keepdims=True)
    return centered * lax.rsqrt(variance + LN_EPS) * gain_vec + bias_vec


def round_up(size, multiple):
    return -(-size // multiple) * multiple


def attention_kernel(head_dim, chunk, q_ref, k_ref, v_ref, out_ref, scores_a, scores_b, max_a, max_b, first_out):
    n_keys = k_ref.shape[0]
    block = q_ref.shape[1]
    n_chunks = n_keys // chunk
    exp_scale = head_dim ** -0.5 * LOG2E

    def score_chunk(head, index, scores, running):
        rows = pl.ds(index * chunk, chunk)
        keys = k_ref[rows, head * LANES:(head + 1) * LANES]
        part = jnp.dot(keys, q_ref[head * LANES:(head + 1) * LANES, :], preferred_element_type=jnp.float32)
        scores[rows, :] = part
        part_max = jnp.max(part.reshape(chunk // 8, 8, block), axis=0)
        return part_max if running is None else jnp.maximum(running, part_max)

    def mix_chunk(head, index, scores, peak, total, mixed):
        rows = pl.ds(index * chunk, chunk)
        weights = jnp.exp2((scores[rows, :] - peak) * exp_scale)
        part_total = jnp.sum(weights.reshape(chunk // 8, 8, block), axis=0)
        values = v_ref[head * v_rows:(head + 1) * v_rows, index * chunk:(index + 1) * chunk]
        part_mixed = jnp.dot(values, weights.astype(jnp.bfloat16), preferred_element_type=jnp.float32)
        if total is None:
            return part_total, part_mixed
        return total + part_total, mixed + part_mixed

    v_rows = v_ref.shape[0] // 2

    def overlap(score_head, score_buf, max_buf, mix_head, mix_buf, mix_max):
        running, total, mixed = None, None, None
        peak = jnp.max(mix_max[...], axis=0, keepdims=True)
        for index in range(n_chunks):
            running = score_chunk(score_head, index, score_buf, running)
            total, mixed = mix_chunk(mix_head, index, mix_buf, peak, total, mixed)
        max_buf[...] = running
        return mixed[:head_dim] / jnp.sum(total, axis=0, keepdims=True)

    @pl.when(pl.program_id(0) == 0)
    def _():
        scores_b[...] = jnp.zeros_like(scores_b)
        max_b[...] = jnp.zeros_like(max_b)
        first_out[...] = jnp.zeros_like(first_out)

    second = overlap(0, scores_a, max_a, 1, scores_b, max_b)
    out_ref[0] = jnp.concatenate([first_out[...], second], axis=0).astype(out_ref.dtype)
    first_out[...] = overlap(1, scores_b, max_b, 0, scores_a, max_a)


def image_attention(queries_t, keys, values_t, head_dim, n_blocks):
    n_keys = keys.shape[0]
    block = n_keys // n_blocks
    flops = 2 * 2 * n_keys * n_keys * 2 * LANES
    return pl.pallas_call(
        functools.partial(attention_kernel, head_dim, 256),
        grid=(n_blocks + 1,),
        out_shape=jax.ShapeDtypeStruct((n_blocks, 2 * head_dim, block), jnp.bfloat16),
        in_specs=[
            pl.BlockSpec((queries_t.shape[0], block), lambda i: (0, jnp.minimum(i, n_blocks - 1))),
            pl.BlockSpec(keys.shape, lambda i: (0, 0)),
            pl.BlockSpec(values_t.shape, lambda i: (0, 0)),
        ],
        out_specs=pl.BlockSpec((1, 2 * head_dim, block), lambda i: (jnp.maximum(i - 1, 0), 0, 0)),
        scratch_shapes=[
            pltpu.VMEM((n_keys, block), jnp.float32),
            pltpu.VMEM((n_keys, block), jnp.float32),
            pltpu.VMEM((8, block), jnp.float32),
            pltpu.VMEM((8, block), jnp.float32),
            pltpu.VMEM((head_dim, block), jnp.float32),
        ],
        compiler_params=pltpu.CompilerParams(dimension_semantics=('arbitrary',), vmem_limit_bytes=44 * 1024 * 1024),
        cost_estimate=pl.CostEstimate(flops=flops, bytes_accessed=8 * 1024 * 1024, transcendentals=2 * n_keys * n_keys),
        name='image_attention',
    )(queries_t, keys, values_t)


def map_tail(pooled_heads, map_wo, map_bo, map_ln_gain, map_ln_bias, map_w_up, map_b_up, map_w_down, map_b_down):
    attn_vec = jnp.einsum('bhe,hed->bd', pooled_heads, map_wo, preferred_element_type=jnp.float32) + map_bo
    map_hidden = layer_norm(attn_vec, map_ln_gain, map_ln_bias).astype(jnp.bfloat16)
    map_act = jax.nn.gelu(jnp.dot(map_hidden, map_w_up, preferred_element_type=jnp.float32) + map_b_up, approximate=True).astype(jnp.bfloat16)
    return (attn_vec + jnp.dot(map_act, map_w_down, preferred_element_type=jnp.float32) + map_b_down).astype(jnp.bfloat16)


def solution(mesh):
    tp_size = mesh.shape['tp']
    in_specs = (P('dp', 'tp', None), P(), P(), P(None, None, 'tp', None), P(None, 'tp', None), P('tp', None, None), P(), P(), P(), P(None, 'tp'), P('tp'), P('tp', None)) + (P(),) * 16

    def local_program(tokens, ln1_gain, ln1_bias, w_qkv, b_qkv, w_out, b_out, ln2_gain, ln2_bias, w_up, b_up, w_down, b_down, lnf_gain, lnf_bias, probe_vec, map_wq, map_bq, map_wkv, map_bkv, map_wo, map_bo, map_ln_gain, map_ln_bias, map_w_up, map_b_up, map_w_down, map_b_down):
        n_images, run, width = tokens.shape
        n_heads, head_dim = w_qkv.shape[2:]
        hidden_units = w_up.shape[1]

        gathered = []
        for image in range(n_images):
            hidden = layer_norm(tokens[image].astype(jnp.float32), ln1_gain, ln1_bias).astype(jnp.bfloat16)
            gathered.append(lax.all_gather(hidden, 'tp', axis=0, tiled=True))

        v_rows = round_up(head_dim, 16)
        wk = jnp.pad(w_qkv[:, 1], ((0, 0), (0, 0), (0, LANES - head_dim))).reshape(width, n_heads * LANES)
        bk = jnp.pad(b_qkv[1], ((0, 0), (0, LANES - head_dim))).reshape(n_heads * LANES)
        wq_t = jnp.pad(jnp.transpose(w_qkv[:, 0], (1, 2, 0)), ((0, 0), (0, LANES - head_dim), (0, 0))).reshape(n_heads * LANES, width)
        bq = jnp.pad(b_qkv[0], ((0, 0), (0, LANES - head_dim))).reshape(n_heads * LANES, 1)
        wv_t = jnp.pad(jnp.transpose(w_qkv[:, 2], (1, 2, 0)), ((0, 0), (0, v_rows - head_dim), (0, 0))).reshape(n_heads * v_rows, width)
        bv = jnp.pad(b_qkv[2], ((0, 0), (0, v_rows - head_dim))).reshape(n_heads * v_rows, 1)

        padded = round_up(hidden_units, 32)
        w_up_t = jnp.pad(w_up.T, ((0, padded - hidden_units), (0, 0)))
        w_down_p = jnp.pad(w_down, ((0, padded - hidden_units), (0, 0)))
        b_up_all = lax.all_gather(jnp.pad(b_up, (0, padded - hidden_units)), 'tp', axis=0, tiled=True)
        w_out_all = lax.all_gather(w_out.reshape(n_heads * head_dim, width), 'tp', axis=0, tiled=True)
        w_up_all = lax.all_gather(w_up_t, 'tp', axis=0, tiled=True)
        w_down_all = lax.all_gather(w_down_p, 'tp', axis=0, tiled=True)

        def swap(mixed):
            return lax.all_to_all(mixed, 'tp', split_axis=0, concat_axis=0, tiled=True).reshape(tp_size * n_heads * head_dim, run)

        exchanged = []
        for image in range(n_images):
            h_all = gathered[image]
            if exchanged:
                h_all, mixed = lax.optimization_barrier((h_all, mixed))
                exchanged[-1] = swap(mixed)
            keys = (jnp.dot(h_all, wk, preferred_element_type=jnp.float32) + bk).astype(jnp.bfloat16)
            queries_t = (lax.dot_general(wq_t, h_all, (((1,), (1,)), ((), ())), preferred_element_type=jnp.float32) + bq).astype(jnp.bfloat16)
            values_t = (lax.dot_general(wv_t, h_all, (((1,), (1,)), ((), ())), preferred_element_type=jnp.float32) + bv).astype(jnp.bfloat16)
            mixed = image_attention(queries_t, keys, values_t, head_dim, tp_size)
            exchanged.append(swap(mixed))

        def finish(images):
            outs = []
            for image in images:
                attn_local = lax.dot_general(exchanged[image], w_out_all, (((0,), (0,)), ((), ())), preferred_element_type=jnp.float32)
                outs.append((tokens[image].astype(jnp.float32) + attn_local + b_out).astype(jnp.bfloat16))
            resid_one = jnp.concatenate(outs, axis=0)
            hidden_two = layer_norm(resid_one.astype(jnp.float32), ln2_gain, ln2_bias).astype(jnp.bfloat16)
            pre_act = lax.dot_general(hidden_two, w_up_all, (((1,), (1,)), ((), ())), preferred_element_type=jnp.float32) + b_up_all
            activated = jax.nn.gelu(pre_act, approximate=True).astype(jnp.bfloat16)
            mlp_local = jnp.dot(activated, w_down_all, preferred_element_type=jnp.float32)
            resid_two = (resid_one.astype(jnp.float32) + mlp_local + b_down).astype(jnp.bfloat16)
            return layer_norm(resid_two.astype(jnp.float32), lnf_gain, lnf_bias).astype(jnp.bfloat16)

        encoded = jnp.concatenate([finish(range(n_images - 1)), finish([n_images - 1])], axis=0)

        probe_q = (jnp.einsum('d,dhe->he', probe_vec, map_wq, preferred_element_type=jnp.float32) + map_bq).astype(jnp.bfloat16)
        kv_local = (jnp.einsum('nd,dthe->nthe', encoded, map_wkv, preferred_element_type=jnp.float32) + map_bkv).astype(jnp.bfloat16)
        kv_local = kv_local.reshape(n_images, run, *kv_local.shape[1:])
        scores = jnp.einsum('he,bnhe->bhn', probe_q, kv_local[:, :, 0], preferred_element_type=jnp.float32) * head_dim ** -0.5
        peak = jnp.max(scores, axis=-1, keepdims=True)
        weights = jnp.exp(scores - peak)
        total = jnp.sum(weights, axis=-1, keepdims=True)
        mixed = jnp.einsum('bhn,bnhe->bhe', weights.astype(jnp.bfloat16), kv_local[:, :, 1], preferred_element_type=jnp.float32)
        parts = lax.all_gather(jnp.concatenate([mixed, total, peak], axis=-1), 'tp', axis=0, tiled=False)
        mixed_all, total_all, peak_all = parts[..., :head_dim], parts[..., head_dim:head_dim + 1], parts[..., head_dim + 1:]
        share = jnp.exp(peak_all - jnp.max(peak_all, axis=0, keepdims=True))
        pooled_heads = (jnp.sum(mixed_all * share, axis=0) / jnp.sum(total_all * share, axis=0)).astype(jnp.bfloat16)
        return map_tail(pooled_heads, map_wo, map_bo, map_ln_gain, map_ln_bias, map_w_up, map_b_up, map_w_down, map_b_down)

    return jax.shard_map(local_program, mesh=mesh, in_specs=in_specs, out_specs=P('dp', None), check_vma=False)
```

time: 2010 us -> 564 us (0.28)
  waiting for transfers between devices: 1130 us -> 70.8 us
  matrix products: 647 us -> 191 us
  other arithmetic: 201 us -> 27.1 us
  Pallas kernels: 0 us -> 155 us
  local copies, waits for them, and re-layouts: 11.7 us -> 50.4 us
  blocking collectives: 0 us -> 37.5 us
    all_gather x3 -> x7, waiting for transfers between devices: 695 us -> 45.6 us  [the longest x1 27.5 us: local_program(): w_down_all = lax.all_gather(w_down_p, 'tp', axis=0, tiled=True)]
    dot_general x25 -> x21, matrix products: 632 us -> 162 us  [the longest x2 44.8 us: finish(): jnp.dot(activated, w_down_all, preferred_element_type=jnp.float32)]
    reduce_scatter x2 -> x0, waiting for transfers between devices: 432 us -> none  [the longest x1 216 us: local_program(): lax.psum_scatter(mlp_part, 'tp', scatter_dimension=1, tiled=True)]
    reduce_sum x9 -> x2, other arithmetic: 170 us -> 0.44 us  [the longest x1 0.29 us: local_program(): jnp.sum(total_all * share, axis=0)]
    pallas_call x0 -> x4, Pallas kernels: none -> 155 us  [image_attention(): pl.pallas_call(functools.partial(attention_kernel, head_dim, 256), grid=(...]
    unnamed x0 -> x1, blocking collectives: none -> 25.9 us
    all_to_all x0 -> x4, waiting for transfers between devices: none -> 22.8 us  [swap(): lax.all_to_all(mixed, 'tp', split_axis=0, concat_axis=0, tiled=True)]
  transfers between devices with their start and end apart: 5 -> 11, of which waited for: 5 -> 5; matrix products, arithmetic and copies ran while one was open for 0% -> 26% of each run, Pallas kernels for 0% -> 28%
where the time goes in v1:
time: 564 us; the launch traced here: 560 us
  matrix products  191 us (34%)
  Pallas kernels  155 us (27%)
  waiting for transfers between devices  70.8 us (13%)
  local copies, waits for them, and re-layouts  50.4 us (9%)
  blocking collectives  37.5 us (7%)
  other arithmetic  27.1 us (5%)
  between operations  14.7 us (3%)
  starting transfers between devices  12.8 us (2%)
    pallas_call x4, Pallas kernels, image_attention(): pl.pallas_call(functools.partial(attention_kernel, head_dim, 256), grid=(...  155 us
    dot_general x2, matrix products, finish(): jnp.dot(activated, w_down_all, preferred_element_type=jnp.float32)  44.8 us
    dot_general x1, matrix products, finish(): lax.dot_general(hidden_two, w_up_all, (((1,), (1,)), ((), ())), preferred...  31.4 us
    all_gather x1, waiting for transfers between devices, local_program(): w_down_all = lax.all_gather(w_down_p, 'tp', axis=0, tiled=True)  27.5 us
    unnamed x1, blocking collectives  25.9 us
    all_to_all x4, waiting for transfers between devices, swap(): lax.all_to_all(mixed, 'tp', split_axis=0, concat_axis=0, tiled=True)  22.8 us
    dot_general x4, matrix products, local_program(): jnp.dot(h_all, wk, preferred_element_type=jnp.float32) + bk  21.3 us
    dot_general x4, matrix products, local_program(): lax.dot_general(wq_t, h_all, (((1,), (1,)), ((), ())), preferred_element_...  20.6 us
  transfers between devices with their start and end apart: 11, of which 5 were waited for; matrix products, arithmetic and copies ran while one was open for 26% of the time, Pallas kernels for 28%

profile of v1, /device:TPU:0, one launch (start us, length us, event | category | flops | bytes accessed | tf_op | source)
XLA Modules:
  0.0 559.6 jit_solution(12974314663905540375)
XLA Ops:
  26.6 25.9 %all-reduce.9 = f32[4352]{0:T(1024)S(1)} all-reduce(f32[4352]{0:T(1024)S(1)} %pad_dynamic-update-slice_fusion), channel_id=1, replica_groups=mesh['dp'=1,'tp'=8] {'tp'}, use_global_device_ids=true, to_apply=%add.9 | all-reduce | flops 4352 | bytes 34816
  56.1 16.6 %all-gather.11.cloned.1.call-done = bf16[4096,1152]{1,0:T(8,128)(2,1)} async-done(((bf16[512,1152]{1,0:T(8,128)(2,1)}), bf16[4096,1152]{1,0:T(8,128)(2,1)}) %all-gather.11.cloned.1.call-update) | async-done | bytes 9437200 | tf_op jit(solution)/shard_map/all_gather | solution.py:117
  72.7 10.0 %fusion.32.q_ref = bf16[256,4096]{1,0:T(8,128)(2,1)S(1)} fusion(bf16[256,1152]{1,0:T(8,128)(2,1)S(1)} %bitcast.202, bf16[4096,1152]{1,0:T(8,128)(2,1)} %all-gather.11.cloned.1.call-done, f32[256]{0:T(256)S(1)} %get-tuple-element.54), kind=kOutput, calls=%fused_computation.47 | convolution fusion | flops 2418016256 | bytes 12125184 | tf_op jit(solution)/shard_map/dot_general | solution.py:145
  89.2 38.8 %image_attention.4 = bf16[8,144,512]{2,1,0:T(8,128)(2,1)S(1)} custom-call(bf16[256,4096]{1,0:T(8,128)(2,1)S(1)} %fusion.32.q_ref, bf16[4096,256]{1,0:T(8,128)(2,1)S(1)} %fusion.33.k_ref, bf16[160,4096]{1,0:T(8,128)(2,1)S(1)} %fusion.40.v_ref), custom_call_target="tpu_custom_call" | custom-call | flops 17179869184 | bytes 8388608 | tf_op jit(solution)/shard_map/image_attention/pallas_call | solution.py:75
  129.1 6.8 %fusion.35.k_ref = bf16[4096,256]{1,0:T(8,128)(2,1)S(1)} fusion(bf16[4096,1152]{1,0:T(8,128)(2,1)} %all-gather.9.cloned.1.call-done, bf16[1152,256]{0,1:T(8,128)(2,1)} %bitcast.206, f32[256]{0:T(256)S(1)} %get-tuple-element.53), kind=kOutput, calls=%fused_computation.50 | convolution fusion | flops 2418016256 | bytes 12125184 | tf_op jit(solution)/shard_map/dot_general | solution.py:144
  142.3 39.0 %image_attention.5 = bf16[8,144,512]{2,1,0:T(8,128)(2,1)S(1)} custom-call(bf16[256,4096]{1,0:T(8,128)(2,1)S(1)} %fusion.34.q_ref, bf16[4096,256]{1,0:T(8,128)(2,1)S(1)} %fusion.35.k_ref, bf16[160,4096]{1,0:T(8,128)(2,1)S(1)} %fusion.41.v_ref), custom_call_target="tpu_custom_call" | custom-call | flops 17179869184 | bytes 8388608 | tf_op jit(solution)/shard_map/image_attention/pallas_call | solution.py:75
  182.4 7.2 %fusion.42.v_ref = bf16[160,4096]{1,0:T(8,128)(2,1)S(1)} fusion(bf16[160,1152]{1,0:T(8,128)(2,1)} %bitcast.210, bf16[4096,1152]{1,0:T(8,128)(2,1)} %all-gather.15.cloned.1.call-done, f32[160]{0:T(256)S(1)} %add.392), kind=kOutput, calls=%fused_computation.61 | convolution fusion | flops 1511260160 | bytes 11117184 | tf_op jit(solution)/shard_map/dot_general | solution.py:146
  195.9 38.5 %image_attention.6 = bf16[8,144,512]{2,1,0:T(8,128)(2,1)S(1)} custom-call(bf16[256,4096]{1,0:T(8,128)(2,1)S(1)} %fusion.36.q_ref, bf16[4096,256]{1,0:T(8,128)(2,1)S(1)} %fusion.37.k_ref, bf16[160,4096]{1,0:T(8,128)(2,1)S(1)} %fusion.42.v_ref), custom_call_target="tpu_custom_call" | custom-call | flops 17179869184 | bytes 8388608 | tf_op jit(solution)/shard_map/image_attention/pallas_call | solution.py:75
  240.1 8.1 %fusion.39.k_ref = bf16[4096,256]{1,0:T(8,128)(2,1)} fusion(bf16[4096,1152]{1,0:T(8,128)(2,1)} %all-gather.17.cloned.1.call-done, bf16[1152,256]{0,1:T(8,128)(2,1)} %bitcast.207, f32[256]{0:T(256)S(1)} %get-tuple-element.53), kind=kOutput, calls=%fused_computation.54 | convolution fusion | flops 2418016256 | bytes 12125184 | tf_op jit(solution)/shard_map/dot_general | solution.py:144
  267.8 38.5 %image_attention.7 = bf16[8,144,512]{2,1,0:T(8,128)(2,1)S(1)} custom-call(bf16[256,4096]{1,0:T(8,128)(2,1)S(1)} %copy-done.6, bf16[4096,256]{1,0:T(8,128)(2,1)S(1)} %copy-done.7, bf16[160,4096]{1,0:T(8,128)(2,1)S(1)} %copy-done.5), custom_call_target="tpu_custom_call" | custom-call | flops 17179869184 | bytes 8388608 | tf_op jit(solution)/shard_map/image_attention/pallas_call | solution.py:75
  310.4 5.5 fusion.69
  315.9 4.6 fusion.68
  320.5 19.3 %all-to-all-done = bf16[8,144,512]{2,1,0:T(8,128)(2,1)} async-done(((bf16[8,144,512]{2,1,0:T(8,128)(2,1)}), bf16[8,144,512]{2,1,0:T(8,128)(2,1)}, u32[]{:S(2)}, u32[]{:S(2)}) %all-to-all-start) | async-done | bytes 1179680 | tf_op jit(solution)/shard_map/all_to_all | solution.py:136
  343.2 4.5 fusion.67
  353.3 31.4 %fusion.7.clone.3.clone.4 = bf16[1536,4352]{1,0:T(8,128)(2,1)} fusion(bf16[4352,1152]{1,0:T(8,128)(2,1)} %all-gather.19.cloned.1.call-done, f32[4352]{0:T(1024)S(1)} %all-reduce.9, f32[1152]{0:T(1024)S(1)} %copy-done.42, f32[1152]{0:T(1024)S(1)} %copy-done.43, f32[1536]{0:T(1024)S(1)} %add_rsqrt_fusion.1, ...), kind=kOutput, calls=%fused_computation.8.clone.clone.clone.clone.clone.clone.clone.1 | convolution fusion | flops 15487795200 | bytes 26974208 | tf_op jit(solution)/shard_map/dot_general | solution.py:157
  384.6 27.5 %all-gather.21.cloned.1.call-done = bf16[4352,1152]{1,0:T(8,128)(2,1)} async-done(((bf16[544,1152]{1,0:T(8,128)(2,1)}), bf16[4352,1152]{1,0:T(8,128)(2,1)}) %all-gather.21.cloned.1.call-update) | async-done | bytes 10027024 | tf_op jit(solution)/shard_map/all_gather | solution.py:133
  412.1 24.0 %convert_reduce_fusion.1 = (f32[1536]{0:T(1024)S(1)}, bf16[1536,1152]{1,0:T(8,128)(2,1)S(1)}) fusion(f32[1152]{0:T(1024)S(1)} %copy-done.41, bf16[4352,1152]{1,0:T(8,128)(2,1)} %all-gather.21.cloned.1.call-done, bf16[512,1152]{1,0:T(8,128)(2,1)} %fusion.69, bf16[512,1152]{1,0:T(8,128)(2,1)} %fusion.68, bf16[512,1152]{1,0:T(8,128)(2,1)} %copy-done.13, ...), kind=kOutput, calls=%fused_computation.24 | convolution fusion | flops 15420946432 | bytes 30484992 | tf_op jit(solution)/shard_map/dot_general | solution.py:159
  439.0 4.5 convert_reduce_fusion.2
  445.0 20.9 %fusion.162 = (f32[512]{0:T(512)S(1)}, f32[512,1152]{1,0:T(8,128)}) fusion(f32[1152]{0:T(1024)S(1)} %copy-done.41, bf16[4352,1152]{1,0:T(8,128)(2,1)} %all-gather.21.cloned.1.call-done, bf16[4352,1152]{1,0:T(8,128)(2,1)} %all-gather.19.cloned.1.call-done, f32[4352]{0:T(1024)S(1)} %all-reduce.9, bf16[512,1152]{1,0:T(8,128)(2,1)} %copy-done.14, ...), kind=kOutput, calls=%fused_computation.229 | convolution fusion | flops 10297016320 | bytes 23630336 | tf_op jit(solution)/shard_map/dot_general | solution.py:159
  471.6 14.4 %fusion.44 = f32[2048,2304]{0,1:S(1)} fusion(bf16[1152,2304]{0,1:T(8,128)(2,1)} %bitcast.220, bf16[512,1152]{1,0:T(8,128)(2,1)S(1)} %add_convert_fusion.1, bf16[1536,1152]{1,0:T(8,128)(2,1)S(1)} %fusion.29), kind=kOutput, calls=%fused_computation.65 | convolution fusion | flops 10881073152 | bytes 28901376
  490.3 16.4 %reshape.175 = bf16[4,512,2,16,72]{1,0,4,3,2:T(4,128)(2,1)} reshape(bf16[2048,2,16,72]{0,3,2,1:T(8,128)(2,1)} %add_convert_fusion) | data formatting | bytes 18874368 | tf_op jit(solution)/shard_map/reshape | solution.py:167
  506.7 13.0 %slice_bitcast_fusion = (bf16[4,512,16,72]{1,0,3,2:T(4,128)(2,1)}, bf16[4,512,16,72]{1,0,3,2:T(4,128)(2,1)}) fusion(bf16[4,512,2,16,72]{1,0,4,3,2:T(4,128)(2,1)} %reshape.175), kind=kLoop, calls=%fused_computation.63 | loop fusion | bytes 18874368 | tf_op jit(solution)/shard_map/squeeze | solution.py:172
  527.3 11.6 %all-gather = f32[32,16,74]{2,1,0:T(8,128)S(1)} all-gather(f32[4,16,74]{2,1,0:T(8,128)S(1)} %pad_maximum_fusion.1), channel_id=2, replica_groups=mesh['dp'=1,'tp'=8] {'tp'}, dimensions={0}, use_global_device_ids=true | all-gather | bytes 170496 | tf_op jit(solution)/shard_map/all_gather | solution.py:173
  541.0 11.3 %fusion.107 = bf16[4,1152]{1,0:T(4,128)(2,1)} fusion(f32[4,1152]{1,0:T(4,128)S(1)} %get-tuple-element.48, bf16[4304,1152]{1,0:T(8,128)(2,1)} %param.54, bf16[1152,4304]{0,1:T(8,128)(2,1)} %param.52, f32[4304]{0:T(1024)S(1)} %copy-done.22, f32[1152]{0:T(1024)S(1)} %copy-done.27, f32[1152]{0:T(1024)S(1)} %copy-done.28, f32[1152]{0:T(1024)S(1)} %copy-done.29, ...), kind=kOutput, calls=%fused_computation.144 | convolution fusion | flops 79540352 | bytes 19891552 | tf_op jit(solution)/shard_map/dot_general | solution.py:102
  (179 shorter events, 106.5 us)
Async XLA Ops:
  6.5 533.4 %copy-start = (bf16[16,72,1152]{2,1,0:T(8,128)(2,1)S(1)}, bf16[16,72,1152]{2,1,0:T(8,128)(2,1)}, u32[]{:S(2)}) copy-start(bf16[16,72,1152]{2,1,0:T(8,128)(2,1)} %param.48) | copy-start | bytes 7962628
  6.5 66.1 %all-gather.11.cloned.1.call-start = ((), (), s32[]{:S(2)}) async-start(), calls=%async_computation.5 | async-start | bytes 10616832 | tf_op jit(solution)/shard_map/all_gather | solution.py:117
  15.6 113.5 %all-gather.9.cloned.1.call-start = ((), (), s32[]{:S(2)}) async-start(), calls=%async_computation.4 | async-start | bytes 10616832 | tf_op jit(solution)/shard_map/all_gather | solution.py:117
  16.4 166.0 %all-gather.15.cloned.1.call-start = ((), (), s32[]{:S(2)}) async-start(), calls=%async_computation.7 | async-start | bytes 10616832 | tf_op jit(solution)/shard_map/all_gather | solution.py:117
  17.1 219.8 %all-gather.17.cloned.1.call-start = ((), (), s32[]{:S(2)}) async-start(), calls=%async_computation.8 | async-start | bytes 10616832 | tf_op jit(solution)/shard_map/all_gather | solution.py:117
  17.7 292.7 %all-gather.13.cloned.1.call-start = ((), (), s32[]{:S(2)}) async-start(), calls=%async_computation.6 | async-start | bytes 2985984 | tf_op jit(solution)/shard_map/all_gather | solution.py:131
  18.3 335.0 %all-gather.19.cloned.1.call-start = ((), (), s32[]{:S(2)}) async-start(), calls=%async_computation.9 | async-start | bytes 11280384 | tf_op jit(solution)/shard_map/all_gather | solution.py:132
  20.8 391.2 %all-gather.21.cloned.1.call-start = ((), (), s32[]{:S(2)}) async-start(), calls=%async_computation.10 | async-start | bytes 11280384 | tf_op jit(solution)/shard_map/all_gather | solution.py:133
  23.3 29.2 %copy-start.33 = (bf16[1152]{0:T(1024)(128)(2,1)S(1)}, bf16[1152]{0:T(1024)(128)(2,1)}, u32[]{:S(2)}) copy-start(bf16[1152]{0:T(1024)(128)(2,1)} %param.43) | copy-start | bytes 6916
  24.7 30.8 %copy-start.30 = (f32[16,72]{1,0:T(8,128)S(1)}, f32[16,72]{1,0:T(8,128)}, u32[]{:S(2)}) copy-start(f32[16,72]{1,0:T(8,128)} %param.45) | copy-start | bytes 13828
  236.9 23.4 %all-to-all-start.2 = ((bf16[8,144,512]{2,1,0:T(8,128)(2,1)}), bf16[8,144,512]{2,1,0:T(8,128)(2,1)}, u32[]{:S(2)}, u32[]{:S(2)}) async-start(bf16[8,144,512]{2,1,0:T(8,128)(2,1)} %copy-done.4), calls=%async_computation.2 | async-start | bytes 2359296 | tf_op jit(solution)/shard_map/all_to_all | solution.py:136
  260.3 47.1 %all-to-all-start.1 = ((bf16[8,144,512]{2,1,0:T(8,128)(2,1)}), bf16[8,144,512]{2,1,0:T(8,128)(2,1)}, u32[]{:S(2)}, u32[]{:S(2)}) async-start(bf16[8,144,512]{2,1,0:T(8,128)(2,1)} %copy-done.3), calls=%async_computation.1 | async-start | bytes 2359296 | tf_op jit(solution)/shard_map/all_to_all | solution.py:136
  267.8 42.6 %copy-start.40 = (f32[1152]{0:T(1024)S(1)}, f32[1152]{0:T(1024)}, u32[]{:S(2)}) copy-start(f32[1152]{0:T(1024)} %param.34) | copy-start | bytes 13828
  307.4 32.4 %all-to-all-start = ((bf16[8,144,512]{2,1,0:T(8,128)(2,1)}), bf16[8,144,512]{2,1,0:T(8,128)(2,1)}, u32[]{:S(2)}, u32[]{:S(2)}) async-start(bf16[8,144,512]{2,1,0:T(8,128)(2,1)} %copy-done.1), calls=%async_computation | async-start | bytes 2359296 | tf_op jit(solution)/shard_map/all_to_all | solution.py:136
  339.8 99.2 %all-to-all-start.3 = ((bf16[8,144,512]{2,1,0:T(8,128)(2,1)}), bf16[8,144,512]{2,1,0:T(8,128)(2,1)}, u32[]{:S(2)}, u32[]{:S(2)}) async-start(bf16[8,144,512]{2,1,0:T(8,128)(2,1)} %copy-done.2), calls=%async_computation.3 | async-start | bytes 2359296 | tf_op jit(solution)/shard_map/all_to_all | solution.py:136
  353.2 58.9 %copy-start.41 = (f32[1152]{0:T(1024)S(1)}, f32[1152]{0:T(1024)}, u32[]{:S(2)}) copy-start(f32[1152]{0:T(1024)} %param.40) | copy-start | bytes 13828
  445.0 22.9 %copy-start.20 = (f32[1152]{0:T(1024)S(1)}, f32[1152]{0:T(1024)}, u32[]{:S(2)}) copy-start(f32[1152]{0:T(1024)} %param.42) | copy-start | bytes 13828
  445.0 22.9 %copy-start.21 = (f32[1152]{0:T(1024)S(1)}, f32[1152]{0:T(1024)}, u32[]{:S(2)}) copy-start(f32[1152]{0:T(1024)} %param.41) | copy-start | bytes 13828
  471.6 14.4 %copy-start.23 = (f32[2,16,72]{2,1,0:T(8,128)S(1)}, f32[2,16,72]{2,1,0:T(8,128)}, u32[]{:S(2)}) copy-start(f32[2,16,72]{2,1,0:T(8,128)} %param.47) | copy-start | bytes 27652
  523.4 16.5 %copy-start.26 = (f32[1152]{0:T(1024)S(1)}, f32[1152]{0:T(1024)}, u32[]{:S(2)}) copy-start(f32[1152]{0:T(1024)} %param.49) | copy-start | bytes 13828
  527.2 13.7 %copy-start.22 = (f32[4304]{0:T(1024)S(1)}, f32[4304]{0:T(1024)}, u32[]{:S(2)}) copy-start(f32[4304]{0:T(1024)} %param.53) | copy-start | bytes 51652
  527.2 13.7 %copy-start.27 = (f32[1152]{0:T(1024)S(1)}, f32[1152]{0:T(1024)}, u32[]{:S(2)}) copy-start(f32[1152]{0:T(1024)} %param.55) | copy-start | bytes 13828
  527.2 13.7 %copy-start.28 = (f32[1152]{0:T(1024)S(1)}, f32[1152]{0:T(1024)}, u32[]{:S(2)}) copy-start(f32[1152]{0:T(1024)} %param.51) | copy-start | bytes 13828
  527.2 13.8 %copy-start.29 = (f32[1152]{0:T(1024)S(1)}, f32[1152]{0:T(1024)}, u32[]{:S(2)}) copy-start(f32[1152]{0:T(1024)} %param.50) | copy-start | bytes 13828
  (31 other events, 136.5 us)
Sparse Core Ops, SparseCore 0:
  15.7 56.9 all-gather.10
  74.5 52.9 all-gather.8
  129.3 52.9 all-gather.14
  183.9 52.9 all-gather.16
  238.6 34.7 all-gather.12
  275.0 76.3 all-gather.18
  353.3 58.7 all-gather.20

commit v2 on v0

v2 whole, which is shorter than its diff:
```python
import functools

import jax
import jax.numpy as jnp
from jax import lax
from jax.experimental import pallas as pl
from jax.experimental.layout import Layout, with_layout_constraint
from jax.experimental.pallas import tpu as pltpu
from jax.sharding import PartitionSpec as P

LN_EPS = 1e-6
LOG2E = 1.4426950408889634
LANES = 128


def layer_norm(values, gain_vec, bias_vec):
    centered = values - jnp.mean(values, axis=-1, keepdims=True)
    variance = jnp.mean(centered * centered, axis=-1, keepdims=True)
    return centered * lax.rsqrt(variance + LN_EPS) * gain_vec + bias_vec


def row_major(values):
    return with_layout_constraint(values, Layout(major_to_minor=tuple(range(values.ndim))))


def round_up(size, multiple):
    return -(-size // multiple) * multiple


def attention_kernel(head_dim, chunk, q_ref, k_own_ref, k_far_ref, v_own_ref, v_far_ref, v_own_last_ref, v_far_last_ref, *refs):
    out_ref, scores_a, scores_b, max_a, max_b, first_out = refs[-6:]
    half_keys = k_own_ref.shape[1]
    block = q_ref.shape[1] // 2
    step = pl.program_id(0)
    exp_scale = head_dim ** -0.5 * LOG2E

    def score_chunk(keys_t, queries, rows, scores, running):
        part = lax.dot_general(keys_t, queries, (((0,), (0,)), ((), ())), preferred_element_type=jnp.float32)
        scores[rows, :] = part
        part_max = jnp.max(part.reshape(chunk // 8, 8, block), axis=0)
        return part_max if running is None else jnp.maximum(running, part_max)

    def mix_chunk(values, rows, scores, peak, total, mixed):
        weights = jnp.exp2((scores[rows, :] - peak) * exp_scale)
        part_total = jnp.sum(weights.reshape(chunk // 8, 8, block), axis=0)
        part_mixed = jnp.dot(values, weights.astype(jnp.bfloat16), preferred_element_type=jnp.float32)
        if total is None:
            return part_total, part_mixed
        return total + part_total, mixed + part_mixed

    def overlap(query_slot, score_buf, max_buf, v_own, v_far, mix_buf, mix_max):
        running, total, mixed = None, None, None
        peak = jnp.max(mix_max[...], axis=0, keepdims=True)
        queries = q_ref[:, query_slot * block:(query_slot + 1) * block]
        for half, (k_ref, v_ref) in enumerate(((k_own_ref, v_own), (k_far_ref, v_far))):
            for start in range(0, half_keys, chunk):
                rows = pl.ds(half * half_keys + start, chunk)
                running = score_chunk(k_ref[:, start:start + chunk], queries, rows, score_buf, running)
                total, mixed = mix_chunk(v_ref[:, start:start + chunk], rows, mix_buf, peak, total, mixed)
        max_buf[...] = running
        return mixed / jnp.sum(total, axis=0, keepdims=True)

    def write(rows, values_t):
        filled = jnp.concatenate([values_t, jnp.zeros((LANES - head_dim, block), jnp.float32)], axis=0)
        out_ref[rows, :] = filled.T.astype(out_ref.dtype)

    @pl.when(step == 0)
    def _():
        scores_b[...] = jnp.zeros_like(scores_b)
        max_b[...] = jnp.zeros_like(max_b)
        first_out[...] = jnp.zeros_like(first_out)

    @pl.when(step >= 0)
    def _():
        second = overlap(0, scores_a, max_a, v_own_last_ref, v_far_last_ref, scores_b, max_b)
        write(slice(0, block), first_out[...])
        write(slice(block, 2 * block), second)

    @pl.when(step >= 0)
    def _():
        first_out[...] = overlap(1, scores_b, max_b, v_own_ref, v_far_ref, scores_a, max_a)


def heads_attention(qkv_own, qkv_far, head_dim, heads, place, stride, previous, n_out):
    first, count = heads
    n_own = qkv_own.shape[1]
    pair = n_own // 2
    per_head = n_own // pair
    last = count * per_head - 1
    now = lambda i: first + jnp.minimum(i, last) // per_head
    before = lambda i: first + jnp.maximum(i - 1, 0) // per_head
    whole = (head_dim, n_own)
    in_specs = [
        pl.BlockSpec((head_dim, pair), lambda i: (3 * now(i), jnp.minimum(i, last) % per_head)),
        pl.BlockSpec(whole, lambda i: (3 * now(i) + 1, 0)),
        pl.BlockSpec(whole, lambda i: (3 * now(i) + 1, 0)),
        pl.BlockSpec(whole, lambda i: (3 * now(i) + 2, 0)),
        pl.BlockSpec(whole, lambda i: (3 * now(i) + 2, 0)),
        pl.BlockSpec(whole, lambda i: (3 * before(i) + 2, 0)),
        pl.BlockSpec(whole, lambda i: (3 * before(i) + 2, 0)),
    ]
    operands = [qkv_own, qkv_own, qkv_far, qkv_own, qkv_far, qkv_own, qkv_far]
    aliases = {}
    if previous is not None:
        in_specs.append(pl.BlockSpec(memory_space=pl.ANY))
        operands.append(previous)
        aliases = {7: 0}
    scored = count * n_own * 2 * n_own
    return pl.pallas_call(
        functools.partial(attention_kernel, head_dim, 256),
        grid=(last + 2,),
        out_shape=jax.ShapeDtypeStruct((n_own, n_out * LANES), jnp.bfloat16),
        in_specs=in_specs,
        out_specs=pl.BlockSpec((pair, LANES), lambda i: (jnp.maximum(i - 1, 0) % per_head, place + stride * before(i))),
        scratch_shapes=[
            pltpu.VMEM((2 * n_own, pair // 2), jnp.float32),
            pltpu.VMEM((2 * n_own, pair // 2), jnp.float32),
            pltpu.VMEM((8, pair // 2), jnp.float32),
            pltpu.VMEM((8, pair // 2), jnp.float32),
            pltpu.VMEM((head_dim, pair // 2), jnp.float32),
        ],
        input_output_aliases=aliases,
        compiler_params=pltpu.CompilerParams(dimension_semantics=('arbitrary',), vmem_limit_bytes=40 * 1024 * 1024),
        cost_estimate=pl.CostEstimate(flops=4 * scored * LANES, bytes_accessed=8 * 1024 * 1024, transcendentals=scored),
        name='heads_attention',
    )(*operands)


def map_tail(pooled_heads, map_wo, map_bo, map_ln_gain, map_ln_bias, map_w_up, map_b_up, map_w_down, map_b_down):
    attn_vec = jnp.einsum('bhe,hed->bd', pooled_heads, map_wo, preferred_element_type=jnp.float32) + map_bo
    map_hidden = layer_norm(attn_vec, map_ln_gain, map_ln_bias).astype(jnp.bfloat16)
    map_act = jax.nn.gelu(jnp.dot(map_hidden, map_w_up, preferred_element_type=jnp.float32) + map_b_up, approximate=True).astype(jnp.bfloat16)
    return (attn_vec + jnp.dot(map_act, map_w_down, preferred_element_type=jnp.float32) + map_b_down).astype(jnp.bfloat16)


def solution(mesh):
    tp_size = mesh.shape['tp']
    in_specs = (P('dp', 'tp', None), P(), P(), P(None, None, 'tp', None), P(None, 'tp', None), P('tp', None, None), P(), P(), P(), P(None, 'tp'), P('tp'), P('tp', None)) + (P(),) * 16
    partner = [(device, device ^ 1) for device in range(tp_size)]

    def local_program(tokens, ln1_gain, ln1_bias, w_qkv, b_qkv, w_out, b_out, ln2_gain, ln2_bias, w_up, b_up, w_down, b_down, lnf_gain, lnf_bias, probe_vec, map_wq, map_bq, map_wkv, map_bkv, map_wo, map_bo, map_ln_gain, map_ln_bias, map_w_up, map_b_up, map_w_down, map_b_down):
        n_images, run, width = tokens.shape
        groups, head_dim = w_qkv.shape[2:]
        n_heads = groups * tp_size
        hidden_units = w_up.shape[1]
        own = n_images * run

        resid = row_major(lax.all_to_all(row_major(tokens.reshape(tp_size, own // tp_size, width)), 'tp', split_axis=0, concat_axis=0, tiled=True).reshape(own, width))

        shards = [jnp.transpose(w_qkv[:, :, group], (1, 2, 0)).reshape(3 * head_dim, width) for group in range(groups)]
        padded = round_up(hidden_units, 32)
        w_up_t = jnp.pad(w_up.T, ((0, padded - hidden_units), (0, 0)))
        w_down_p = jnp.pad(w_down, ((0, padded - hidden_units), (0, 0)))
        biases = jnp.concatenate([b_qkv.reshape(-1), b_up])
        biases = jnp.pad(biases, (0, -biases.shape[0] % (8 * LANES))).reshape(8, -1)
        biases = lax.all_gather(biases, 'tp', axis=0, tiled=False).reshape(tp_size, -1)
        b_qkv_all = biases[:, :3 * groups * head_dim].reshape(tp_size, 3, groups, head_dim)
        b_up_all = jnp.pad(biases[:, 3 * groups * head_dim:][:, :hidden_units], ((0, 0), (0, padded - hidden_units))).reshape(tp_size * padded)

        gathered = [lax.all_gather(shards[0], 'tp', axis=0, tiled=True)]
        resid, later, w_out, w_up_t, w_down_p = lax.optimization_barrier((resid, shards[1:], w_out, w_up_t, w_down_p))
        gathered += [lax.all_gather(shard, 'tp', axis=0, tiled=True) for shard in later]
        w_out_all = lax.all_gather(w_out.reshape(groups * head_dim, width), 'tp', axis=0, tiled=True)
        w_up_all = lax.all_gather(w_up_t, 'tp', axis=0, tiled=True)
        w_down_all = lax.all_gather(w_down_p, 'tp', axis=0, tiled=True)

        hidden = row_major(layer_norm(resid.astype(jnp.float32), ln1_gain, ln1_bias).astype(jnp.bfloat16))

        def projections(group, hidden):
            product = lax.dot_general(gathered[group], hidden, (((1,), (1,)), ((), ())), preferred_element_type=jnp.float32)
            qkv_t = (product + b_qkv_all[:, :, group].reshape(-1, 1)).astype(jnp.bfloat16)
            return qkv_t, lax.ppermute(qkv_t, 'tp', partner)

        half = tp_size // 2
        first_group = projections(0, hidden)
        mixed = heads_attention(*first_group, head_dim, (0, half), 0, groups, None, n_heads)
        mixed, hidden_later = lax.optimization_barrier((mixed, hidden))
        second_group = projections(1, hidden_later)
        mixed = heads_attention(*first_group, head_dim, (half, half), 0, groups, mixed, n_heads)
        mixed = heads_attention(*second_group, head_dim, (0, tp_size), 1, groups, mixed, n_heads)

        w_out_rows = jnp.pad(w_out_all.reshape(n_heads, head_dim, width), ((0, 0), (0, LANES - head_dim), (0, 0))).reshape(n_heads * LANES, width)
        attn_local = jnp.dot(mixed, w_out_rows, preferred_element_type=jnp.float32)
        resid_one = row_major((resid.astype(jnp.float32) + attn_local + b_out).astype(jnp.bfloat16))
        hidden_two = layer_norm(resid_one.astype(jnp.float32), ln2_gain, ln2_bias).astype(jnp.bfloat16)
        pre_act = lax.dot_general(hidden_two, w_up_all, (((1,), (1,)), ((), ())), preferred_element_type=jnp.float32) + b_up_all
        activated = jax.nn.gelu(pre_act, approximate=True).astype(jnp.bfloat16)
        mlp_local = jnp.dot(activated, w_down_all, preferred_element_type=jnp.float32)
        resid_two = row_major((resid_one.astype(jnp.float32) + mlp_local + b_down).astype(jnp.bfloat16))
        encoded = layer_norm(resid_two.astype(jnp.float32), lnf_gain, lnf_bias).astype(jnp.bfloat16)

        probe_q = (jnp.dot(probe_vec[None], map_wq.reshape(width, width), preferred_element_type=jnp.float32)[0] + map_bq.reshape(width)).astype(jnp.bfloat16)
        head_of = jnp.arange(width) // head_dim
        on_head = head_of[:, None] == jnp.arange(n_heads)[None]
        probe_cols = jnp.where(on_head, probe_q[:, None], jnp.zeros((), jnp.bfloat16))
        map_keys = (jnp.dot(encoded, map_wkv[:, 0].reshape(width, width), preferred_element_type=jnp.float32) + map_bkv[0].reshape(width)).astype(jnp.bfloat16)
        map_vals = (jnp.dot(encoded, map_wkv[:, 1].reshape(width, width), preferred_element_type=jnp.float32) + map_bkv[1].reshape(width)).astype(jnp.bfloat16)
        scores = lax.dot_general(probe_cols, map_keys, (((0,), (1,)), ((), ())), preferred_element_type=jnp.float32) * head_dim ** -0.5
        peak = jnp.max(scores, axis=-1, keepdims=True)
        weights = jnp.exp(scores - peak)
        total = jnp.sum(weights, axis=-1, keepdims=True)
        every_head = jnp.dot(weights.astype(jnp.bfloat16), map_vals, preferred_element_type=jnp.float32)
        pooled = jnp.sum(jnp.where(on_head.T, every_head, 0.0).reshape(n_heads, n_heads, head_dim), axis=1)
        parts = lax.all_gather(jnp.concatenate([pooled, total, peak], axis=-1), 'tp', axis=0, tiled=False)
        parts = parts.reshape(n_images, tp_size // n_images, n_heads, head_dim + 2)
        pooled_all, total_all, peak_all = parts[..., :head_dim], parts[..., head_dim:head_dim + 1], parts[..., head_dim + 1:]
        share = jnp.exp(peak_all - jnp.max(peak_all, axis=1, keepdims=True))
        pooled_heads = (jnp.sum(pooled_all * share, axis=1) / jnp.sum(total_all * share, axis=1)).astype(jnp.bfloat16)
        return map_tail(pooled_heads, map_wo, map_bo, map_ln_gain, map_ln_bias, map_w_up, map_b_up, map_w_down, map_b_down)

    return jax.shard_map(local_program, mesh=mesh, in_specs=in_specs, out_specs=P('dp', None), check_vma=False)
```

time: 2010 us -> 482 us (0.24)
  waiting for transfers between devices: 1130 us -> 79.5 us
  matrix products: 647 us -> 147 us
  other arithmetic: 201 us -> 16.9 us
  Pallas kernels: 0 us -> 167 us
  blocking collectives: 0 us -> 22.4 us
    all_gather x3 -> x5, waiting for transfers between devices: 695 us -> 0.07 us  [the longest x1 0.02 us: local_program(): w_down_all = lax.all_gather(w_down_p, 'tp', axis=0, tiled=True)]
    dot_general x26 -> x8, matrix products: 635 us -> 135 us  [the longest x1 37.1 us: local_program(): lax.dot_general(hidden_two, w_up_all, (((1,), (1,)), ((), ())), preferred...]
    reduce_scatter x2 -> x0, waiting for transfers between devices: 432 us -> none  [the longest x1 216 us: local_program(): lax.psum_scatter(mlp_part, 'tp', scatter_dimension=1, tiled=True)]
    reduce_sum x9 -> x4, other arithmetic: 170 us -> 0.55 us  [the longest x1 0.22 us: local_program(): jnp.sum(total_all * share, axis=1)]
    pallas_call x0 -> x3, Pallas kernels: none -> 167 us  [heads_attention(): pl.pallas_call(functools.partial(attention_kernel, head_dim, 256), grid=(...]
    all_to_all x0 -> x1, waiting for transfers between devices: none -> 65.8 us  [local_program(): lax.all_to_all(row_major(tokens.reshape(tp_size, own // tp_size, width)),...]
    all_gather x0 -> x2, blocking collectives: none -> 22.4 us  [the longest x1 11.3 us: local_program(): lax.all_gather(biases, 'tp', axis=0, tiled=False).reshape(tp_size, -1)]
  transfers between devices with their start and end apart: 5 -> 8, of which waited for: 5 -> 2; matrix products, arithmetic and copies ran while one was open for 0% -> 23% of each run, Pallas kernels for 0% -> 35%
where the time goes in v2:
time: 482 us; the launch traced here: 473 us
  Pallas kernels  167 us (35%)
  matrix products  147 us (30%)
  waiting for transfers between devices  79.5 us (16%)
  blocking collectives  22.4 us (5%)
  local copies, waits for them, and re-layouts  21.6 us (4%)
  other arithmetic  16.9 us (4%)
  between operations  14.1 us (3%)
    pallas_call x3, Pallas kernels, heads_attention(): pl.pallas_call(functools.partial(attention_kernel, head_dim, 256), grid=(...  167 us
    all_to_all x1, waiting for transfers between devices, local_program(): lax.all_to_all(row_major(tokens.reshape(tp_size, own // tp_size, width)),...  65.8 us
    dot_general x1, matrix products, local_program(): lax.dot_general(hidden_two, w_up_all, (((1,), (1,)), ((), ())), preferred...  37.1 us
    dot_general x1, matrix products, local_program(): jnp.dot(activated, w_down_all, preferred_element_type=jnp.float32)  30 us
    dot_general x2, matrix products, projections(): lax.dot_general(gathered[group], hidden, (((1,), (1,)), ((), ())), prefer...  28.8 us
    dot_general x1, matrix products, local_program(): attn_local = jnp.dot(mixed, w_out_rows, preferred_element_type=jnp.float32)  14.4 us
    ppermute x2, waiting for transfers between devices, projections(): return (qkv_t, lax.ppermute(qkv_t, 'tp', partner))  12.6 us
    dot_general x1, matrix products, local_program(): lax.dot_general(probe_cols, map_keys, (((0,), (1,)), ((), ())), preferred...  12.1 us
  transfers between devices with their start and end apart: 8, of which 2 were waited for; matrix products, arithmetic and copies ran while one was open for 23% of the time, Pallas kernels for 35%

profile of v2, /device:TPU:0, one launch (start us, length us, event | category | flops | bytes accessed | tf_op | source)
XLA Modules:
  0.0 472.7 jit_solution(16794101974095125113)
XLA Ops:
  6.5 2.4 fusion.97
  8.9 4.3 all-to-all-start
  13.3 2.4 pad.19
  15.8 2.4 pad.20
  18.2 65.8 %all-to-all-done = bf16[8,256,1152]{2,1,0:T(8,128)(2,1)} async-done(((bf16[8,256,1152]{2,1,0:T(8,128)(2,1)}), bf16[8,256,1152]{2,1,0:T(8,128)(2,1)}, u32[]{:S(2)}, u32[]{:S(2)}) %all-to-all-start) | async-done | bytes 4718624 | tf_op jit(solution)/shard_map/all_to_all | solution.py:148
  85.4 11.3 %all_gather.26 = f32[8,8,128]{2,1,0:T(8,128)S(1)} all-gather(f32[1,8,128]{2,1,0:T(8,128)S(1)} %fusion.82), channel_id=1, replica_groups=mesh['dp'=1,'tp'=8] {'tp'}, dimensions={0}, use_global_device_ids=true | all-gather | bytes 36864 | tf_op jit(solution)/shard_map/all_gather | solution.py:156
  97.0 3.0 convert_reduce_fusion.1
  100.1 3.7 fusion.19
  103.8 5.0 %fusion.22 = bf16[2048,1152]{1,0:T(8,128)(2,1)} fusion(bf16[2048,1152]{1,0:T(8,128)(2,1)} %bitcast.2, f32[1152]{0:T(1024)S(1)} %copy-done.8, f32[1152]{0:T(1024)S(1)} %copy-done.9, f32[2048]{0:T(1024)S(1)} %add_rsqrt_fusion.2, f32[2048]{0:T(1024)S(1)} %broadcast_multiply_fusion.2), kind=kLoop, calls=%fused_computation.33 | loop fusion | flops 14155776 | bytes 9462784 | tf_op jit(solution)/shard_map/convert_element_type | solution.py:167
  108.8 14.2 %fusion.31.q_ref.k_own_ref.v_own_ref.v_own_last_ref = bf16[1728,2048]{1,0:T(8,128)(2,1)} fusion(f32[1728]{0:T(1024)S(1)} %add.206, bf16[2048,1152]{1,0:T(8,128)(2,1)} %fusion.22, bf16[1728,1152]{1,0:T(8,128)(2,1)} %all-gather.9.cloned.1.call-done), kind=kOutput, calls=%fused_computation.44 | convolution fusion | flops 8160804864 | bytes 15784704 | tf_op jit(solution)/shard_map/dot_general | solution.py:170
  123.1 12.6 %collective-permute-done.k_far_ref.v_far_ref.v_far_last_ref = bf16[1728,2048]{1,0:T(8,128)(2,1)} collective-permute-done((bf16[1728,2048]{1,0:T(8,128)(2,1)}, bf16[1728,2048]{1,0:T(8,128)(2,1)}, u32[]{:S(2)}, u32[]{:S(2)}) %collective-permute-start) | collective-permute-done | bytes 7077920 | tf_op jit(solution)/shard_map/ppermute | solution.py:172
  135.7 43.3 %heads_attention.3.refs_0_ = bf16[2048,2048]{1,0:T(8,128)(2,1)} custom-call(bf16[1728,2048]{1,0:T(8,128)(2,1)} %fusion.31.q_ref.k_own_ref.v_own_ref.v_own_last_ref, bf16[1728,2048]{1,0:T(8,128)(2,1)} %fusion.31.q_ref.k_own_ref.v_own_ref.v_own_last_ref, bf16[1728,2048]{1,0:T(8,128)(2,1)} %collective-permute-done.k_far_ref.v_far_ref.v_far_last_ref, ...), custom_call_target="tpu_custom_call" | custom-call | flops 17179869184 | bytes 8388608 | tf_op jit(solution)/shard_map/heads_attention/pallas_call | solution.py:109
  179.1 14.6 %add_convert_fusion.q_ref.k_own_ref.v_own_ref.v_own_last_ref = bf16[1728,2048]{1,0:T(8,128)(2,1)} fusion(bf16[1728,1152]{1,0:T(8,128)(2,1)} %all-gather.7.cloned.1.call-done, bf16[2048,1152]{1,0:T(8,128)(2,1)} %fusion.22, f32[1728]{0:T(1024)S(1)} %add.209), kind=kOutput, calls=%fused_computation.9 | convolution fusion | flops 8160804864 | bytes 15784704 | tf_op jit(solution)/shard_map/dot_general | solution.py:170
  197.5 5.2 %fusion.96 = (bf16[1152,1,16,72]{0,3,2,1:T(8,128)(2,1)}, bf16[1152,1,16,72]{0,3,2,1:T(8,128)(2,1)}) fusion(bf16[1152,2,16,72]{0,3,2,1:T(8,128)(2,1)} %param.46), kind=kLoop, calls=%fused_computation.129 | loop fusion | bytes 10616832 | tf_op jit(solution)/shard_map/slice | solution.py:197
  202.7 2.4 pad.22
  205.1 43.4 %heads_attention.4.refs_0_ = bf16[2048,2048]{1,0:T(8,128)(2,1)} custom-call(bf16[1728,2048]{1,0:T(8,128)(2,1)} %fusion.31.q_ref.k_own_ref.v_own_ref.v_own_last_ref, bf16[1728,2048]{1,0:T(8,128)(2,1)} %fusion.31.q_ref.k_own_ref.v_own_ref.v_own_last_ref, ...), custom_call_target="tpu_custom_call", output_to_operand_aliasing={{}: (7, {})} | custom-call | flops 17179869184 | bytes 8388608 | tf_op jit(solution)/shard_map/heads_attention/pallas_call | solution.py:109
  248.5 80.0 %heads_attention.5 = bf16[2048,2048]{1,0:T(8,128)(2,1)} custom-call(bf16[1728,2048]{1,0:T(8,128)(2,1)} %add_convert_fusion.q_ref.k_own_ref.v_own_ref.v_own_last_ref, bf16[1728,2048]{1,0:T(8,128)(2,1)} %add_convert_fusion.q_ref.k_own_ref.v_own_ref.v_own_last_ref, ...), custom_call_target="tpu_custom_call", output_to_operand_aliasing={{}: (7, {})} | custom-call | flops 34359738368 | bytes 8388608 | tf_op jit(solution)/shard_map/heads_attention/pallas_call | solution.py:109
  328.5 14.4 %convert_reduce_fusion = (f32[2048]{0:T(1024)S(1)}, bf16[2048,1152]{1,0:T(8,128)(2,1)S(1)}) fusion(f32[1152]{0:T(1024)S(1)} %copy-done.22, bf16[2048,2048]{1,0:T(8,128)(2,1)} %heads_attention.5, bf16[2048,1152]{1,0:T(8,128)(2,1)S(1)} %bitcast.56, bf16[2048,1152]{1,0:T(8,128)(2,1)} %bitcast.2), kind=kOutput, calls=%fused_computation.13 | convolution fusion | flops 9677830144 | bytes 22557184 | tf_op jit(solution)/shard_map/dot_general | solution.py:183
  346.5 37.1 %fusion.7.clone.3.clone.4 = bf16[2048,4352]{1,0:T(8,128)(2,1)} fusion(bf16[4352,1152]{1,0:T(8,128)(2,1)} %all-gather.13.cloned.1.call-done, f32[4352]{0:T(1024)S(1)} %add.218, bf16[2048,1152]{1,0:T(8,128)(2,1)} %copy-done.2, f32[1152]{0:T(1024)S(1)} %copy-done.23, f32[1152]{0:T(1024)S(1)} %copy-done.24, ...), kind=kOutput, calls=%fused_computation.8.clone.clone.clone.clone.clone.clone.clone.1 | convolution fusion | flops 20638597120 | bytes 32614400 | tf_op jit(solution)/shard_map/dot_general | solution.py:186
  383.7 30.0 %convert_reduce_fusion.2 = (f32[2048]{0:T(1024)S(1)}, bf16[2048,1152]{1,0:T(8,128)(2,1)S(1)}) fusion(f32[1152]{0:T(1024)S(1)} %copy-done.25, bf16[4352,1152]{1,0:T(8,128)(2,1)} %all-gather.15.cloned.1.call-done, bf16[2048,1152]{1,0:T(8,128)(2,1)} %copy-done.2, bf16[2048,4352]{1,0:T(8,128)(2,1)} %fusion.7.clone.3.clone.4), kind=kOutput, calls=%fused_computation.19 | convolution fusion | flops 20549466112 | bytes 37302784 | tf_op jit(solution)/shard_map/dot_general | solution.py:188
  417.2 12.1 %fusion.101 = (f32[16]{0:T(128)S(1)}, f32[16,2048]{1,0:T(8,128)S(1)}) fusion(bf16[1152,1152]{0,1:T(8,128)(2,1)S(1)} %bitcast.58, f32[1152]{0:T(1024)S(1)} %copy-done.17, bf16[2048,1152]{1,0:T(8,128)(2,1)} %copy-done.3, f32[1152]{0:T(1024)S(1)} %copy-done.26, f32[1152]{0:T(1024)S(1)} %copy-done.27, f32[2048]{0:T(1024)S(1)} %add_rsqrt_fusion, ...), kind=kOutput, calls=%fused_computation.132 | convolution fusion | flops 5530292224 | bytes 7541056 | tf_op jit(solution)/shard_map/dot_general | solution.py:198
  429.6 11.6 %convolution_select_fusion = f32[16,1152]{1,0:T(8,128)S(1)} fusion(bf16[1152,1152]{0,1:T(8,128)(2,1)} %bitcast.57, f32[1152]{0:T(1024)S(1)} %copy-done.15, f32[16,2048]{1,0:T(8,128)S(1)} %get-tuple-element.34, f32[16]{0:T(128)S(1)} %get-tuple-element.33, s32[1152]{0:T(1024)S(1)} %copy-done.16, bf16[2048,1152]{1,0:T(8,128)(2,1)} %copy-done.3, ...), kind=kOutput, calls=%fused_computation.50 | convolution fusion | flops 5530292224 | bytes 7612480 | tf_op jit(solution)/shard_map/dot_general | solution.py:202
  441.6 11.0 %all-gather = f32[128,74]{1,0:T(8,128)S(1)} all-gather(f32[16,74]{1,0:T(8,128)S(1)} %pad_maximum_fusion), channel_id=2, replica_groups=mesh['dp'=1,'tp'=8] {'tp'}, dimensions={0}, use_global_device_ids=true | all-gather | bytes 42624 | tf_op jit(solution)/shard_map/all_gather | solution.py:204
  454.3 11.4 %fusion.44 = bf16[4,1152]{1,0:T(4,128)(2,1)} fusion(f32[4,1152]{1,0:T(4,128)S(1)} %get-tuple-element.36, bf16[4304,1152]{1,0:T(8,128)(2,1)} %param.54, bf16[1152,4304]{0,1:T(8,128)(2,1)} %param.52, f32[4304]{0:T(1024)S(1)} %copy-done.6, f32[1152]{0:T(1024)S(1)} %copy-done.11, f32[1152]{0:T(1024)S(1)} %copy-done.12, f32[1152]{0:T(1024)S(1)} %copy-done.13, ...), kind=kOutput, calls=%fused_computation.56 | convolution fusion | flops 79540352 | bytes 19891552 | tf_op jit(solution)/shard_map/dot_general | solution.py:133
  (115 shorter events, 14.9 us)
Async XLA Ops:
  6.5 189.5 %copy-start = (bf16[1152,16,72]{0,2,1:T(8,128)(2,1)S(1)}, bf16[1152,16,72]{0,2,1:T(8,128)(2,1)}, u32[]{:S(2)}) copy-start(bf16[1152,16,72]{0,2,1:T(8,128)(2,1)} %param.44) | copy-start | bytes 7962628
  6.5 78.3 %copy-start.21 = (f32[3,2,72]{2,1,0:T(2,128)S(1)}, f32[3,2,72]{2,1,0:T(2,128)}, u32[]{:S(2)}) copy-start(f32[3,2,72]{2,1,0:T(2,128)} %param.32) | copy-start | bytes 5188
  6.5 78.4 %copy-start.19 = (f32[538]{0:T(1024)S(1)}, f32[538]{0:T(1024)}, u32[]{:S(2)}) copy-start(f32[538]{0:T(1024)} %param.38) | copy-start | bytes 6460
  6.5 102.3 %all-gather.9.cloned.1.call-start = ((), (), s32[]{:S(2)}) async-start(), calls=%async_computation.2 | async-start | bytes 4478976 | tf_op jit(solution)/shard_map/all_gather | solution.py:160
  8.9 75.0 %all-to-all-start = ((bf16[8,256,1152]{2,1,0:T(8,128)(2,1)}), bf16[8,256,1152]{2,1,0:T(8,128)(2,1)}, u32[]{:S(2)}, u32[]{:S(2)}) async-start(bf16[8,256,1152]{2,1,0:T(8,128)(2,1)} %bitcast.55), calls=%async_computation | async-start | bytes 9437184 | tf_op jit(solution)/shard_map/all_to_all | solution.py:148
  13.3 90.5 %copy-start.8 = (f32[1152]{0:T(1024)S(1)}, f32[1152]{0:T(1024)}, u32[]{:S(2)}) copy-start(f32[1152]{0:T(1024)} %param.30) | copy-start | bytes 13828
  13.3 90.5 %copy-start.9 = (f32[1152]{0:T(1024)S(1)}, f32[1152]{0:T(1024)}, u32[]{:S(2)}) copy-start(f32[1152]{0:T(1024)} %param.29) | copy-start | bytes 13828
  13.3 165.8 %all-gather.7.cloned.1.call-start = ((), (), s32[]{:S(2)}) async-start(), calls=%async_computation.1 | async-start | bytes 4478976 | tf_op jit(solution)/shard_map/all_gather | solution.py:162
  84.0 118.7 %all-gather.11.cloned.1.call-start = ((), (), s32[]{:S(2)}) async-start(), calls=%async_computation.3 | async-start | bytes 2985984 | tf_op jit(solution)/shard_map/all_gather | solution.py:163
  84.8 261.7 %all-gather.13.cloned.1.call-start = ((), (), s32[]{:S(2)}) async-start(), calls=%async_computation.4 | async-start | bytes 11280384 | tf_op jit(solution)/shard_map/all_gather | solution.py:164
  85.3 298.4 %all-gather.15.cloned.1.call-start = ((), (), s32[]{:S(2)}) async-start(), calls=%async_computation.5 | async-start | bytes 11280384 | tf_op jit(solution)/shard_map/all_gather | solution.py:165
  123.0 12.7 %collective-permute-start = (bf16[1728,2048]{1,0:T(8,128)(2,1)}, bf16[1728,2048]{1,0:T(8,128)(2,1)}, u32[]{:S(2)}, u32[]{:S(2)}) collective-permute-start(bf16[1728,2048]{1,0:T(8,128)(2,1)} %fusion.31.q_ref.k_own_ref.v_own_ref.v_own_last_ref), channel_id=1, source_target_pairs={{0,1},{1,0},{2,3},{3,2},{4,5},{5,4},{6,7},{7,6}} | collective-permute-start | bytes 21233672 | tf_op jit(solution)/shard_map/ppermute | solution.py:172
  193.6 54.9 %collective-permute-start.1 = (bf16[1728,2048]{1,0:T(8,128)(2,1)}, bf16[1728,2048]{1,0:T(8,128)(2,1)}, u32[]{:S(2)}, u32[]{:S(2)}) collective-permute-start(bf16[1728,2048]{1,0:T(8,128)(2,1)} %add_convert_fusion.q_ref.k_own_ref.v_own_ref.v_own_last_ref), channel_id=1, source_target_pairs={{0,1},{1,0},{2,3},{3,2},{4,5},{5,4},{6,7},{7,6}} | collective-permute-start | bytes 21233672 | tf_op jit(solution)/shard_map/ppermute | solution.py:172
  248.5 80.0 %copy-start.22 = (f32[1152]{0:T(1024)S(1)}, f32[1152]{0:T(1024)}, u32[]{:S(2)}) copy-start(f32[1152]{0:T(1024)} %param.34) | copy-start | bytes 13828
  346.4 37.3 %copy-start.25 = (f32[1152]{0:T(1024)S(1)}, f32[1152]{0:T(1024)}, u32[]{:S(2)}) copy-start(f32[1152]{0:T(1024)} %param.40) | copy-start | bytes 13828
  383.6 33.6 %copy-start.5 = (bf16[1152,1,16,72]{0,3,2,1:T(8,128)(2,1)S(1)}, bf16[1152,1,16,72]{0,3,2,1:T(8,128)(2,1)}, u32[]{:S(2)}) copy-start(bf16[1152,1,16,72]{0,3,2,1:T(8,128)(2,1)} %get-tuple-element.24) | copy-start | bytes 7962628
  383.6 33.6 %copy-start.16 = (s32[1152]{0:T(1024)S(1)}, s32[1152]{0:T(1024)}, u32[]{:S(2)}) copy-start(s32[1152]{0:T(1024)} %add_select_fusion) | copy-start | bytes 13828
  383.6 33.6 %copy-start.17 = (f32[1152]{0:T(1024)S(1)}, f32[1152]{0:T(1024)}, u32[]{:S(2)}) copy-start(f32[1152]{0:T(1024)} %add.230) | copy-start | bytes 13828
  383.6 33.6 %copy-start.18 = (bf16[1152]{0:T(1024)(128)(2,1)S(1)}, bf16[1152]{0:T(1024)(128)(2,1)}, u32[]{:S(2)}) copy-start(bf16[1152]{0:T(1024)(128)(2,1)} %add_convert_fusion.7) | copy-start | bytes 6916
  383.6 33.6 %copy-start.26 = (f32[1152]{0:T(1024)S(1)}, f32[1152]{0:T(1024)}, u32[]{:S(2)}) copy-start(f32[1152]{0:T(1024)} %param.42) | copy-start | bytes 13828
  383.7 33.6 %copy-start.27 = (f32[1152]{0:T(1024)S(1)}, f32[1152]{0:T(1024)}, u32[]{:S(2)}) copy-start(f32[1152]{0:T(1024)} %param.41) | copy-start | bytes 13828
  429.6 24.7 %copy-start.6 = (f32[4304]{0:T(1024)S(1)}, f32[4304]{0:T(1024)}, u32[]{:S(2)}) copy-start(f32[4304]{0:T(1024)} %param.53) | copy-start | bytes 51652
  429.6 24.7 %copy-start.11 = (f32[1152]{0:T(1024)S(1)}, f32[1152]{0:T(1024)}, u32[]{:S(2)}) copy-start(f32[1152]{0:T(1024)} %param.55) | copy-start | bytes 13828
  429.6 24.7 %copy-start.12 = (f32[1152]{0:T(1024)S(1)}, f32[1152]{0:T(1024)}, u32[]{:S(2)}) copy-start(f32[1152]{0:T(1024)} %param.51) | copy-start | bytes 13828
  (12 other events, 182.3 us)
Sparse Core Ops, SparseCore 0:
  9.2 61.4 all-gather.8
  84.1 29.3 all-gather.6
  115.4 24.2 all-gather.10
  141.4 56.1 all-gather.12
  199.2 55.4 all-gather.14

commit v3 on v2

--- a/solution.py
+++ b/solution.py
@@ -11,6 +11,7 @@
 LN_EPS = 1e-6
 LOG2E = 1.4426950408889634
 LANES = 128
+BF16_MAX = 3.3895313892515355e38
 
 
 def layer_norm(values, gain_vec, bias_vec):
@@ -28,7 +29,7 @@
 
 
 def attention_kernel(head_dim, chunk, q_ref, k_own_ref, k_far_ref, v_own_ref, v_far_ref, v_own_last_ref, v_far_last_ref, *refs):
-    out_ref, scores_a, scores_b, max_a, max_b, first_out = refs[-6:]
+    out_ref, scores_a, scores_b, max_a, max_b, first_out, apart = refs[-7:]
     half_keys = k_own_ref.shape[1]
     block = q_ref.shape[1] // 2
     step = pl.program_id(0)
@@ -58,7 +59,7 @@
                 running = score_chunk(k_ref[:, start:start + chunk], queries, rows, score_buf, running)
                 total, mixed = mix_chunk(v_ref[:, start:start + chunk], rows, mix_buf, peak, total, mixed)
         max_buf[...] = running
-        return mixed / jnp.sum(total, axis=0, keepdims=True)
+        return mixed[:head_dim] / jnp.sum(total, axis=0, keepdims=True)
 
     def write(rows, values_t):
         filled = jnp.concatenate([values_t, jnp.zeros((LANES - head_dim, block), jnp.float32)], axis=0)
@@ -66,17 +67,18 @@
 
     @pl.when(step == 0)
     def _():
+        apart[0] = 0
         scores_b[...] = jnp.zeros_like(scores_b)
         max_b[...] = jnp.zeros_like(max_b)
         first_out[...] = jnp.zeros_like(first_out)
 
-    @pl.when(step >= 0)
+    @pl.when(apart[0] == 0)
     def _():
         second = overlap(0, scores_a, max_a, v_own_last_ref, v_far_last_ref, scores_b, max_b)
         write(slice(0, block), first_out[...])
         write(slice(block, 2 * block), second)
 
-    @pl.when(step >= 0)
+    @pl.when(apart[0] == 0)
     def _():
         first_out[...] = overlap(1, scores_b, max_b, v_own_ref, v_far_ref, scores_a, max_a)
 
@@ -89,9 +91,10 @@
     last = count * per_head - 1
     now = lambda i: first + jnp.minimum(i, last) // per_head
     before = lambda i: first + jnp.maximum(i - 1, 0) // per_head
-    whole = (head_dim, n_own)
+    rows = round_up(head_dim, 16)
+    whole = (rows, n_own)
     in_specs = [
-        pl.BlockSpec((head_dim, pair), lambda i: (3 * now(i), jnp.minimum(i, last) % per_head)),
+        pl.BlockSpec((rows, pair), lambda i: (3 * now(i), jnp.minimum(i, last) % per_head)),
         pl.BlockSpec(whole, lambda i: (3 * now(i) + 1, 0)),
         pl.BlockSpec(whole, lambda i: (3 * now(i) + 1, 0)),
         pl.BlockSpec(whole, lambda i: (3 * now(i) + 2, 0)),
@@ -118,6 +121,7 @@
             pltpu.VMEM((8, pair // 2), jnp.float32),
             pltpu.VMEM((8, pair // 2), jnp.float32),
             pltpu.VMEM((head_dim, pair // 2), jnp.float32),
+            pltpu.SMEM((1,), jnp.int32),
         ],
         input_output_aliases=aliases,
         compiler_params=pltpu.CompilerParams(dimension_semantics=('arbitrary',), vmem_limit_bytes=40 * 1024 * 1024),
@@ -126,6 +130,39 @@
     )(*operands)
 
 
+def project_kernel(x_ref, gain_ref, shift_ref, weight_ref, bias_ref, out_ref):
+    hidden = layer_norm(x_ref[...].astype(jnp.float32), gain_ref[...], shift_ref[...]).astype(jnp.bfloat16)
+    product = lax.dot_general(weight_ref[...], hidden, (((1,), (1,)), ((), ())), preferred_element_type=jnp.float32)
+    out_ref[...] = (product + bias_ref[...]).astype(out_ref.dtype)
+
+
+def project_tokens(resid, gain, shift, weight, bias, block=256):
+    n_own, width = resid.shape
+    rows = weight.shape[0]
+    fixed = lambda shape: pl.BlockSpec(shape, lambda i: (0, 0))
+    return pl.pallas_call(
+        project_kernel,
+        grid=(n_own // block,),
+        out_shape=jax.ShapeDtypeStruct((rows, n_own), jnp.bfloat16),
+        in_specs=[pl.BlockSpec((block, width), lambda i: (i, 0)), fixed((1, width)), fixed((1, width)), fixed((rows, width)), fixed((rows, 1))],
+        out_specs=pl.BlockSpec((rows, block), lambda i: (0, i)),
+        compiler_params=pltpu.CompilerParams(dimension_semantics=('arbitrary',), vmem_limit_bytes=32 * 1024 * 1024),
+        cost_estimate=pl.CostEstimate(flops=2 * n_own * width * rows, bytes_accessed=2 * (n_own * width + rows * width + rows * n_own), transcendentals=n_own),
+        name='project_tokens',
+    )(resid, gain[None], shift[None], weight, bias)
+
+
+def split_three(values):
+    high = lax.reduce_precision(jnp.clip(values, -BF16_MAX, BF16_MAX), 8, 7)
+    middle = lax.reduce_precision(values - high, 8, 7)
+    return [high.astype(jnp.bfloat16), middle.astype(jnp.bfloat16), (values - high - middle).astype(jnp.bfloat16)]
+
+
+def join_three(parts):
+    high, middle, low = (part.astype(jnp.float32) for part in parts)
+    return high + middle + low
+
+
 def map_tail(pooled_heads, map_wo, map_bo, map_ln_gain, map_ln_bias, map_w_up, map_b_up, map_w_down, map_b_down):
     attn_vec = jnp.einsum('bhe,hed->bd', pooled_heads, map_wo, preferred_element_type=jnp.float32) + map_bo
     map_hidden = layer_norm(attn_vec, map_ln_gain, map_ln_bias).astype(jnp.bfloat16)
@@ -147,15 +184,20 @@
 
         resid = row_major(lax.all_to_all(row_major(tokens.reshape(tp_size, own // tp_size, width)), 'tp', split_axis=0, concat_axis=0, tiled=True).reshape(own, width))
 
-        shards = [jnp.transpose(w_qkv[:, :, group], (1, 2, 0)).reshape(3 * head_dim, width) for group in range(groups)]
+        rows_padded = round_up(head_dim, 16)
+        shards = []
+        for group in range(groups):
+            rows = jnp.transpose(w_qkv[:, :, group], (1, 2, 0))
+            bias_row = jnp.concatenate(split_three(b_qkv[:, group].reshape(3 * head_dim)))
+            bias_row = jnp.pad(bias_row, (0, width - bias_row.shape[0]))[None]
+            extra = jnp.pad(bias_row, ((0, rows_padded - head_dim - 1), (0, 0)))
+            none = jnp.zeros_like(extra)
+            shards.append(jnp.concatenate([rows[0], none, rows[1], none, rows[2], extra], axis=0))
         padded = round_up(hidden_units, 32)
         w_up_t = jnp.pad(w_up.T, ((0, padded - hidden_units), (0, 0)))
-        w_down_p = jnp.pad(w_down, ((0, padded - hidden_units), (0, 0)))
-        biases = jnp.concatenate([b_qkv.reshape(-1), b_up])
-        biases = jnp.pad(biases, (0, -biases.shape[0] % (8 * LANES))).reshape(8, -1)
-        biases = lax.all_gather(biases, 'tp', axis=0, tiled=False).reshape(tp_size, -1)
-        b_qkv_all = biases[:, :3 * groups * head_dim].reshape(tp_size, 3, groups, head_dim)
-        b_up_all = jnp.pad(biases[:, 3 * groups * head_dim:][:, :hidden_units], ((0, 0), (0, padded - hidden_units))).reshape(tp_size * padded)
+        high, middle, low = split_three(b_up)
+        up_rows = jnp.stack([jnp.pad(jnp.concatenate([high, middle]), (0, width - 2 * hidden_units)), jnp.pad(low, (0, width - hidden_units))])
+        w_down_p = jnp.pad(jnp.concatenate([w_down, up_rows], axis=0), ((0, padded - hidden_units - 2), (0, 0)))
 
         gathered = [lax.all_gather(shards[0], 'tp', axis=0, tiled=True)]
         resid, later, w_out, w_up_t, w_down_p = lax.optimization_barrier((resid, shards[1:], w_out, w_up_t, w_down_p))
@@ -164,18 +206,19 @@
         w_up_all = lax.all_gather(w_up_t, 'tp', axis=0, tiled=True)
         w_down_all = lax.all_gather(w_down_p, 'tp', axis=0, tiled=True)
 
-        hidden = row_major(layer_norm(resid.astype(jnp.float32), ln1_gain, ln1_bias).astype(jnp.bfloat16))
-
-        def projections(group, hidden):
-            product = lax.dot_general(gathered[group], hidden, (((1,), (1,)), ((), ())), preferred_element_type=jnp.float32)
-            qkv_t = (product + b_qkv_all[:, :, group].reshape(-1, 1)).astype(jnp.bfloat16)
+        def projections(group, resid):
+            bias_row = gathered[group].reshape(tp_size, 3 * rows_padded, width)[:, 2 * rows_padded + head_dim, :9 * head_dim]
+            bias_row = bias_row.reshape(tp_size, 3, 3, head_dim)
+            bias = join_three([bias_row[:, part] for part in range(3)])
+            bias = jnp.pad(bias, ((0, 0), (0, 0), (0, rows_padded - head_dim))).reshape(-1, 1)
+            qkv_t = project_tokens(resid, ln1_gain, ln1_bias, gathered[group], bias)
             return qkv_t, lax.ppermute(qkv_t, 'tp', partner)
 
         half = tp_size // 2
-        first_group = projections(0, hidden)
+        first_group = projections(0, resid)
         mixed = heads_attention(*first_group, head_dim, (0, half), 0, groups, None, n_heads)
-        mixed, hidden_later = lax.optimization_barrier((mixed, hidden))
-        second_group = projections(1, hidden_later)
+        mixed, resid_later = lax.optimization_barrier((mixed, resid))
+        second_group = projections(1, resid_later)
         mixed = heads_attention(*first_group, head_dim, (half, half), 0, groups, mixed, n_heads)
         mixed = heads_attention(*second_group, head_dim, (0, tp_size), 1, groups, mixed, n_heads)
 
@@ -183,6 +226,9 @@
         attn_local = jnp.dot(mixed, w_out_rows, preferred_element_type=jnp.float32)
         resid_one = row_major((resid.astype(jnp.float32) + attn_local + b_out).astype(jnp.bfloat16))
         hidden_two = layer_norm(resid_one.astype(jnp.float32), ln2_gain, ln2_bias).astype(jnp.bfloat16)
+        bias_rows = w_down_all.reshape(tp_size, padded, width)[:, hidden_units:hidden_units + 2]
+        b_up_all = join_three([bias_rows[:, 0, :hidden_units], bias_rows[:, 0, hidden_units:2 * hidden_units], bias_rows[:, 1, :hidden_units]])
+        b_up_all = jnp.pad(b_up_all, ((0, 0), (0, padded - hidden_units))).reshape(tp_size * padded)
         pre_act = lax.dot_general(hidden_two, w_up_all, (((1,), (1,)), ((), ())), preferred_element_type=jnp.float32) + b_up_all
         activated = jax.nn.gelu(pre_act, approximate=True).astype(jnp.bfloat16)
         mlp_local = jnp.dot(activated, w_down_all, preferred_element_type=jnp.float32)

time: 482 us -> 460 us (0.954)
  matrix products: 147 us -> 118 us
  Pallas kernels: 167 us -> 184 us
  local copies, waits for them, and re-layouts: 21.6 us -> 34.7 us
  blocking collectives: 22.4 us -> 11 us
  other arithmetic: 16.9 us -> 8.96 us
    pallas_call x0 -> x2, Pallas kernels: none -> 33.2 us  [project_tokens(): pl.pallas_call(project_kernel, grid=(n_own // block,), out_shape=jax.Shap...]
    dot_general x2 -> x0, matrix products: 28.8 us -> none  [projections(): lax.dot_general(gathered[group], hidden, (((1,), (1,)), ((), ())), prefer...]
    pallas_call x3, Pallas kernels: 167 us -> 151 us  [heads_attention(): pl.pallas_call(functools.partial(attention_kernel, head_dim, 256), grid=(...]
    all_gather x1 -> x0, blocking collectives: 11.3 us -> none  [local_program(): lax.all_gather(biases, 'tp', axis=0, tiled=False).reshape(tp_size, -1)]
    ppermute x2, waiting for transfers between devices: 12.6 us -> 2.51 us  [projections(): return (qkv_t, lax.ppermute(qkv_t, 'tp', partner))]
    all_gather x1, waiting for transfers between devices: 0.02 us -> 8.14 us  [local_program(): lax.all_gather(shard, 'tp', axis=0, tiled=True)]
    unnamed x58 -> x82, local copies, waits for them, and re-layouts: 4.32 us -> 12.1 us
    convert_element_type x1 -> x3, other arithmetic: 4.99 us -> 0.03 us  [split_three(): high.astype(jnp.bfloat16)]
  transfers between devices with their start and end apart: 8 -> 8, of which waited for: 2 -> 3; matrix products, arithmetic and copies ran while one was open for 23% -> 10% of each run, Pallas kernels for 35% -> 41%
where the time goes in v3:
time: 460 us; the launch traced here: 452 us
  Pallas kernels  184 us (40%)
  matrix products  118 us (26%)
  waiting for transfers between devices  75.3 us (16%)
  local copies, waits for them, and re-layouts  34.7 us (8%)
  between operations  14.1 us (3%)
  blocking collectives  11 us (2%)
  other arithmetic  8.96 us (2%)
  starting transfers between devices  4.73 us (1%)
    pallas_call x3, Pallas kernels, heads_attention(): pl.pallas_call(functools.partial(attention_kernel, head_dim, 256), grid=(...  151 us
    all_to_all x1, waiting for transfers between devices, local_program(): lax.all_to_all(row_major(tokens.reshape(tp_size, own // tp_size, width)),...  63.4 us
    dot_general x1, matrix products, local_program(): lax.dot_general(hidden_two, w_up_all, (((1,), (1,)), ((), ())), preferred...  36.9 us
    pallas_call x2, Pallas kernels, project_tokens(): pl.pallas_call(project_kernel, grid=(n_own // block,), out_shape=jax.Shap...  33.2 us
    dot_general x1, matrix products, local_program(): jnp.dot(activated, w_down_all, preferred_element_type=jnp.float32)  29.9 us
    dot_general x1, matrix products, local_program(): attn_local = jnp.dot(mixed, w_out_rows, preferred_element_type=jnp.float32)  14.8 us
    dot_general x1, matrix products, local_program(): lax.dot_general(probe_cols, map_keys, (((0,), (1,)), ((), ())), preferred...  12.1 us
    unnamed x82, local copies, waits for them, and re-layouts  12.1 us
  transfers between devices with their start and end apart: 8, of which 3 were waited for; matrix products, arithmetic and copies ran while one was open for 10% of the time, Pallas kernels for 41%

profile of v3, /device:TPU:0, one launch (start us, length us, event | category | flops | bytes accessed | tf_op | source)
XLA Modules:
  0.0 451.5 jit_solution(3881059054642710475)
XLA Ops:
  10.5 4.3 all-to-all-start
  15.2 2.5 pad.47
  21.5 2.5 fusion.40
  24.0 63.4 %all-to-all-done = bf16[8,256,1152]{2,1,0:T(8,128)(2,1)} async-done(((bf16[8,256,1152]{2,1,0:T(8,128)(2,1)}), bf16[8,256,1152]{2,1,0:T(8,128)(2,1)}, u32[]{:S(2)}, u32[]{:S(2)}) %all-to-all-start) | async-done | bytes 4718624 | tf_op jit(solution)/shard_map/all_to_all | solution.py:185
  92.5 2.3 copy-done.4
  94.7 16.6 %project_tokens.2.q_ref.k_own_ref.v_own_ref.v_own_last_ref = bf16[1920,2048]{1,0:T(8,128)(2,1)} custom-call(bf16[2048,1152]{1,0:T(8,128)(2,1)} %bitcast.2.x_ref, f32[1,1152]{1,0:T(1,128)S(1)} %broadcast_in_dim.30.gain_ref, f32[1,1152]{1,0:T(1,128)S(1)} %broadcast_in_dim.32.shift_ref, bf16[1920,1152]{1,0:T(8,128)(2,1)S(1)} %copy-done.4, f32[1920,1]{1,0:T(8,128)S(1)} %copy-done.3), custom_call_target="tpu_custom_call" | custom-call | flops 9059696640 | bytes 17006592 | tf_op jit(solution)/shard_map/project_tokens/pallas_call | solution.py:143
  111.3 8.1 %all-gather.9.cloned.1.call-done.weight_ref = bf16[1920,1152]{1,0:T(8,128)(2,1)} async-done(((bf16[240,1152]{1,0:T(8,128)(2,1)}), bf16[1920,1152]{1,0:T(8,128)(2,1)}) %all-gather.9.cloned.1.call-update) | async-done | bytes 4423696 | tf_op jit(solution)/shard_map/all_gather | solution.py:204
  120.5 1.4 reshape.158.bias_ref
  122.0 2.5 collective-permute-done.k_far_ref.v_far_ref.v_far_last_ref
  124.5 39.5 %heads_attention.3.refs_0_ = bf16[2048,2048]{1,0:T(8,128)(2,1)} custom-call(bf16[1920,2048]{1,0:T(8,128)(2,1)} %project_tokens.2.q_ref.k_own_ref.v_own_ref.v_own_last_ref, bf16[1920,2048]{1,0:T(8,128)(2,1)} %project_tokens.2.q_ref.k_own_ref.v_own_ref.v_own_last_ref, bf16[1920,2048]{1,0:T(8,128)(2,1)} %collective-permute-done.k_far_ref.v_far_ref.v_far_last_ref, ...), custom_call_target="tpu_custom_call" | custom-call | flops 17179869184 | bytes 8388608 | tf_op jit(solution)/shard_map/heads_attention/pallas_call | solution.py:112
  164.0 16.7 %project_tokens.3.q_ref.k_own_ref.v_own_ref.v_own_last_ref = bf16[1920,2048]{1,0:T(8,128)(2,1)} custom-call(bf16[2048,1152]{1,0:T(8,128)(2,1)} %bitcast.2.x_ref, f32[1,1152]{1,0:T(1,128)S(1)} %broadcast_in_dim.30.gain_ref, f32[1,1152]{1,0:T(1,128)S(1)} %broadcast_in_dim.32.shift_ref, bf16[1920,1152]{1,0:T(8,128)(2,1)S(1)} %copy-done.5, f32[1920,1]{1,0:T(8,128)S(1)} %copy-done.2), custom_call_target="tpu_custom_call" | custom-call | flops 9059696640 | bytes 17006592 | tf_op jit(solution)/shard_map/project_tokens/pallas_call | solution.py:143
  184.4 5.3 %fusion.121 = (bf16[1152,1,16,72]{0,3,2,1:T(8,128)(2,1)}, bf16[1152,1,16,72]{0,3,2,1:T(8,128)(2,1)}) fusion(bf16[1152,2,16,72]{0,3,2,1:T(8,128)(2,1)} %param.46), kind=kLoop, calls=%fused_computation.177 | loop fusion | bytes 10616832 | tf_op jit(solution)/shard_map/slice | solution.py:243
  189.8 4.6 %pad.55 = bf16[16,128,1152]{2,1,0:T(8,128)(2,1)} pad(bf16[16,72,1152]{2,1,0:T(8,128)(2,1)} %bitcast.91, bf16[]{:T(256)} %constant.20.clone.1), padding=0_0x0_56x0_0 | pad | bytes 7372802 | tf_op jit(solution)/shard_map/jit(_pad)/pad | solution.py:225
  194.3 39.6 %heads_attention.4.refs_0_ = bf16[2048,2048]{1,0:T(8,128)(2,1)} custom-call(bf16[1920,2048]{1,0:T(8,128)(2,1)} %project_tokens.2.q_ref.k_own_ref.v_own_ref.v_own_last_ref, bf16[1920,2048]{1,0:T(8,128)(2,1)} %project_tokens.2.q_ref.k_own_ref.v_own_ref.v_own_last_ref, ...), custom_call_target="tpu_custom_call", output_to_operand_aliasing={{}: (7, {})} | custom-call | flops 17179869184 | bytes 8388608 | tf_op jit(solution)/shard_map/heads_attention/pallas_call | solution.py:112
  235.2 72.1 %heads_attention.5 = bf16[2048,2048]{1,0:T(8,128)(2,1)} custom-call(bf16[1920,2048]{1,0:T(8,128)(2,1)} %project_tokens.3.q_ref.k_own_ref.v_own_ref.v_own_last_ref, bf16[1920,2048]{1,0:T(8,128)(2,1)} %project_tokens.3.q_ref.k_own_ref.v_own_ref.v_own_last_ref, ...), custom_call_target="tpu_custom_call", output_to_operand_aliasing={{}: (7, {})} | custom-call | flops 34359738368 | bytes 8388608 | tf_op jit(solution)/shard_map/heads_attention/pallas_call | solution.py:112
  307.4 14.8 %convert_reduce_fusion = (f32[2048]{0:T(1024)S(1)}, bf16[2048,1152]{1,0:T(8,128)(2,1)S(1)}) fusion(f32[1152]{0:T(1024)S(1)} %copy-done.26, bf16[2048,2048]{1,0:T(8,128)(2,1)} %heads_attention.5, bf16[2048,1152]{1,0:T(8,128)(2,1)S(1)} %bitcast.88, bf16[2048,1152]{1,0:T(8,128)(2,1)} %bitcast.2.x_ref), kind=kOutput, calls=%fused_computation.11 | convolution fusion | flops 9677830144 | bytes 22557184 | tf_op jit(solution)/shard_map/dot_general | solution.py:226
  322.3 2.2 copy-done.6
  325.9 36.9 %fusion.7.clone.3.clone.4 = bf16[2048,4352]{1,0:T(8,128)(2,1)} fusion(bf16[4352,1152]{1,0:T(8,128)(2,1)} %all-gather.13.cloned.1.call-done, f32[4352]{0:T(1024)S(1)} %add.225, bf16[2048,1152]{1,0:T(8,128)(2,1)} %copy-done.6, f32[1152]{0:T(1024)S(1)} %copy-done.27, f32[1152]{0:T(1024)S(1)} %copy-done.28, ...), kind=kOutput, calls=%fused_computation.8.clone.clone.clone.clone.clone.clone.clone.1 | convolution fusion | flops 20638597120 | bytes 32614400 | tf_op jit(solution)/shard_map/dot_general | solution.py:232
  362.9 29.9 %convert_reduce_fusion.1 = (f32[2048]{0:T(1024)S(1)}, bf16[2048,1152]{1,0:T(8,128)(2,1)S(1)}) fusion(f32[1152]{0:T(1024)S(1)} %copy-done.29, bf16[4352,1152]{1,0:T(8,128)(2,1)} %all-gather.15.cloned.1.call-done, bf16[2048,1152]{1,0:T(8,128)(2,1)} %copy-done.6, bf16[2048,4352]{1,0:T(8,128)(2,1)} %fusion.7.clone.3.clone.4), kind=kOutput, calls=%fused_computation.14 | convolution fusion | flops 20549466112 | bytes 37302784 | tf_op jit(solution)/shard_map/dot_general | solution.py:234
  392.8 2.1 copy-done.7
  396.4 12.1 %fusion.125 = (f32[16]{0:T(128)S(1)}, f32[16,2048]{1,0:T(8,128)S(1)}) fusion(bf16[1152,1152]{0,1:T(8,128)(2,1)S(1)} %bitcast.90, f32[1152]{0:T(1024)S(1)} %copy-done.22, bf16[2048,1152]{1,0:T(8,128)(2,1)} %copy-done.7, f32[1152]{0:T(1024)S(1)} %copy-done.30, f32[1152]{0:T(1024)S(1)} %copy-done.31, f32[2048]{0:T(1024)S(1)} %add_rsqrt_fusion, ...), kind=kOutput, calls=%fused_computation.179 | convolution fusion | flops 5530292224 | bytes 7541056 | tf_op jit(solution)/shard_map/dot_general | solution.py:244
  408.8 11.5 %convolution_select_fusion = f32[16,1152]{1,0:T(8,128)S(1)} fusion(bf16[1152,1152]{0,1:T(8,128)(2,1)} %bitcast.89, f32[1152]{0:T(1024)S(1)} %copy-done.20, f32[16,2048]{1,0:T(8,128)S(1)} %get-tuple-element.43, f32[16]{0:T(128)S(1)} %get-tuple-element.42, s32[1152]{0:T(1024)S(1)} %copy-done.21, bf16[2048,1152]{1,0:T(8,128)(2,1)} %copy-done.7, ...), kind=kOutput, calls=%fused_computation.41 | convolution fusion | flops 5530292224 | bytes 7612480 | tf_op jit(solution)/shard_map/dot_general | solution.py:248
  420.7 11.0 %all-gather = f32[128,74]{1,0:T(8,128)S(1)} all-gather(f32[16,74]{1,0:T(8,128)S(1)} %pad_maximum_fusion), channel_id=2, replica_groups=mesh['dp'=1,'tp'=8] {'tp'}, dimensions={0}, use_global_device_ids=true | all-gather | bytes 42624 | tf_op jit(solution)/shard_map/all_gather | solution.py:250
  433.4 11.4 %fusion.38 = bf16[4,1152]{1,0:T(4,128)(2,1)} fusion(f32[4,1152]{1,0:T(4,128)S(1)} %get-tuple-element.45, bf16[4304,1152]{1,0:T(8,128)(2,1)} %param.54, bf16[1152,4304]{0,1:T(8,128)(2,1)} %param.52, f32[4304]{0:T(1024)S(1)} %copy-done.11, f32[1152]{0:T(1024)S(1)} %copy-done.14, f32[1152]{0:T(1024)S(1)} %copy-done.15, f32[1152]{0:T(1024)S(1)} %copy-done.16, ...), kind=kOutput, calls=%fused_computation.47 | convolution fusion | flops 79540352 | bytes 19891552 | tf_op jit(solution)/shard_map/dot_general | solution.py:170
  (155 shorter events, 24.2 us)
Async XLA Ops:
  6.5 176.5 %copy-start = (bf16[1152,16,72]{0,2,1:T(8,128)(2,1)S(1)}, bf16[1152,16,72]{0,2,1:T(8,128)(2,1)}, u32[]{:S(2)}) copy-start(bf16[1152,16,72]{0,2,1:T(8,128)(2,1)} %param.44) | copy-start | bytes 7962628
  6.5 82.3 %all-gather.7.cloned.1.call-start = ((), (), s32[]{:S(2)}) async-start(), calls=%async_computation.1 | async-start | bytes 4976640 | tf_op jit(solution)/shard_map/all_gather | solution.py:202
  8.8 79.9 %copy-start.17 = (f32[1152]{0:T(1024)S(1)}, f32[1152]{0:T(1024)}, u32[]{:S(2)}) copy-start(f32[1152]{0:T(1024)} %param.29) | copy-start | bytes 13828
  8.8 79.9 %copy-start.18 = (f32[1152]{0:T(1024)S(1)}, f32[1152]{0:T(1024)}, u32[]{:S(2)}) copy-start(f32[1152]{0:T(1024)} %param.30) | copy-start | bytes 13828
  10.5 76.8 %all-to-all-start = ((bf16[8,256,1152]{2,1,0:T(8,128)(2,1)}), bf16[8,256,1152]{2,1,0:T(8,128)(2,1)}, u32[]{:S(2)}, u32[]{:S(2)}) async-start(bf16[8,256,1152]{2,1,0:T(8,128)(2,1)} %bitcast.85), calls=%async_computation | async-start | bytes 9437184 | tf_op jit(solution)/shard_map/all_to_all | solution.py:185
  14.8 104.7 %all-gather.9.cloned.1.call-start = ((), (), s32[]{:S(2)}) async-start(), calls=%async_computation.2 | async-start | bytes 4976640 | tf_op jit(solution)/shard_map/all_gather | solution.py:204
  87.4 102.4 %all-gather.11.cloned.1.call-start = ((), (), s32[]{:S(2)}) async-start(), calls=%async_computation.3 | async-start | bytes 2985984 | tf_op jit(solution)/shard_map/all_gather | solution.py:205
  88.1 145.8 %all-gather.15.cloned.1.call-start = ((), (), s32[]{:S(2)}) async-start(), calls=%async_computation.5 | async-start | bytes 11280384 | tf_op jit(solution)/shard_map/all_gather | solution.py:207
  88.7 237.2 %all-gather.13.cloned.1.call-start = ((), (), s32[]{:S(2)}) async-start(), calls=%async_computation.4 | async-start | bytes 11280384 | tf_op jit(solution)/shard_map/all_gather | solution.py:206
  111.3 13.2 %collective-permute-start = (bf16[1920,2048]{1,0:T(8,128)(2,1)}, bf16[1920,2048]{1,0:T(8,128)(2,1)}, u32[]{:S(2)}, u32[]{:S(2)}) collective-permute-start(bf16[1920,2048]{1,0:T(8,128)(2,1)} %project_tokens.2.q_ref.k_own_ref.v_own_ref.v_own_last_ref), channel_id=1, source_target_pairs={{0,1},{1,0},{2,3},{3,2},{4,5},{5,4},{6,7},{7,6}} | collective-permute-start | bytes 23592968 | tf_op jit(solution)/shard_map/ppermute | solution.py:215
  122.0 42.0 %copy-start.2 = (f32[1920,1]{1,0:T(8,128)S(1)}, f32[1920,1]{1,0:T(8,128)}, u32[]{:S(2)}) copy-start(f32[1920,1]{1,0:T(8,128)} %reshape.158.bias_ref) | copy-start | bytes 23044
  122.0 42.0 %copy-start.5 = (bf16[1920,1152]{1,0:T(8,128)(2,1)S(1)}, bf16[1920,1152]{1,0:T(8,128)(2,1)}, u32[]{:S(2)}) copy-start(bf16[1920,1152]{1,0:T(8,128)(2,1)} %all-gather.9.cloned.1.call-done.weight_ref) | copy-start | bytes 13271044
  180.7 54.5 %collective-permute-start.1 = (bf16[1920,2048]{1,0:T(8,128)(2,1)}, bf16[1920,2048]{1,0:T(8,128)(2,1)}, u32[]{:S(2)}, u32[]{:S(2)}) collective-permute-start(bf16[1920,2048]{1,0:T(8,128)(2,1)} %project_tokens.3.q_ref.k_own_ref.v_own_ref.v_own_last_ref), channel_id=1, source_target_pairs={{0,1},{1,0},{2,3},{3,2},{4,5},{5,4},{6,7},{7,6}} | collective-permute-start | bytes 23592968 | tf_op jit(solution)/shard_map/ppermute | solution.py:215
  235.1 72.2 %slice-start = ((s8[4718592]{0:T(1024)(128)(4,1)}), s8[524288]{0:T(1024)(128)(4,1)S(1)}, s32[]{:S(2)}) async-start(s8[4718592]{0:T(1024)(128)(4,1)} %bitcast.86), calls=%async_computation.6 | async-start | bytes 1048576
  235.2 72.2 %slice-start.1 = ((s8[4718592]{0:T(1024)(128)(4,1)}), s8[4194304]{0:T(1024)(128)(4,1)S(1)}, s32[]{:S(2)}) async-start(s8[4718592]{0:T(1024)(128)(4,1)} %bitcast.86), calls=%async_computation.7 | async-start | bytes 8388608
  235.2 72.2 %copy-start.26 = (f32[1152]{0:T(1024)S(1)}, f32[1152]{0:T(1024)}, u32[]{:S(2)}) copy-start(f32[1152]{0:T(1024)} %param.34) | copy-start | bytes 13828
  325.8 37.0 %copy-start.29 = (f32[1152]{0:T(1024)S(1)}, f32[1152]{0:T(1024)}, u32[]{:S(2)}) copy-start(f32[1152]{0:T(1024)} %param.40) | copy-start | bytes 13828
  362.8 33.5 %copy-start.9 = (bf16[1152,1,16,72]{0,3,2,1:T(8,128)(2,1)S(1)}, bf16[1152,1,16,72]{0,3,2,1:T(8,128)(2,1)}, u32[]{:S(2)}) copy-start(bf16[1152,1,16,72]{0,3,2,1:T(8,128)(2,1)} %get-tuple-element.24) | copy-start | bytes 7962628
  362.8 33.5 %copy-start.21 = (s32[1152]{0:T(1024)S(1)}, s32[1152]{0:T(1024)}, u32[]{:S(2)}) copy-start(s32[1152]{0:T(1024)} %add_select_fusion) | copy-start | bytes 13828
  362.8 33.5 %copy-start.22 = (f32[1152]{0:T(1024)S(1)}, f32[1152]{0:T(1024)}, u32[]{:S(2)}) copy-start(f32[1152]{0:T(1024)} %add.237) | copy-start | bytes 13828
  362.8 33.5 %copy-start.23 = (bf16[1152]{0:T(1024)(128)(2,1)S(1)}, bf16[1152]{0:T(1024)(128)(2,1)}, u32[]{:S(2)}) copy-start(bf16[1152]{0:T(1024)(128)(2,1)} %add_convert_fusion.6) | copy-start | bytes 6916
  362.8 33.5 %copy-start.30 = (f32[1152]{0:T(1024)S(1)}, f32[1152]{0:T(1024)}, u32[]{:S(2)}) copy-start(f32[1152]{0:T(1024)} %param.42) | copy-start | bytes 13828
  362.9 33.5 %copy-start.31 = (f32[1152]{0:T(1024)S(1)}, f32[1152]{0:T(1024)}, u32[]{:S(2)}) copy-start(f32[1152]{0:T(1024)} %param.41) | copy-start | bytes 13828
  408.7 24.6 %copy-start.11 = (f32[4304]{0:T(1024)S(1)}, f32[4304]{0:T(1024)}, u32[]{:S(2)}) copy-start(f32[4304]{0:T(1024)} %param.53) | copy-start | bytes 51652
  (18 other events, 251.1 us)
Sparse Core Ops, SparseCore 0:
  10.6 64.0 all-gather.6
  87.5 31.9 all-gather.8
  121.3 24.2 all-gather.10
  147.3 55.4 all-gather.14
  204.4 55.4 all-gather.12

commit v4 on v3

--- a/solution.py
+++ b/solution.py
@@ -78,7 +78,7 @@
         write(slice(0, block), first_out[...])
         write(slice(block, 2 * block), second)
 
-    @pl.when(apart[0] == 0)
+    @pl.when(step < pl.num_programs(0) - 1)
     def _():
         first_out[...] = overlap(1, scores_b, max_b, v_own_ref, v_far_ref, scores_a, max_a)
 
@@ -136,7 +136,7 @@
     out_ref[...] = (product + bias_ref[...]).astype(out_ref.dtype)
 
 
-def project_tokens(resid, gain, shift, weight, bias, block=256):
+def project_tokens(resid, gain, shift, weight, bias, block=512):
     n_own, width = resid.shape
     rows = weight.shape[0]
     fixed = lambda shape: pl.BlockSpec(shape, lambda i: (0, 0))
@@ -200,9 +200,16 @@
         w_down_p = jnp.pad(jnp.concatenate([w_down, up_rows], axis=0), ((0, padded - hidden_units - 2), (0, 0)))
 
         gathered = [lax.all_gather(shards[0], 'tp', axis=0, tiled=True)]
-        resid, later, w_out, w_up_t, w_down_p = lax.optimization_barrier((resid, shards[1:], w_out, w_up_t, w_down_p))
+        probe_q = (jnp.dot(probe_vec[None], map_wq.reshape(width, width), preferred_element_type=jnp.float32)[0] + map_bq.reshape(width)).astype(jnp.bfloat16)
+        head_of = jnp.arange(width) // head_dim
+        on_head = head_of[:, None] == jnp.arange(n_heads)[None]
+        probe_cols = jnp.where(on_head, probe_q[:, None], jnp.zeros((), jnp.bfloat16))
+        pool_wk, pool_wv = map_wkv[:, 0].reshape(width, width), map_wkv[:, 1].reshape(width, width)
+        w_out_p = jnp.pad(w_out, ((0, 0), (0, LANES - head_dim), (0, 0))).reshape(groups * LANES, width)
+        resid, later, w_out_p, w_up_t, w_down_p, probe_cols, pool_wk, pool_wv = lax.optimization_barrier(
+            (resid, shards[1:], w_out_p, w_up_t, w_down_p, probe_cols, pool_wk, pool_wv))
         gathered += [lax.all_gather(shard, 'tp', axis=0, tiled=True) for shard in later]
-        w_out_all = lax.all_gather(w_out.reshape(groups * head_dim, width), 'tp', axis=0, tiled=True)
+        w_out_all = lax.all_gather(w_out_p, 'tp', axis=0, tiled=True)
         w_up_all = lax.all_gather(w_up_t, 'tp', axis=0, tiled=True)
         w_down_all = lax.all_gather(w_down_p, 'tp', axis=0, tiled=True)
 
@@ -217,13 +224,12 @@
         half = tp_size // 2
         first_group = projections(0, resid)
         mixed = heads_attention(*first_group, head_dim, (0, half), 0, groups, None, n_heads)
-        mixed, resid_later = lax.optimization_barrier((mixed, resid))
+        mixed, resid_later, gathered[1] = lax.optimization_barrier((mixed, resid, gathered[1]))
         second_group = projections(1, resid_later)
         mixed = heads_attention(*first_group, head_dim, (half, half), 0, groups, mixed, n_heads)
         mixed = heads_attention(*second_group, head_dim, (0, tp_size), 1, groups, mixed, n_heads)
 
-        w_out_rows = jnp.pad(w_out_all.reshape(n_heads, head_dim, width), ((0, 0), (0, LANES - head_dim), (0, 0))).reshape(n_heads * LANES, width)
-        attn_local = jnp.dot(mixed, w_out_rows, preferred_element_type=jnp.float32)
+        attn_local = jnp.dot(mixed, w_out_all, preferred_element_type=jnp.float32)
         resid_one = row_major((resid.astype(jnp.float32) + attn_local + b_out).astype(jnp.bfloat16))
         hidden_two = layer_norm(resid_one.astype(jnp.float32), ln2_gain, ln2_bias).astype(jnp.bfloat16)
         bias_rows = w_down_all.reshape(tp_size, padded, width)[:, hidden_units:hidden_units + 2]
@@ -235,12 +241,8 @@
         resid_two = row_major((resid_one.astype(jnp.float32) + mlp_local + b_down).astype(jnp.bfloat16))
         encoded = layer_norm(resid_two.astype(jnp.float32), lnf_gain, lnf_bias).astype(jnp.bfloat16)
 
-        probe_q = (jnp.dot(probe_vec[None], map_wq.reshape(width, width), preferred_element_type=jnp.float32)[0] + map_bq.reshape(width)).astype(jnp.bfloat16)
-        head_of = jnp.arange(width) // head_dim
-        on_head = head_of[:, None] == jnp.arange(n_heads)[None]
-        probe_cols = jnp.where(on_head, probe_q[:, None], jnp.zeros((), jnp.bfloat16))
-        map_keys = (jnp.dot(encoded, map_wkv[:, 0].reshape(width, width), preferred_element_type=jnp.float32) + map_bkv[0].reshape(width)).astype(jnp.bfloat16)
-        map_vals = (jnp.dot(encoded, map_wkv[:, 1].reshape(width, width), preferred_element_type=jnp.float32) + map_bkv[1].reshape(width)).astype(jnp.bfloat16)
+        map_keys = (jnp.dot(encoded, pool_wk, preferred_element_type=jnp.float32) + map_bkv[0].reshape(width)).astype(jnp.bfloat16)
+        map_vals = (jnp.dot(encoded, pool_wv, preferred_element_type=jnp.float32) + map_bkv[1].reshape(width)).astype(jnp.bfloat16)
         scores = lax.dot_general(probe_cols, map_keys, (((0,), (1,)), ((), ())), preferred_element_type=jnp.float32) * head_dim ** -0.5
         peak = jnp.max(scores, axis=-1, keepdims=True)
         weights = jnp.exp(scores - peak)

time: 460 us -> 440 us (0.957); the launches traced: 452 us -> 437 us
  local copies, waits for them, and re-layouts: 34.7 us -> 26.3 us
  Pallas kernels: 184 us -> 179 us
    ppermute x2, waiting for transfers between devices: 2.51 us -> 13.5 us  [projections(): return (qkv_t, lax.ppermute(qkv_t, 'tp', partner))]
    all_gather x1, waiting for transfers between devices: 8.14 us -> 0.01 us  [local_program(): lax.all_gather(shard, 'tp', axis=0, tiled=True)]
    pallas_call x3, Pallas kernels: 151 us -> 146 us  [heads_attention(): pl.pallas_call(functools.partial(attention_kernel, head_dim, 256), grid=(...]
    all_to_all x1, waiting for transfers between devices: 63.4 us -> 58.7 us  [local_program(): lax.all_to_all(row_major(tokens.reshape(tp_size, own // tp_size, width)),...]
    unnamed x82 -> x80, local copies, waits for them, and re-layouts: 12.1 us -> 9.9 us
  transfers between devices with their start and end apart: 8 -> 8, of which waited for: 3 -> 2; matrix products, arithmetic and copies ran while one was open for 10% -> 8% of each run, Pallas kernels for 41% -> 41%
where the time goes in v4:
time: 440 us; the launch traced here: 437 us
  Pallas kernels  179 us (41%)
  matrix products  120 us (27%)
  waiting for transfers between devices  73.5 us (17%)
  local copies, waits for them, and re-layouts  26.3 us (6%)
  between operations  14.1 us (3%)
  blocking collectives  11 us (2%)
  other arithmetic  9.02 us (2%)
  starting transfers between devices  4.8 us (1%)
    pallas_call x3, Pallas kernels, heads_attention(): pl.pallas_call(functools.partial(attention_kernel, head_dim, 256), grid=(...  146 us
    all_to_all x1, waiting for transfers between devices, local_program(): lax.all_to_all(row_major(tokens.reshape(tp_size, own // tp_size, width)),...  58.7 us
    dot_general x1, matrix products, local_program(): lax.dot_general(hidden_two, w_up_all, (((1,), (1,)), ((), ())), preferred...  36.9 us
    pallas_call x2, Pallas kernels, project_tokens(): pl.pallas_call(project_kernel, grid=(n_own // block,), out_shape=jax.Shap...  32.8 us
    dot_general x1, matrix products, local_program(): jnp.dot(activated, w_down_all, preferred_element_type=jnp.float32)  30.1 us
    dot_general x1, matrix products, local_program(): attn_local = jnp.dot(mixed, w_out_all, preferred_element_type=jnp.float32)  16 us
    ppermute x2, waiting for transfers between devices, projections(): return (qkv_t, lax.ppermute(qkv_t, 'tp', partner))  13.5 us
    dot_general x1, matrix products, local_program(): lax.dot_general(probe_cols, map_keys, (((0,), (1,)), ((), ())), preferred...  12.1 us
  transfers between devices with their start and end apart: 8, of which 2 were waited for; matrix products, arithmetic and copies ran while one was open for 8% of the time, Pallas kernels for 41%

profile of v4, /device:TPU:0, one launch (start us, length us, event | category | flops | bytes accessed | tf_op | source)
XLA Modules:
  0.0 436.8 jit_solution(2357160811626282976)
XLA Ops:
  6.6 1.4 slice_bitcast_fusion
  10.6 4.3 all-to-all-start
  15.4 2.4 pad.48
  19.7 2.7 fusion.40
  23.4 5.3 %fusion.116 = (bf16[1152,1,16,72]{0,3,2,1:T(8,128)(2,1)}, bf16[1152,1,16,72]{0,3,2,1:T(8,128)(2,1)}) fusion(bf16[1152,2,16,72]{0,3,2,1:T(8,128)(2,1)} %param.46), kind=kLoop, calls=%fused_computation.173 | loop fusion | bytes 10616832 | tf_op jit(solution)/shard_map/slice | solution.py:207
  28.7 58.7 %all-to-all-done = bf16[8,256,1152]{2,1,0:T(8,128)(2,1)} async-done(((bf16[8,256,1152]{2,1,0:T(8,128)(2,1)}), bf16[8,256,1152]{2,1,0:T(8,128)(2,1)}, u32[]{:S(2)}, u32[]{:S(2)}) %all-to-all-start) | async-done | bytes 4718624 | tf_op jit(solution)/shard_map/all_to_all | solution.py:185
  90.3 2.2 copy-done.2
  92.6 16.5 %project_tokens.2.q_ref.k_own_ref.v_own_ref.v_own_last_ref = bf16[1920,2048]{1,0:T(8,128)(2,1)} custom-call(bf16[2048,1152]{1,0:T(8,128)(2,1)} %bitcast.1.x_ref, f32[1,1152]{1,0:T(1,128)S(1)} %broadcast_in_dim.30.gain_ref, f32[1,1152]{1,0:T(1,128)S(1)} %broadcast_in_dim.32.shift_ref, bf16[1920,1152]{1,0:T(8,128)(2,1)S(1)} %copy-done.2, ...), custom_call_target="tpu_custom_call" | custom-call | flops 9059696640 | bytes 17006592 | tf_op jit(solution)/shard_map/project_tokens/pallas_call | solution.py:143
  109.1 13.5 %collective-permute-done.k_far_ref.v_far_ref.v_far_last_ref = bf16[1920,2048]{1,0:T(8,128)(2,1)} collective-permute-done((bf16[1920,2048]{1,0:T(8,128)(2,1)}, bf16[1920,2048]{1,0:T(8,128)(2,1)}, u32[]{:S(2)}, u32[]{:S(2)}) %collective-permute-start) | collective-permute-done | bytes 7864352 | tf_op jit(solution)/shard_map/ppermute | solution.py:222
  122.6 37.6 %heads_attention.3.refs_0_ = bf16[2048,2048]{1,0:T(8,128)(2,1)} custom-call(bf16[1920,2048]{1,0:T(8,128)(2,1)} %project_tokens.2.q_ref.k_own_ref.v_own_ref.v_own_last_ref, bf16[1920,2048]{1,0:T(8,128)(2,1)} %project_tokens.2.q_ref.k_own_ref.v_own_ref.v_own_last_ref, bf16[1920,2048]{1,0:T(8,128)(2,1)} %collective-permute-done.k_far_ref.v_far_ref.v_far_last_ref, ...), custom_call_target="tpu_custom_call" | custom-call | flops 17179869184 | bytes 8388608 | tf_op jit(solution)/shard_map/heads_attention/pallas_call | solution.py:112
  161.7 2.2 copy-done.3
  164.0 16.3 %project_tokens.3.q_ref.k_own_ref.v_own_ref.v_own_last_ref = bf16[1920,2048]{1,0:T(8,128)(2,1)} custom-call(bf16[2048,1152]{1,0:T(8,128)(2,1)} %bitcast.1.x_ref, f32[1,1152]{1,0:T(1,128)S(1)} %broadcast_in_dim.30.gain_ref, f32[1,1152]{1,0:T(1,128)S(1)} %broadcast_in_dim.32.shift_ref, bf16[1920,1152]{1,0:T(8,128)(2,1)S(1)} %copy-done.3, ...), custom_call_target="tpu_custom_call" | custom-call | flops 9059696640 | bytes 17006592 | tf_op jit(solution)/shard_map/project_tokens/pallas_call | solution.py:143
  181.9 38.1 %heads_attention.4.refs_0_ = bf16[2048,2048]{1,0:T(8,128)(2,1)} custom-call(bf16[1920,2048]{1,0:T(8,128)(2,1)} %project_tokens.2.q_ref.k_own_ref.v_own_ref.v_own_last_ref, bf16[1920,2048]{1,0:T(8,128)(2,1)} %project_tokens.2.q_ref.k_own_ref.v_own_ref.v_own_last_ref, ...), custom_call_target="tpu_custom_call", output_to_operand_aliasing={{}: (7, {})} | custom-call | flops 17179869184 | bytes 8388608 | tf_op jit(solution)/shard_map/heads_attention/pallas_call | solution.py:112
  221.2 70.1 %heads_attention.5 = bf16[2048,2048]{1,0:T(8,128)(2,1)} custom-call(bf16[1920,2048]{1,0:T(8,128)(2,1)} %project_tokens.3.q_ref.k_own_ref.v_own_ref.v_own_last_ref, bf16[1920,2048]{1,0:T(8,128)(2,1)} %project_tokens.3.q_ref.k_own_ref.v_own_ref.v_own_last_ref, ...), custom_call_target="tpu_custom_call", output_to_operand_aliasing={{}: (7, {})} | custom-call | flops 34359738368 | bytes 8388608 | tf_op jit(solution)/shard_map/heads_attention/pallas_call | solution.py:112
  291.4 16.0 %convert_reduce_fusion = (f32[2048]{0:T(1024)S(1)}, bf16[2048,1152]{1,0:T(8,128)(2,1)S(1)}) fusion(f32[1152]{0:T(1024)S(1)} %copy-done.27, bf16[2048,2048]{1,0:T(8,128)(2,1)} %heads_attention.5, bf16[2048,1152]{1,0:T(8,128)(2,1)} %all-gather.11.cloned.1.call-done, bf16[2048,1152]{1,0:T(8,128)(2,1)} %bitcast.1.x_ref), kind=kOutput, calls=%fused_computation.11 | convolution fusion | flops 9677830144 | bytes 22557184 | tf_op jit(solution)/shard_map/dot_general | solution.py:232
  307.4 2.1 copy-done.4
  309.5 1.4 fusion.13
  311.0 36.9 %fusion.7.clone.3.clone.4 = bf16[2048,4352]{1,0:T(8,128)(2,1)} fusion(bf16[4352,1152]{1,0:T(8,128)(2,1)} %all-gather.13.cloned.1.call-done, f32[4352]{0:T(1024)S(1)} %add.225, bf16[2048,1152]{1,0:T(8,128)(2,1)} %copy-done.4, f32[1152]{0:T(1024)S(1)} %copy-done.28, f32[1152]{0:T(1024)S(1)} %copy-done.29, ...), kind=kOutput, calls=%fused_computation.8.clone.clone.clone.clone.clone.clone.clone.1 | convolution fusion | flops 20638597120 | bytes 32614400 | tf_op jit(solution)/shard_map/dot_general | solution.py:238
  348.0 30.1 %convert_reduce_fusion.1 = (f32[2048]{0:T(1024)S(1)}, bf16[2048,1152]{1,0:T(8,128)(2,1)S(1)}) fusion(f32[1152]{0:T(1024)S(1)} %copy-done.30, bf16[4352,1152]{1,0:T(8,128)(2,1)} %all-gather.15.cloned.1.call-done, bf16[2048,1152]{1,0:T(8,128)(2,1)} %copy-done.4, bf16[2048,4352]{1,0:T(8,128)(2,1)} %fusion.7.clone.3.clone.4), kind=kOutput, calls=%fused_computation.14 | convolution fusion | flops 20549466112 | bytes 37302784 | tf_op jit(solution)/shard_map/dot_general | solution.py:240
  378.2 2.1 copy-done.5
  381.7 12.1 %fusion.120 = (f32[16]{0:T(128)S(1)}, f32[16,2048]{1,0:T(8,128)S(1)}) fusion(bf16[1152,16]{1,0:T(8,128)(2,1)S(1)} %copy-done.11, bf16[1152,1152]{0,1:T(8,128)(2,1)S(1)} %bitcast.86, f32[1152]{0:T(1024)S(1)} %copy-done.24, bf16[2048,1152]{1,0:T(8,128)(2,1)} %copy-done.5, f32[1152]{0:T(1024)S(1)} %copy-done.31, f32[1152]{0:T(1024)S(1)} %copy-done.32, ...), kind=kOutput, calls=%fused_computation.175 | convolution fusion | flops 5530255360 | bytes 7571008 | tf_op jit(solution)/shard_map/dot_general | solution.py:246
  394.1 11.5 %convolution_select_fusion = f32[16,1152]{1,0:T(8,128)S(1)} fusion(bf16[1152,1152]{0,1:T(8,128)(2,1)} %bitcast.85, f32[1152]{0:T(1024)S(1)} %copy-done.23, f32[16,2048]{1,0:T(8,128)S(1)} %get-tuple-element.51, f32[16]{0:T(128)S(1)} %get-tuple-element.50, s32[1152]{0:T(1024)S(1)} %copy-done.13, bf16[2048,1152]{1,0:T(8,128)(2,1)} %copy-done.5, ...), kind=kOutput, calls=%fused_computation.41 | convolution fusion | flops 5530292224 | bytes 7612480 | tf_op jit(solution)/shard_map/dot_general | solution.py:250
  406.0 11.0 %all-gather = f32[128,74]{1,0:T(8,128)S(1)} all-gather(f32[16,74]{1,0:T(8,128)S(1)} %pad_maximum_fusion), channel_id=2, replica_groups=mesh['dp'=1,'tp'=8] {'tp'}, dimensions={0}, use_global_device_ids=true | all-gather | bytes 42624 | tf_op jit(solution)/shard_map/all_gather | solution.py:252
  418.7 11.4 %fusion.38 = bf16[4,1152]{1,0:T(4,128)(2,1)} fusion(f32[4,1152]{1,0:T(4,128)S(1)} %get-tuple-element.53, bf16[4304,1152]{1,0:T(8,128)(2,1)} %param.54, bf16[1152,4304]{0,1:T(8,128)(2,1)} %param.52, f32[4304]{0:T(1024)S(1)} %copy-done.14, f32[1152]{0:T(1024)S(1)} %copy-done.17, f32[1152]{0:T(1024)S(1)} %copy-done.18, f32[1152]{0:T(1024)S(1)} %copy-done.19, ...), kind=kOutput, calls=%fused_computation.47 | convolution fusion | flops 79540352 | bytes 19891552 | tf_op jit(solution)/shard_map/dot_general | solution.py:170
  (153 shorter events, 16.7 us)
Async XLA Ops:
  6.5 82.3 %all-gather.7.cloned.1.call-start = ((), (), s32[]{:S(2)}) async-start(), calls=%async_computation.1 | async-start | bytes 4976640 | tf_op jit(solution)/shard_map/all_gather | solution.py:202
  10.6 76.8 %all-to-all-start = ((bf16[8,256,1152]{2,1,0:T(8,128)(2,1)}), bf16[8,256,1152]{2,1,0:T(8,128)(2,1)}, u32[]{:S(2)}, u32[]{:S(2)}) async-start(bf16[8,256,1152]{2,1,0:T(8,128)(2,1)} %bitcast.84), calls=%async_computation | async-start | bytes 9437184 | tf_op jit(solution)/shard_map/all_to_all | solution.py:185
  14.9 145.4 %all-gather.9.cloned.1.call-start = ((), (), s32[]{:S(2)}) async-start(), calls=%async_computation.2 | async-start | bytes 4976640 | tf_op jit(solution)/shard_map/all_gather | solution.py:211
  18.7 69.5 %copy-start.12 = (s32[1152]{0:T(1024)}, s32[1152]{0:T(1024)S(1)}, u32[]{:S(2)}) copy-start(s32[1152]{0:T(1024)S(1)} %add_select_fusion) | copy-start | bytes 13828
  18.7 69.5 %copy-start.21 = (f32[1152]{0:T(1024)S(1)}, f32[1152]{0:T(1024)}, u32[]{:S(2)}) copy-start(f32[1152]{0:T(1024)} %param.29) | copy-start | bytes 13828
  18.7 69.5 %copy-start.22 = (f32[1152]{0:T(1024)S(1)}, f32[1152]{0:T(1024)}, u32[]{:S(2)}) copy-start(f32[1152]{0:T(1024)} %param.30) | copy-start | bytes 13828
  19.7 67.7 %copy-start.9 = (bf16[240,1152]{1,0:T(8,128)(2,1)}, bf16[240,1152]{1,0:T(8,128)(2,1)S(1)}, u32[]{:S(2)}) copy-start(bf16[240,1152]{1,0:T(8,128)(2,1)S(1)} %constant_dynamic-update-slice_fusion) | copy-start | bytes 1658884
  87.4 132.5 %all-gather.15.cloned.1.call-start = ((), (), s32[]{:S(2)}) async-start(), calls=%async_computation.5 | async-start | bytes 11280384 | tf_op jit(solution)/shard_map/all_gather | solution.py:214
  88.2 203.2 %all-gather.11.cloned.1.call-start = ((), (), s32[]{:S(2)}) async-start(), calls=%async_computation.3 | async-start | bytes 5308416 | tf_op jit(solution)/shard_map/all_gather | solution.py:212
  88.8 222.2 %all-gather.13.cloned.1.call-start = ((), (), s32[]{:S(2)}) async-start(), calls=%async_computation.4 | async-start | bytes 11280384 | tf_op jit(solution)/shard_map/all_gather | solution.py:213
  109.1 13.5 %collective-permute-start = (bf16[1920,2048]{1,0:T(8,128)(2,1)}, bf16[1920,2048]{1,0:T(8,128)(2,1)}, u32[]{:S(2)}, u32[]{:S(2)}) collective-permute-start(bf16[1920,2048]{1,0:T(8,128)(2,1)} %project_tokens.2.q_ref.k_own_ref.v_own_ref.v_own_last_ref), channel_id=1, source_target_pairs={{0,1},{1,0},{2,3},{3,2},{4,5},{5,4},{6,7},{7,6}} | collective-permute-start | bytes 23592968 | tf_op jit(solution)/shard_map/ppermute | solution.py:222
  180.2 41.0 %collective-permute-start.1 = (bf16[1920,2048]{1,0:T(8,128)(2,1)}, bf16[1920,2048]{1,0:T(8,128)(2,1)}, u32[]{:S(2)}, u32[]{:S(2)}) collective-permute-start(bf16[1920,2048]{1,0:T(8,128)(2,1)} %project_tokens.3.q_ref.k_own_ref.v_own_ref.v_own_last_ref), channel_id=1, source_target_pairs={{0,1},{1,0},{2,3},{3,2},{4,5},{5,4},{6,7},{7,6}} | collective-permute-start | bytes 23592968 | tf_op jit(solution)/shard_map/ppermute | solution.py:222
  221.2 70.2 %copy-start.27 = (f32[1152]{0:T(1024)S(1)}, f32[1152]{0:T(1024)}, u32[]{:S(2)}) copy-start(f32[1152]{0:T(1024)} %param.34) | copy-start | bytes 13828
  310.9 37.0 %copy-start.30 = (f32[1152]{0:T(1024)S(1)}, f32[1152]{0:T(1024)}, u32[]{:S(2)}) copy-start(f32[1152]{0:T(1024)} %param.40) | copy-start | bytes 13828
  347.9 33.7 %copy-start.7 = (bf16[1152,1,16,72]{0,3,2,1:T(8,128)(2,1)S(1)}, bf16[1152,1,16,72]{0,3,2,1:T(8,128)(2,1)}, u32[]{:S(2)}) copy-start(bf16[1152,1,16,72]{0,3,2,1:T(8,128)(2,1)} %get-tuple-element.32) | copy-start | bytes 7962628
  347.9 33.7 %copy-start.11 = (bf16[1152,16]{1,0:T(8,128)(2,1)S(1)}, bf16[1152,16]{1,0:T(8,128)(2,1)}, u32[]{:S(2)}) copy-start(bf16[1152,16]{1,0:T(8,128)(2,1)} %fusion.41) | copy-start | bytes 110596
  347.9 33.7 %copy-start.24 = (f32[1152]{0:T(1024)S(1)}, f32[1152]{0:T(1024)}, u32[]{:S(2)}) copy-start(f32[1152]{0:T(1024)} %add.237) | copy-start | bytes 13828
  347.9 33.7 %copy-start.31 = (f32[1152]{0:T(1024)S(1)}, f32[1152]{0:T(1024)}, u32[]{:S(2)}) copy-start(f32[1152]{0:T(1024)} %param.42) | copy-start | bytes 13828
  348.0 33.7 %copy-start.32 = (f32[1152]{0:T(1024)S(1)}, f32[1152]{0:T(1024)}, u32[]{:S(2)}) copy-start(f32[1152]{0:T(1024)} %param.41) | copy-start | bytes 13828
  394.1 23.6 %copy-start.6 = (bf16[16,72,1152]{2,1,0:T(8,128)(2,1)S(1)}, bf16[16,72,1152]{2,1,0:T(8,128)(2,1)}, u32[]{:S(2)}) copy-start(bf16[16,72,1152]{2,1,0:T(8,128)(2,1)} %param.48) | copy-start | bytes 7962628
  394.1 24.6 %copy-start.14 = (f32[4304]{0:T(1024)S(1)}, f32[4304]{0:T(1024)}, u32[]{:S(2)}) copy-start(f32[4304]{0:T(1024)} %param.53) | copy-start | bytes 51652
  394.1 24.6 %copy-start.17 = (f32[1152]{0:T(1024)S(1)}, f32[1152]{0:T(1024)}, u32[]{:S(2)}) copy-start(f32[1152]{0:T(1024)} %param.55) | copy-start | bytes 13828
  394.1 24.6 %copy-start.18 = (f32[1152]{0:T(1024)S(1)}, f32[1152]{0:T(1024)}, u32[]{:S(2)}) copy-start(f32[1152]{0:T(1024)} %param.51) | copy-start | bytes 13828
  394.1 24.6 %copy-start.19 = (f32[1152]{0:T(1024)S(1)}, f32[1152]{0:T(1024)}, u32[]{:S(2)}) copy-start(f32[1152]{0:T(1024)} %param.50) | copy-start | bytes 13828
  (17 other events, 174.6 us)
Sparse Core Ops, SparseCore 0:
  10.7 64.0 all-gather.6
  87.6 31.9 all-gather.8
  121.4 55.4 all-gather.14
  178.5 32.9 all-gather.10
  213.1 55.4 all-gather.12

commit v5 on v4

--- a/solution.py
+++ b/solution.py
@@ -163,6 +163,74 @@
     return high + middle + low
 
 
+def finish_kernel(head_dim, up_chunk, mixed_ref, resid_ref, vec_ref, up_bias_ref, pool_bias_ref, probe_ref, w_out_hbm, w_up_hbm, w_down_hbm, wk_hbm, wv_hbm,
+                  pooled_ref, total_ref, peak_ref, w_out, w_up, w_down, wk, wv, units, sems):
+    step = pl.program_id(0)
+    copies = [pltpu.make_async_copy(src, dst, sems.at[index]) for index, (src, dst) in enumerate(
+        ((w_out_hbm, w_out), (w_up_hbm, w_up), (w_down_hbm, w_down), (wk_hbm, wk), (wv_hbm, wv)))]
+
+    @pl.when(step == 0)
+    def _():
+        for copy in copies:
+            copy.start()
+        pooled_ref[...] = jnp.zeros_like(pooled_ref)
+        total_ref[...] = jnp.zeros_like(total_ref)
+        peak_ref[...] = jnp.full_like(peak_ref, -jnp.inf)
+
+    def arrive(index):
+        @pl.when(step == 0)
+        def _():
+            copies[index].wait()
+
+    b_out, ln2_gain, ln2_bias, b_down, lnf_gain, lnf_bias = (vec_ref[index:index + 1, :] for index in range(6))
+    arrive(0)
+    attn_local = jnp.dot(mixed_ref[...], w_out[...], preferred_element_type=jnp.float32)
+    resid_one = (resid_ref[...].astype(jnp.float32) + attn_local + b_out).astype(jnp.bfloat16)
+    hidden_two = layer_norm(resid_one.astype(jnp.float32), ln2_gain, ln2_bias).astype(jnp.bfloat16)
+    arrive(1)
+    n_units = w_up.shape[0]
+    for start in range(0, n_units, up_chunk):
+        cols = slice(start, min(start + up_chunk, n_units))
+        pre_act = lax.dot_general(hidden_two, w_up[cols, :], (((1,), (1,)), ((), ())), preferred_element_type=jnp.float32) + up_bias_ref[:, cols]
+        units[:, cols] = jax.nn.gelu(pre_act, approximate=True).astype(jnp.bfloat16)
+    arrive(2)
+    mlp_local = jnp.dot(units[...], w_down[...], preferred_element_type=jnp.float32)
+    resid_two = (resid_one.astype(jnp.float32) + mlp_local + b_down).astype(jnp.bfloat16)
+    encoded = layer_norm(resid_two.astype(jnp.float32), lnf_gain, lnf_bias).astype(jnp.bfloat16)
+    arrive(3)
+    keys = (jnp.dot(encoded, wk[...], preferred_element_type=jnp.float32) + pool_bias_ref[0:1, :]).astype(jnp.bfloat16)
+    arrive(4)
+    values = (jnp.dot(encoded, wv[...], preferred_element_type=jnp.float32) + pool_bias_ref[1:2, :]).astype(jnp.bfloat16)
+    scores = lax.dot_general(probe_ref[...], keys, (((1,), (1,)), ((), ())), preferred_element_type=jnp.float32) * head_dim ** -0.5
+    peak = jnp.maximum(peak_ref[...], jnp.max(scores, axis=-1, keepdims=True))
+    weights = jnp.exp(scores - peak)
+    keep = jnp.exp(peak_ref[...] - peak)
+    total_ref[...] = total_ref[...] * keep + jnp.sum(weights, axis=-1, keepdims=True)
+    pooled_ref[...] = pooled_ref[...] * keep + jnp.dot(weights.astype(jnp.bfloat16), values, preferred_element_type=jnp.float32)
+    peak_ref[...] = peak
+
+
+def finish_tokens(mixed, resid, vectors, up_bias, pool_bias, probe, weights, head_dim, block=512):
+    n_own, width = resid.shape
+    n_heads = probe.shape[0]
+    n_units = up_bias.shape[1]
+    fixed = lambda shape: pl.BlockSpec(shape, lambda i: (0, 0))
+    small = [vectors, up_bias, pool_bias, probe]
+    return pl.pallas_call(
+        functools.partial(finish_kernel, head_dim, 512),
+        grid=(n_own // block,),
+        out_shape=[jax.ShapeDtypeStruct((n_heads, columns), jnp.float32) for columns in (width, 1, 1)],
+        in_specs=[pl.BlockSpec((block, mixed.shape[1]), lambda i: (i, 0)), pl.BlockSpec((block, width), lambda i: (i, 0))]
+        + [fixed(array.shape) for array in small] + [pl.BlockSpec(memory_space=pl.ANY)] * len(weights),
+        out_specs=[fixed((n_heads, columns)) for columns in (width, 1, 1)],
+        scratch_shapes=[pltpu.VMEM(weight.shape, jnp.bfloat16) for weight in weights]
+        + [pltpu.VMEM((block, n_units), jnp.bfloat16), pltpu.SemaphoreType.DMA((len(weights),))],
+        compiler_params=pltpu.CompilerParams(dimension_semantics=('arbitrary',), vmem_limit_bytes=60 * 1024 * 1024),
+        cost_estimate=pl.CostEstimate(flops=2 * n_own * sum(weight.size for weight in weights), bytes_accessed=40 * 1024 * 1024, transcendentals=n_own * n_units),
+        name='finish_tokens',
+    )(mixed, resid, *small, *weights)
+
+
 def map_tail(pooled_heads, map_wo, map_bo, map_ln_gain, map_ln_bias, map_w_up, map_b_up, map_w_down, map_b_down):
     attn_vec = jnp.einsum('bhe,hed->bd', pooled_heads, map_wo, preferred_element_type=jnp.float32) + map_bo
     map_hidden = layer_norm(attn_vec, map_ln_gain, map_ln_bias).astype(jnp.bfloat16)
@@ -203,7 +271,7 @@
         probe_q = (jnp.dot(probe_vec[None], map_wq.reshape(width, width), preferred_element_type=jnp.float32)[0] + map_bq.reshape(width)).astype(jnp.bfloat16)
         head_of = jnp.arange(width) // head_dim
         on_head = head_of[:, None] == jnp.arange(n_heads)[None]
-        probe_cols = jnp.where(on_head, probe_q[:, None], jnp.zeros((), jnp.bfloat16))
+        probe_cols = jnp.where(on_head.T, probe_q[None], jnp.zeros((), jnp.bfloat16))
         pool_wk, pool_wv = map_wkv[:, 0].reshape(width, width), map_wkv[:, 1].reshape(width, width)
         w_out_p = jnp.pad(w_out, ((0, 0), (0, LANES - head_dim), (0, 0))).reshape(groups * LANES, width)
         resid, later, w_out_p, w_up_t, w_down_p, probe_cols, pool_wk, pool_wv = lax.optimization_barrier(
@@ -229,25 +297,12 @@
         mixed = heads_attention(*first_group, head_dim, (half, half), 0, groups, mixed, n_heads)
         mixed = heads_attention(*second_group, head_dim, (0, tp_size), 1, groups, mixed, n_heads)
 
-        attn_local = jnp.dot(mixed, w_out_all, preferred_element_type=jnp.float32)
-        resid_one = row_major((resid.astype(jnp.float32) + attn_local + b_out).astype(jnp.bfloat16))
-        hidden_two = layer_norm(resid_one.astype(jnp.float32), ln2_gain, ln2_bias).astype(jnp.bfloat16)
         bias_rows = w_down_all.reshape(tp_size, padded, width)[:, hidden_units:hidden_units + 2]
         b_up_all = join_three([bias_rows[:, 0, :hidden_units], bias_rows[:, 0, hidden_units:2 * hidden_units], bias_rows[:, 1, :hidden_units]])
         b_up_all = jnp.pad(b_up_all, ((0, 0), (0, padded - hidden_units))).reshape(tp_size * padded)
-        pre_act = lax.dot_general(hidden_two, w_up_all, (((1,), (1,)), ((), ())), preferred_element_type=jnp.float32) + b_up_all
-        activated = jax.nn.gelu(pre_act, approximate=True).astype(jnp.bfloat16)
-        mlp_local = jnp.dot(activated, w_down_all, preferred_element_type=jnp.float32)
-        resid_two = row_major((resid_one.astype(jnp.float32) + mlp_local + b_down).astype(jnp.bfloat16))
-        encoded = layer_norm(resid_two.astype(jnp.float32), lnf_gain, lnf_bias).astype(jnp.bfloat16)
-
-        map_keys = (jnp.dot(encoded, pool_wk, preferred_element_type=jnp.float32) + map_bkv[0].reshape(width)).astype(jnp.bfloat16)
-        map_vals = (jnp.dot(encoded, pool_wv, preferred_element_type=jnp.float32) + map_bkv[1].reshape(width)).astype(jnp.bfloat16)
-        scores = lax.dot_general(probe_cols, map_keys, (((0,), (1,)), ((), ())), preferred_element_type=jnp.float32) * head_dim ** -0.5
-        peak = jnp.max(scores, axis=-1, keepdims=True)
-        weights = jnp.exp(scores - peak)
-        total = jnp.sum(weights, axis=-1, keepdims=True)
-        every_head = jnp.dot(weights.astype(jnp.bfloat16), map_vals, preferred_element_type=jnp.float32)
+        vectors = jnp.stack([b_out, ln2_gain, ln2_bias, b_down, lnf_gain, lnf_bias])
+        every_head, total, peak = finish_tokens(
+            mixed, resid, vectors, b_up_all[None], map_bkv.reshape(2, width), probe_cols, (w_out_all, w_up_all, w_down_all, pool_wk, pool_wv), head_dim)
         pooled = jnp.sum(jnp.where(on_head.T, every_head, 0.0).reshape(n_heads, n_heads, head_dim), axis=1)
         parts = lax.all_gather(jnp.concatenate([pooled, total, peak], axis=-1), 'tp', axis=0, tiled=False)
         parts = parts.reshape(n_images, tp_size // n_images, n_heads, head_dim + 2)

time: 440 us -> 431 us (0.980)
  matrix products: 120 us -> 13 us
  Pallas kernels: 179 us -> 272 us
  local copies, waits for them, and re-layouts: 26.3 us -> 31.2 us
    dot_general x5 -> x0, matrix products: 107 us -> none  [the longest x1 36.9 us: local_program(): lax.dot_general(hidden_two, w_up_all, (((1,), (1,)), ((), ())), preferred...]
    pallas_call x0 -> x1, Pallas kernels: none -> 93.8 us  [finish_tokens(): pl.pallas_call(functools.partial(finish_kernel, head_dim, 512), grid=(n_o...]
    optimization_barrier x0 -> x2, local copies, waits for them, and re-layouts: none -> 8.81 us  [local_program(): lax.optimization_barrier((resid, shards[1:], w_out_p, w_up_t, w_down_p, p...]
    unnamed x80 -> x70, local copies, waits for them, and re-layouts: 9.9 us -> 5.57 us
  transfers between devices with their start and end apart: 8 -> 8, of which waited for: 2 -> 2; matrix products, arithmetic and copies ran while one was open for 8% -> 7% of each run, Pallas kernels for 41% -> 42%
where the time goes in v5:
time: 431 us; the launch traced here: 427 us
  Pallas kernels  272 us (63%)
  waiting for transfers between devices  73.9 us (17%)
  local copies, waits for them, and re-layouts  31.2 us (7%)
  between operations  14.1 us (3%)
  matrix products  13 us (3%)
  blocking collectives  11 us (3%)
  other arithmetic  7.24 us (2%)
  starting transfers between devices  4.79 us (1%)
    pallas_call x3, Pallas kernels, heads_attention(): pl.pallas_call(functools.partial(attention_kernel, head_dim, 256), grid=(...  145 us
    pallas_call x1, Pallas kernels, finish_tokens(): pl.pallas_call(functools.partial(finish_kernel, head_dim, 512), grid=(n_o...  93.8 us
    all_to_all x1, waiting for transfers between devices, local_program(): lax.all_to_all(row_major(tokens.reshape(tp_size, own // tp_size, width)),...  59 us
    pallas_call x2, Pallas kernels, project_tokens(): pl.pallas_call(project_kernel, grid=(n_own // block,), out_shape=jax.Shap...  33.1 us
    ppermute x2, waiting for transfers between devices, projections(): return (qkv_t, lax.ppermute(qkv_t, 'tp', partner))  13.5 us
    dot_general x1, matrix products, map_tail(): jnp.dot(map_act, map_w_down, preferred_element_type=jnp.float32)  11.4 us
    all_gather x1, blocking collectives, local_program(): lax.all_gather(jnp.concatenate([pooled, total, peak], axis=-1), 'tp', axi...  11 us
    optimization_barrier x2, local copies, waits for them, and re-layouts, local_program(): lax.optimization_barrier((resid, shards[1:], w_out_p, w_up_t, w_down_p, p...  8.81 us
  transfers between devices with their start and end apart: 8, of which 2 were waited for; matrix products, arithmetic and copies ran while one was open for 7% of the time, Pallas kernels for 42%

profile of v5, /device:TPU:0, one launch (start us, length us, event | category | flops | bytes accessed | tf_op | source)
XLA Modules:
  0.0 427.4 jit_solution(8945661784367961623)
XLA Ops:
  6.5 1.4 slice_bitcast_fusion
  10.5 4.3 %all-to-all-start = ((bf16[8,256,1152]{2,1,0:T(8,128)(2,1)}), bf16[8,256,1152]{2,1,0:T(8,128)(2,1)}, u32[]{:S(2)}, u32[]{:S(2)}) async-start(bf16[8,256,1152]{2,1,0:T(8,128)(2,1)} %bitcast.72), calls=%async_computation | async-start | bytes 9437184 | tf_op jit(solution)/shard_map/all_to_all | solution.py:253
  15.3 2.5 pad.48
  17.8 0.9 pad.47
  19.6 2.7 fusion.7
  23.0 5.3 %fusion.72 = (bf16[1152,1,16,72]{0,3,2,1:T(8,128)(2,1)}, bf16[1152,1,16,72]{0,3,2,1:T(8,128)(2,1)}) fusion(bf16[1152,2,16,72]{0,3,2,1:T(8,128)(2,1)} %param.46), kind=kLoop, calls=%fused_computation.123 | loop fusion | bytes 10616832 | tf_op jit(solution)/shard_map/slice | solution.py:275
  28.3 59.0 %all-to-all-done = bf16[8,256,1152]{2,1,0:T(8,128)(2,1)} async-done(((bf16[8,256,1152]{2,1,0:T(8,128)(2,1)}), bf16[8,256,1152]{2,1,0:T(8,128)(2,1)}, u32[]{:S(2)}, u32[]{:S(2)}) %all-to-all-start) | async-done | bytes 4718624 | tf_op jit(solution)/shard_map/all_to_all | solution.py:253
  88.8 0.9 slice.114
  90.3 2.2 copy-done.2
  92.5 16.8 %project_tokens.2.q_ref.k_own_ref.v_own_ref.v_own_last_ref = bf16[1920,2048]{1,0:T(8,128)(2,1)} custom-call(bf16[2048,1152]{1,0:T(8,128)(2,1)} %bitcast.1.x_ref.resid_ref, f32[1,1152]{1,0:T(1,128)S(1)} %broadcast_in_dim.27.gain_ref, f32[1,1152]{1,0:T(1,128)S(1)} %broadcast_in_dim.46.shift_ref, bf16[1920,1152]{1,0:T(8,128)(2,1)S(1)} %copy-done.2, ...), custom_call_target="tpu_custom_call" | custom-call | flops 9059696640 | bytes 17006592 | tf_op jit(solution)/shard_map/project_tokens/pallas_call | solution.py:143
  109.3 13.5 %collective-permute-done.k_far_ref.v_far_ref.v_far_last_ref = bf16[1920,2048]{1,0:T(8,128)(2,1)} collective-permute-done((bf16[1920,2048]{1,0:T(8,128)(2,1)}, bf16[1920,2048]{1,0:T(8,128)(2,1)}, u32[]{:S(2)}, u32[]{:S(2)}) %collective-permute-start) | collective-permute-done | bytes 7864352 | tf_op jit(solution)/shard_map/ppermute | solution.py:290
  122.8 37.5 %heads_attention.3.refs_0_ = bf16[2048,2048]{1,0:T(8,128)(2,1)} custom-call(bf16[1920,2048]{1,0:T(8,128)(2,1)} %project_tokens.2.q_ref.k_own_ref.v_own_ref.v_own_last_ref, bf16[1920,2048]{1,0:T(8,128)(2,1)} %project_tokens.2.q_ref.k_own_ref.v_own_ref.v_own_last_ref, bf16[1920,2048]{1,0:T(8,128)(2,1)} %collective-permute-done.k_far_ref.v_far_ref.v_far_last_ref, ...), custom_call_target="tpu_custom_call" | custom-call | flops 17179869184 | bytes 8388608 | tf_op jit(solution)/shard_map/heads_attention/pallas_call | solution.py:112
  160.4 0.9 slice.118
  161.9 2.2 copy-done.3
  164.2 16.3 %project_tokens.3.q_ref.k_own_ref.v_own_ref.v_own_last_ref = bf16[1920,2048]{1,0:T(8,128)(2,1)} custom-call(bf16[2048,1152]{1,0:T(8,128)(2,1)} %bitcast.1.x_ref.resid_ref, f32[1,1152]{1,0:T(1,128)S(1)} %broadcast_in_dim.27.gain_ref, f32[1,1152]{1,0:T(1,128)S(1)} %broadcast_in_dim.46.shift_ref, bf16[1920,1152]{1,0:T(8,128)(2,1)S(1)} %copy-done.3, ...), custom_call_target="tpu_custom_call" | custom-call | flops 9059696640 | bytes 17006592 | tf_op jit(solution)/shard_map/project_tokens/pallas_call | solution.py:143
  182.3 5.4 %copy.59.wk_hbm = bf16[1152,1152]{1,0:T(8,128)(2,1)} copy(bf16[1152,1152]{0,1:T(8,128)(2,1)} %bitcast.71) | data formatting | bytes 5308416 | tf_op jit(solution)/shard_map/optimization_barrier | solution.py:277
  187.7 3.4 copy.60.wv_hbm
  191.1 37.5 %heads_attention.4.refs_0_ = bf16[2048,2048]{1,0:T(8,128)(2,1)} custom-call(bf16[1920,2048]{1,0:T(8,128)(2,1)} %project_tokens.2.q_ref.k_own_ref.v_own_ref.v_own_last_ref, bf16[1920,2048]{1,0:T(8,128)(2,1)} %project_tokens.2.q_ref.k_own_ref.v_own_ref.v_own_last_ref, ...), custom_call_target="tpu_custom_call", output_to_operand_aliasing={{}: (7, {})} | custom-call | flops 17179869184 | bytes 8388608 | tf_op jit(solution)/shard_map/heads_attention/pallas_call | solution.py:112
  228.6 1.1 fusion.32
  230.5 70.2 %heads_attention.5.mixed_ref = bf16[2048,2048]{1,0:T(8,128)(2,1)} custom-call(bf16[1920,2048]{1,0:T(8,128)(2,1)} %project_tokens.3.q_ref.k_own_ref.v_own_ref.v_own_last_ref, bf16[1920,2048]{1,0:T(8,128)(2,1)} %project_tokens.3.q_ref.k_own_ref.v_own_ref.v_own_last_ref, ...), custom_call_target="tpu_custom_call", output_to_operand_aliasing={{}: (7, {})} | custom-call | flops 34359738368 | bytes 8388608 | tf_op jit(solution)/shard_map/heads_attention/pallas_call | solution.py:112
  300.7 93.8 %finish_tokens.1 = (f32[16,1152]{1,0:T(8,128)}, f32[16,1]{1,0:T(8,128)}, f32[16,1]{1,0:T(8,128)}) custom-call(bf16[2048,2048]{1,0:T(8,128)(2,1)} %heads_attention.5.mixed_ref, bf16[2048,1152]{1,0:T(8,128)(2,1)} %bitcast.1.x_ref.resid_ref, f32[6,1152]{1,0:T(8,128)} %stack.35.vec_ref, f32[1,4352]{1,0:T(1,128)} %broadcast_in_dim_reshape.3.up_bias_ref, ...), custom_call_target="tpu_custom_call" | custom-call | flops 61605937152 | bytes 41943040 | tf_op jit(solution)/shard_map/finish_tokens/pallas_call | solution.py:219
  394.6 0.9 fusion.14
  396.5 11.0 %all-gather = f32[128,74]{1,0:T(8,128)S(1)} all-gather(f32[16,74]{1,0:T(8,128)S(1)} %pad_maximum_fusion), channel_id=2, replica_groups=mesh['dp'=1,'tp'=8] {'tp'}, dimensions={0}, use_global_device_ids=true | all-gather | bytes 42624 | tf_op jit(solution)/shard_map/all_gather | solution.py:307
  409.2 11.4 %fusion.5 = bf16[4,1152]{1,0:T(4,128)(2,1)} fusion(f32[4,1152]{1,0:T(4,128)S(1)} %get-tuple-element.51, bf16[4304,1152]{1,0:T(8,128)(2,1)} %param.54, bf16[1152,4304]{0,1:T(8,128)(2,1)} %param.52, f32[4304]{0:T(1024)S(1)} %copy-done.11, f32[1152]{0:T(1024)S(1)} %copy-done.14, f32[1152]{0:T(1024)S(1)} %copy-done.15, f32[1152]{0:T(1024)S(1)} %copy-done.16, ...), kind=kOutput, calls=%fused_computation.9 | convolution fusion | flops 79540352 | bytes 19891552 | tf_op jit(solution)/shard_map/dot_general | solution.py:238
  (138 shorter events, 11.9 us)
Async XLA Ops:
  6.5 82.2 %all-gather.7.cloned.1.call-start = ((), (), s32[]{:S(2)}) async-start(), calls=%async_computation.1 | async-start | bytes 4976640 | tf_op jit(solution)/shard_map/all_gather | solution.py:270
  10.5 76.8 %all-to-all-start = ((bf16[8,256,1152]{2,1,0:T(8,128)(2,1)}), bf16[8,256,1152]{2,1,0:T(8,128)(2,1)}, u32[]{:S(2)}, u32[]{:S(2)}) async-start(bf16[8,256,1152]{2,1,0:T(8,128)(2,1)} %bitcast.72), calls=%async_computation | async-start | bytes 9437184 | tf_op jit(solution)/shard_map/all_to_all | solution.py:253
  14.8 145.6 %all-gather.9.cloned.1.call-start = ((), (), s32[]{:S(2)}) async-start(), calls=%async_computation.2 | async-start | bytes 4976640 | tf_op jit(solution)/shard_map/all_gather | solution.py:279
  23.0 65.7 %copy-start.18 = (f32[1152]{0:T(1024)S(1)}, f32[1152]{0:T(1024)}, u32[]{:S(2)}) copy-start(f32[1152]{0:T(1024)} %param.29) | copy-start | bytes 13828
  23.0 65.7 %copy-start.19 = (f32[1152]{0:T(1024)S(1)}, f32[1152]{0:T(1024)}, u32[]{:S(2)}) copy-start(f32[1152]{0:T(1024)} %param.30) | copy-start | bytes 13828
  87.3 141.3 %all-gather.11.cloned.1.call-start = ((), (), s32[]{:S(2)}) async-start(), calls=%async_computation.3 | async-start | bytes 11280384 | tf_op jit(solution)/shard_map/all_gather | solution.py:282
  88.1 212.6 %all-gather.13.cloned.1.call-start = ((), (), s32[]{:S(2)}) async-start(), calls=%async_computation.4 | async-start | bytes 5308416 | tf_op jit(solution)/shard_map/all_gather | solution.py:280
  88.6 212.1 %all-gather.15.cloned.1.call-start = ((), (), s32[]{:S(2)}) async-start(), calls=%async_computation.5 | async-start | bytes 11280384 | tf_op jit(solution)/shard_map/all_gather | solution.py:281
  109.3 13.5 %collective-permute-start = (bf16[1920,2048]{1,0:T(8,128)(2,1)}, bf16[1920,2048]{1,0:T(8,128)(2,1)}, u32[]{:S(2)}, u32[]{:S(2)}) collective-permute-start(bf16[1920,2048]{1,0:T(8,128)(2,1)} %project_tokens.2.q_ref.k_own_ref.v_own_ref.v_own_last_ref), channel_id=1, source_target_pairs={{0,1},{1,0},{2,3},{3,2},{4,5},{5,4},{6,7},{7,6}} | collective-permute-start | bytes 23592968 | tf_op jit(solution)/shard_map/ppermute | solution.py:290
  164.1 16.7 %copy-start.20 = (f32[1152]{0:T(1024)S(1)}, f32[1152]{0:T(1024)}, u32[]{:S(2)}) copy-start(f32[1152]{0:T(1024)} %param.34) | copy-start | bytes 13828
  164.1 16.7 %copy-start.21 = (f32[1152]{0:T(1024)S(1)}, f32[1152]{0:T(1024)}, u32[]{:S(2)}) copy-start(f32[1152]{0:T(1024)} %param.35) | copy-start | bytes 13828
  164.1 16.7 %copy-start.22 = (f32[1152]{0:T(1024)S(1)}, f32[1152]{0:T(1024)}, u32[]{:S(2)}) copy-start(f32[1152]{0:T(1024)} %param.36) | copy-start | bytes 13828
  164.1 16.7 %copy-start.23 = (f32[1152]{0:T(1024)S(1)}, f32[1152]{0:T(1024)}, u32[]{:S(2)}) copy-start(f32[1152]{0:T(1024)} %param.40) | copy-start | bytes 13828
  164.1 16.8 %copy-start.24 = (f32[1152]{0:T(1024)S(1)}, f32[1152]{0:T(1024)}, u32[]{:S(2)}) copy-start(f32[1152]{0:T(1024)} %param.41) | copy-start | bytes 13828
  164.1 16.8 %copy-start.25 = (f32[1152]{0:T(1024)S(1)}, f32[1152]{0:T(1024)}, u32[]{:S(2)}) copy-start(f32[1152]{0:T(1024)} %param.42) | copy-start | bytes 13828
  164.2 16.8 %copy-start.12 = (f32[2,16,72]{2,1,0:T(8,128)S(1)}, f32[2,16,72]{2,1,0:T(8,128)}, u32[]{:S(2)}) copy-start(f32[2,16,72]{2,1,0:T(8,128)} %param.47) | copy-start | bytes 27652
  180.5 50.0 %collective-permute-start.1 = (bf16[1920,2048]{1,0:T(8,128)(2,1)}, bf16[1920,2048]{1,0:T(8,128)(2,1)}, u32[]{:S(2)}, u32[]{:S(2)}) collective-permute-start(bf16[1920,2048]{1,0:T(8,128)(2,1)} %project_tokens.3.q_ref.k_own_ref.v_own_ref.v_own_last_ref), channel_id=1, source_target_pairs={{0,1},{1,0},{2,3},{3,2},{4,5},{5,4},{6,7},{7,6}} | collective-permute-start | bytes 23592968 | tf_op jit(solution)/shard_map/ppermute | solution.py:290
  300.7 94.0 %copy-start.10 = (s32[1152]{0:T(1024)S(1)}, s32[1152]{0:T(1024)}, u32[]{:S(2)}) copy-start(s32[1152]{0:T(1024)} %copy-done.9) | copy-start | bytes 13828
  300.7 107.4 %copy-start.5 = (bf16[16,72,1152]{2,1,0:T(8,128)(2,1)S(1)}, bf16[16,72,1152]{2,1,0:T(8,128)(2,1)}, u32[]{:S(2)}) copy-start(bf16[16,72,1152]{2,1,0:T(8,128)(2,1)} %param.48) | copy-start | bytes 7962628
  300.7 107.4 %copy-start.13 = (f32[1152]{0:T(1024)S(1)}, f32[1152]{0:T(1024)}, u32[]{:S(2)}) copy-start(f32[1152]{0:T(1024)} %param.49) | copy-start | bytes 13828
  394.6 14.5 %copy-start.11 = (f32[4304]{0:T(1024)S(1)}, f32[4304]{0:T(1024)}, u32[]{:S(2)}) copy-start(f32[4304]{0:T(1024)} %param.53) | copy-start | bytes 51652
  394.6 14.5 %copy-start.14 = (f32[1152]{0:T(1024)S(1)}, f32[1152]{0:T(1024)}, u32[]{:S(2)}) copy-start(f32[1152]{0:T(1024)} %param.55) | copy-start | bytes 13828
  394.6 14.5 %copy-start.15 = (f32[1152]{0:T(1024)S(1)}, f32[1152]{0:T(1024)}, u32[]{:S(2)}) copy-start(f32[1152]{0:T(1024)} %param.51) | copy-start | bytes 13828
  394.6 14.5 %copy-start.16 = (f32[1152]{0:T(1024)S(1)}, f32[1152]{0:T(1024)}, u32[]{:S(2)}) copy-start(f32[1152]{0:T(1024)} %param.50) | copy-start | bytes 13828
  (12 other events, 67.1 us)
Sparse Core Ops, SparseCore 0:
  10.6 64.0 all-gather.6
  87.5 31.9 all-gather.8
  121.3 55.4 all-gather.10
  178.4 32.9 all-gather.12
  213.1 55.4 all-gather.14

commit v6 on v5

--- a/solution.py
+++ b/solution.py
@@ -28,10 +28,11 @@
     return -(-size // multiple) * multiple
 
 
-def attention_kernel(head_dim, chunk, q_ref, k_own_ref, k_far_ref, v_own_ref, v_far_ref, v_own_last_ref, v_far_last_ref, *refs):
+def attention_kernel(head_dim, chunk, *refs):
     out_ref, scores_a, scores_b, max_a, max_b, first_out, apart = refs[-7:]
-    half_keys = k_own_ref.shape[1]
-    block = q_ref.shape[1] // 2
+    q_refs, k_refs, v_refs, v_last_refs = refs[:2], refs[2:6], refs[6:10], refs[10:14]
+    part_keys = k_refs[0].shape[1]
+    block = q_refs[0].shape[1]
     step = pl.program_id(0)
     exp_scale = head_dim ** -0.5 * LOG2E
 
@@ -49,21 +50,21 @@
             return part_total, part_mixed
         return total + part_total, mixed + part_mixed
 
-    def overlap(query_slot, score_buf, max_buf, v_own, v_far, mix_buf, mix_max):
+    def overlap(query_slot, score_buf, max_buf, v_parts, mix_buf, mix_max):
         running, total, mixed = None, None, None
         peak = jnp.max(mix_max[...], axis=0, keepdims=True)
-        queries = q_ref[:, query_slot * block:(query_slot + 1) * block]
-        for half, (k_ref, v_ref) in enumerate(((k_own_ref, v_own), (k_far_ref, v_far))):
-            for start in range(0, half_keys, chunk):
-                rows = pl.ds(half * half_keys + start, chunk)
+        queries = q_refs[query_slot][...]
+        for part, (k_ref, v_ref) in enumerate(zip(k_refs, v_parts)):
+            for start in range(0, part_keys, chunk):
+                rows = pl.ds(part * part_keys + start, chunk)
                 running = score_chunk(k_ref[:, start:start + chunk], queries, rows, score_buf, running)
                 total, mixed = mix_chunk(v_ref[:, start:start + chunk], rows, mix_buf, peak, total, mixed)
         max_buf[...] = running
         return mixed[:head_dim] / jnp.sum(total, axis=0, keepdims=True)
 
-    def write(rows, values_t):
+    def write(half, values_t):
         filled = jnp.concatenate([values_t, jnp.zeros((LANES - head_dim, block), jnp.float32)], axis=0)
-        out_ref[rows, :] = filled.T.astype(out_ref.dtype)
+        out_ref[half] = filled.T.astype(out_ref.dtype)
 
     @pl.when(step == 0)
     def _():
@@ -74,53 +75,48 @@
 
     @pl.when(apart[0] == 0)
     def _():
-        second = overlap(0, scores_a, max_a, v_own_last_ref, v_far_last_ref, scores_b, max_b)
-        write(slice(0, block), first_out[...])
-        write(slice(block, 2 * block), second)
+        second = overlap(0, scores_a, max_a, v_last_refs, scores_b, max_b)
+        write(0, first_out[...])
+        write(1, second)
 
     @pl.when(step < pl.num_programs(0) - 1)
     def _():
-        first_out[...] = overlap(1, scores_b, max_b, v_own_ref, v_far_ref, scores_a, max_a)
-
-
-def heads_attention(qkv_own, qkv_far, head_dim, heads, place, stride, previous, n_out):
+        first_out[...] = overlap(1, scores_b, max_b, v_refs, scores_a, max_a)
+
+
+def heads_attention(parts, head_dim, heads, place, stride, previous, n_out):
     first, count = heads
-    n_own = qkv_own.shape[1]
-    pair = n_own // 2
-    per_head = n_own // pair
+    n_part = parts[0].shape[1]
+    block = n_part // 2
+    per_head = n_part // block
     last = count * per_head - 1
     now = lambda i: first + jnp.minimum(i, last) // per_head
     before = lambda i: first + jnp.maximum(i - 1, 0) // per_head
     rows = round_up(head_dim, 16)
-    whole = (rows, n_own)
-    in_specs = [
-        pl.BlockSpec((rows, pair), lambda i: (3 * now(i), jnp.minimum(i, last) % per_head)),
-        pl.BlockSpec(whole, lambda i: (3 * now(i) + 1, 0)),
-        pl.BlockSpec(whole, lambda i: (3 * now(i) + 1, 0)),
-        pl.BlockSpec(whole, lambda i: (3 * now(i) + 2, 0)),
-        pl.BlockSpec(whole, lambda i: (3 * now(i) + 2, 0)),
-        pl.BlockSpec(whole, lambda i: (3 * before(i) + 2, 0)),
-        pl.BlockSpec(whole, lambda i: (3 * before(i) + 2, 0)),
-    ]
-    operands = [qkv_own, qkv_own, qkv_far, qkv_own, qkv_far, qkv_own, qkv_far]
+    whole = (rows, n_part)
+    in_specs = [pl.BlockSpec((rows, block), lambda i: (3 * now(i), jnp.minimum(i, last) % per_head))] * 2
+    in_specs += [pl.BlockSpec(whole, lambda i: (3 * now(i) + 1, 0))] * 4
+    in_specs += [pl.BlockSpec(whole, lambda i: (3 * now(i) + 2, 0))] * 4
+    in_specs += [pl.BlockSpec(whole, lambda i: (3 * before(i) + 2, 0))] * 4
+    operands = [*parts[:2], *parts, *parts, *parts]
     aliases = {}
     if previous is not None:
         in_specs.append(pl.BlockSpec(memory_space=pl.ANY))
         operands.append(previous)
-        aliases = {7: 0}
-    scored = count * n_own * 2 * n_own
+        aliases = {len(operands) - 1: 0}
+    scored = count * 2 * n_part * 4 * n_part
     return pl.pallas_call(
         functools.partial(attention_kernel, head_dim, 256),
         grid=(last + 2,),
-        out_shape=jax.ShapeDtypeStruct((n_own, n_out * LANES), jnp.bfloat16),
+        out_shape=jax.ShapeDtypeStruct((2, n_part, n_out * LANES), jnp.bfloat16),
         in_specs=in_specs,
-        out_specs=pl.BlockSpec((pair, LANES), lambda i: (jnp.maximum(i - 1, 0) % per_head, place + stride * before(i))),
+        out_specs=pl.BlockSpec((2, block, LANES), lambda i: (0, jnp.maximum(i - 1, 0) % per_head, place + stride * before(i))),
         scratch_shapes=[
-            pltpu.VMEM((2 * n_own, pair // 2), jnp.float32),
-            pltpu.VMEM((2 * n_own, pair // 2), jnp.float32),
-            pltpu.VMEM((8, pair // 2), jnp.float32),
-            pltpu.VMEM((8, pair // 2), jnp.float32),
-            pltpu.VMEM((head_dim, pair // 2), jnp.float32),
+            pltpu.VMEM((4 * n_part, block), jnp.float32),
+            pltpu.VMEM((4 * n_part, block), jnp.float32),
+            pltpu.VMEM((8, block), jnp.float32),
+            pltpu.VMEM((8, block), jnp.float32),
+            pltpu.VMEM((head_dim, block), jnp.float32),
             pltpu.SMEM((1,), jnp.int32),
         ],
         input_output_aliases=aliases,
@@ -163,7 +159,7 @@
     return high + middle + low
 
 
-def finish_kernel(head_dim, up_chunk, mixed_ref, resid_ref, vec_ref, up_bias_ref, pool_bias_ref, probe_ref, w_out_hbm, w_up_hbm, w_down_hbm, wk_hbm, wv_hbm,
+def finish_kernel(head_dim, up_chunk, mixed_ref, resid_a_ref, resid_b_ref, vec_ref, up_bias_ref, pool_bias_ref, probe_ref, w_out_hbm, w_up_hbm, w_down_hbm, wk_hbm, wv_hbm,
                   pooled_ref, total_ref, peak_ref, w_out, w_up, w_down, wk, wv, units, sems):
     step = pl.program_id(0)
     copies = [pltpu.make_async_copy(src, dst, sems.at[index]) for index, (src, dst) in enumerate(
@@ -185,7 +181,8 @@
     b_out, ln2_gain, ln2_bias, b_down, lnf_gain, lnf_bias = (vec_ref[index:index + 1, :] for index in range(6))
     arrive(0)
     attn_local = jnp.dot(mixed_ref[...], w_out[...], preferred_element_type=jnp.float32)
-    resid_one = (resid_ref[...].astype(jnp.float32) + attn_local + b_out).astype(jnp.bfloat16)
+    resid = jnp.where(step < pl.num_programs(0) // 2, resid_a_ref[...].astype(jnp.float32), resid_b_ref[...].astype(jnp.float32))
+    resid_one = (resid + attn_local + b_out).astype(jnp.bfloat16)
     hidden_two = layer_norm(resid_one.astype(jnp.float32), ln2_gain, ln2_bias).astype(jnp.bfloat16)
     arrive(1)
     n_units = w_up.shape[0]
@@ -210,9 +207,10 @@
     peak_ref[...] = peak
 
 
-def finish_tokens(mixed, resid, vectors, up_bias, pool_bias, probe, weights, head_dim, block=512):
-    n_own, width = resid.shape
+def finish_tokens(mixed, resid_parts, vectors, up_bias, pool_bias, probe, weights, head_dim, block=512):
+    n_own, width = mixed.shape[0], resid_parts[0].shape[1]
     n_heads = probe.shape[0]
+    per_part = n_own // 2 // block
     n_units = up_bias.shape[1]
     fixed = lambda shape: pl.BlockSpec(shape, lambda i: (0, 0))
     small = [vectors, up_bias, pool_bias, probe]
@@ -220,7 +218,7 @@
         functools.partial(finish_kernel, head_dim, 512),
         grid=(n_own // block,),
         out_shape=[jax.ShapeDtypeStruct((n_heads, columns), jnp.float32) for columns in (width, 1, 1)],
-        in_specs=[pl.BlockSpec((block, mixed.shape[1]), lambda i: (i, 0)), pl.BlockSpec((block, width), lambda i: (i, 0))]
+        in_specs=[pl.BlockSpec((block, mixed.shape[1]), lambda i: (i, 0)), pl.BlockSpec((block, width), lambda i: (jnp.minimum(i, per_part - 1), 0)), pl.BlockSpec((block, width), lambda i: (jnp.maximum(i - per_part, 0), 0))]
         + [fixed(array.shape) for array in small] + [pl.BlockSpec(memory_space=pl.ANY)] * len(weights),
         out_specs=[fixed((n_heads, columns)) for columns in (width, 1, 1)],
         scratch_shapes=[pltpu.VMEM(weight.shape, jnp.bfloat16) for weight in weights]
@@ -228,7 +226,7 @@
         compiler_params=pltpu.CompilerParams(dimension_semantics=('arbitrary',), vmem_limit_bytes=60 * 1024 * 1024),
         cost_estimate=pl.CostEstimate(flops=2 * n_own * sum(weight.size for weight in weights), bytes_accessed=40 * 1024 * 1024, transcendentals=n_own * n_units),
         name='finish_tokens',
-    )(mixed, resid, *small, *weights)
+    )(mixed, *resid_parts, *small, *weights)
 
 
 def map_tail(pooled_heads, map_wo, map_bo, map_ln_gain, map_ln_bias, map_w_up, map_b_up, map_w_down, map_b_down):
@@ -250,7 +248,12 @@
         hidden_units = w_up.shape[1]
         own = n_images * run
 
-        resid = row_major(lax.all_to_all(row_major(tokens.reshape(tp_size, own // tp_size, width)), 'tp', split_axis=0, concat_axis=0, tiled=True).reshape(own, width))
+        pieces = tokens.reshape(tp_size, 2, own // tp_size // 2, width)
+
+        def send(piece):
+            return row_major(lax.all_to_all(row_major(pieces[:, piece]), 'tp', split_axis=0, concat_axis=0, tiled=True).reshape(own // 2, width))
+
+        resid_a, resid_b = send(0), send(1)
 
         rows_padded = round_up(head_dim, 16)
         shards = []
@@ -272,37 +275,43 @@
         head_of = jnp.arange(width) // head_dim
         on_head = head_of[:, None] == jnp.arange(n_heads)[None]
         probe_cols = jnp.where(on_head.T, probe_q[None], jnp.zeros((), jnp.bfloat16))
-        pool_wk, pool_wv = map_wkv[:, 0].reshape(width, width), map_wkv[:, 1].reshape(width, width)
+        pool_wk, pool_wv = (row_major(map_wkv[:, index].reshape(width, width)) for index in range(2))
+        vectors = jnp.stack([b_out, ln2_gain, ln2_bias, b_down, lnf_gain, lnf_bias])
         w_out_p = jnp.pad(w_out, ((0, 0), (0, LANES - head_dim), (0, 0))).reshape(groups * LANES, width)
-        resid, later, w_out_p, w_up_t, w_down_p, probe_cols, pool_wk, pool_wv = lax.optimization_barrier(
-            (resid, shards[1:], w_out_p, w_up_t, w_down_p, probe_cols, pool_wk, pool_wv))
+        def project(group_rows, part):
+            bias_row = group_rows.reshape(tp_size, 3 * rows_padded, width)[:, 2 * rows_padded + head_dim, :9 * head_dim]
+            bias_row = bias_row.reshape(tp_size, 3, 3, head_dim)
+            bias = join_three([bias_row[:, term] for term in range(3)])
+            bias = jnp.pad(bias, ((0, 0), (0, 0), (0, rows_padded - head_dim))).reshape(-1, 1)
+            return project_tokens(part, ln1_gain, ln1_bias, group_rows, bias)
+
+        def swap(part):
+            return lax.ppermute(part, 'tp', partner)
+
+        first_a = project(gathered[0], resid_a)
+        far_a = swap(first_a)
+        first_b = project(gathered[0], resid_b)
+        far_a_later, later_parts, later, w_out_p, w_up_t, w_down_p, probe_cols, pool_wk, pool_wv, vectors = lax.optimization_barrier(
+            (far_a, (resid_a, resid_b), shards[1:], w_out_p, w_up_t, w_down_p, probe_cols, pool_wk, pool_wv, vectors))
         gathered += [lax.all_gather(shard, 'tp', axis=0, tiled=True) for shard in later]
         w_out_all = lax.all_gather(w_out_p, 'tp', axis=0, tiled=True)
         w_up_all = lax.all_gather(w_up_t, 'tp', axis=0, tiled=True)
         w_down_all = lax.all_gather(w_down_p, 'tp', axis=0, tiled=True)
 
-        def projections(group, resid):
-            bias_row = gathered[group].reshape(tp_size, 3 * rows_padded, width)[:, 2 * rows_padded + head_dim, :9 * head_dim]
-            bias_row = bias_row.reshape(tp_size, 3, 3, head_dim)
-            bias = join_three([bias_row[:, part] for part in range(3)])
-            bias = jnp.pad(bias, ((0, 0), (0, 0), (0, rows_padded - head_dim))).reshape(-1, 1)
-            qkv_t = project_tokens(resid, ln1_gain, ln1_bias, gathered[group], bias)
-            return qkv_t, lax.ppermute(qkv_t, 'tp', partner)
-
         half = tp_size // 2
-        first_group = projections(0, resid)
-        mixed = heads_attention(*first_group, head_dim, (0, half), 0, groups, None, n_heads)
-        mixed, resid_later, gathered[1] = lax.optimization_barrier((mixed, resid, gathered[1]))
-        second_group = projections(1, resid_later)
-        mixed = heads_attention(*first_group, head_dim, (half, half), 0, groups, mixed, n_heads)
-        mixed = heads_attention(*second_group, head_dim, (0, tp_size), 1, groups, mixed, n_heads)
+        first_group = [first_a, first_b, far_a, swap(first_b)]
+        mixed = heads_attention(first_group, head_dim, (0, half), 0, groups, None, n_heads)
+        mixed, later_parts, gathered[1] = lax.optimization_barrier((mixed, later_parts, gathered[1]))
+        second_group = [project(gathered[1], part) for part in later_parts]
+        second_group += [swap(part) for part in second_group]
+        mixed = heads_attention([first_a, first_b, far_a_later, first_group[3]], head_dim, (half, half), 0, groups, mixed, n_heads)
+        mixed = heads_attention(second_group, head_dim, (0, tp_size), 1, groups, mixed, n_heads)
 
         bias_rows = w_down_all.reshape(tp_size, padded, width)[:, hidden_units:hidden_units + 2]
         b_up_all = join_three([bias_rows[:, 0, :hidden_units], bias_rows[:, 0, hidden_units:2 * hidden_units], bias_rows[:, 1, :hidden_units]])
         b_up_all = jnp.pad(b_up_all, ((0, 0), (0, padded - hidden_units))).reshape(tp_size * padded)
-        vectors = jnp.stack([b_out, ln2_gain, ln2_bias, b_down, lnf_gain, lnf_bias])
         every_head, total, peak = finish_tokens(
-            mixed, resid, vectors, b_up_all[None], map_bkv.reshape(2, width), probe_cols, (w_out_all, w_up_all, w_down_all, pool_wk, pool_wv), head_dim)
+            mixed.reshape(own, n_heads * LANES), later_parts, vectors, b_up_all[None], map_bkv.reshape(2, width), probe_cols, (w_out_all, w_up_all, w_down_all, pool_wk, pool_wv), head_dim)
         pooled = jnp.sum(jnp.where(on_head.T, every_head, 0.0).reshape(n_heads, n_heads, head_dim), axis=1)
         parts = lax.all_gather(jnp.concatenate([pooled, total, peak], axis=-1), 'tp', axis=0, tiled=False)
         parts = parts.reshape(n_images, tp_size // n_images, n_heads, head_dim + 2)

time: 431 us -> 446 us (1.035)
  local copies, waits for them, and re-layouts: 31.2 us -> 51.7 us
  waiting for transfers between devices: 73.9 us -> 55.4 us
  Pallas kernels: 272 us -> 277 us
    all_to_all x1 -> x2, waiting for transfers between devices: 59 us -> 0.01 us  [send(): lax.all_to_all(row_major(pieces[:, piece]), 'tp', split_axis=0, concat_ax...]
    all_gather x1, waiting for transfers between devices: 0.02 us -> 45.5 us  [local_program(): gathered = [lax.all_gather(shards[0], 'tp', axis=0, tiled=True)]]
    another operation x2 -> x4, local copies, waits for them, and re-layouts: 0.19 us -> 10.7 us  [the longest x2 10.5 us: local_program(): map_wkv[:, index].reshape(width, width)]
    unnamed x70, local copies, waits for them, and re-layouts: 5.57 us -> 14.9 us
    optimization_barrier x2 -> x0, local copies, waits for them, and re-layouts: 8.81 us -> none  [local_program(): lax.optimization_barrier((resid, shards[1:], w_out_p, w_up_t, w_down_p, p...]
    ppermute x2 -> x4, waiting for transfers between devices: 13.5 us -> 8.19 us  [swap(): return lax.ppermute(part, 'tp', partner)]
    squeeze x0 -> x1, local copies, waits for them, and re-layouts: none -> 5.06 us  [send(): pieces[:, piece]]
    pallas_call x2 -> x4, Pallas kernels: 33.1 us -> 36.9 us  [project_tokens(): pl.pallas_call(project_kernel, grid=(n_own // block,), out_shape=jax.Shap...]
  transfers between devices with their start and end apart: 8 -> 11, of which waited for: 2 -> 2; matrix products, arithmetic and copies ran while one was open for 7% -> 9% of each run, Pallas kernels for 42% -> 42%
where the time goes in v6:
time: 446 us; the launch traced here: 439 us
  Pallas kernels  277 us (62%)
  waiting for transfers between devices  55.4 us (12%)
  local copies, waits for them, and re-layouts  51.7 us (12%)
  between operations  13.9 us (3%)
  matrix products  13 us (3%)
  blocking collectives  12.2 us (3%)
  starting transfers between devices  8.82 us (2%)
  other arithmetic  7.25 us (2%)
    pallas_call x3, Pallas kernels, heads_attention(): pl.pallas_call(functools.partial(attention_kernel, head_dim, 256), grid=(...  145 us
    pallas_call x1, Pallas kernels, finish_tokens(): pl.pallas_call(functools.partial(finish_kernel, head_dim, 512), grid=(n_o...  94.1 us
    all_gather x1, waiting for transfers between devices, local_program(): gathered = [lax.all_gather(shards[0], 'tp', axis=0, tiled=True)]  45.5 us
    pallas_call x4, Pallas kernels, project_tokens(): pl.pallas_call(project_kernel, grid=(n_own // block,), out_shape=jax.Shap...  36.9 us
    unnamed x70, local copies, waits for them, and re-layouts  14.9 us
    all_gather x1, blocking collectives, local_program(): lax.all_gather(jnp.concatenate([pooled, total, peak], axis=-1), 'tp', axi...  12.2 us
    dot_general x1, matrix products, map_tail(): jnp.dot(map_act, map_w_down, preferred_element_type=jnp.float32)  11.4 us
    another operation x2, local copies, waits for them, and re-layouts, local_program(): map_wkv[:, index].reshape(width, width)  10.5 us
  transfers between devices with their start and end apart: 11, of which 2 were waited for; matrix products, arithmetic and copies ran while one was open for 9% of the time, Pallas kernels for 42%

profile of v6, /device:TPU:0, one launch (start us, length us, event | category | flops | bytes accessed | tf_op | source)
XLA Modules:
  0.0 438.8 jit_solution(11021761996592280868)
XLA Ops:
  9.7 5.1 %slice_bitcast_fusion = (bf16[8,128,1152]{2,1,0:T(8,128)(2,1)}, bf16[8,128,1152]{2,1,0:T(8,128)(2,1)}) fusion(bf16[8,2,128,1152]{3,2,1,0:T(8,128)(2,1)} %bitcast.83), kind=kLoop, calls=%fused_computation.5 | loop fusion | bytes 9437184 | tf_op jit(solution)/shard_map/squeeze | solution.py:254
  14.8 4.3 all-to-all-start
  19.5 45.5 %all-gather.7.cloned.1.call-done.weight_ref = bf16[1920,1152]{1,0:T(8,128)(2,1)} async-done(((bf16[240,1152]{1,0:T(8,128)(2,1)}), bf16[1920,1152]{1,0:T(8,128)(2,1)}) %all-gather.7.cloned.1.call-update) | async-done | bytes 4423696 | tf_op jit(solution)/shard_map/all_gather | solution.py:273
  67.5 3.1 all-to-all-start.1
  71.9 2.3 copy-done.6
  74.1 9.4 %project_tokens.4.refs_0_.refs_2_.refs_6_.refs_10_ = bf16[1920,1024]{1,0:T(8,128)(2,1)} custom-call(bf16[1024,1152]{1,0:T(8,128)(2,1)} %bitcast.2.x_ref.resid_a_ref, f32[1,1152]{1,0:T(1,128)S(1)} %broadcast_in_dim.24.gain_ref, f32[1,1152]{1,0:T(1,128)S(1)} %broadcast_in_dim.25.shift_ref, bf16[1920,1152]{1,0:T(8,128)(2,1)S(1)} %copy-done.6, ...), custom_call_target="tpu_custom_call" | custom-call | flops 4529848320 | bytes 10715136 | tf_op jit(solution)/shard_map/project_tokens/pallas_call | solution.py:139
  83.9 5.3 %fusion.72 = (bf16[1152,1,16,72]{0,3,2,1:T(8,128)(2,1)}, bf16[1152,1,16,72]{0,3,2,1:T(8,128)(2,1)}) fusion(bf16[1152,2,16,72]{0,3,2,1:T(8,128)(2,1)} %param.46), kind=kLoop, calls=%fused_computation.125 | loop fusion | bytes 10616832 | tf_op jit(solution)/shard_map/slice | solution.py:278
  89.2 5.2 %copy.68.wk_hbm = bf16[1152,1152]{1,0:T(8,128)(2,1)} copy(bf16[1152,1152]{0,1:T(8,128)(2,1)} %bitcast.81) | data formatting | bytes 5308416 | tf_op jit(solution)/shard_map/reshape;squeeze | solution.py:278
  94.4 5.3 %copy.69.wv_hbm = bf16[1152,1152]{1,0:T(8,128)(2,1)} copy(bf16[1152,1152]{0,1:T(8,128)(2,1)} %bitcast.80) | data formatting | bytes 5308416 | tf_op jit(solution)/shard_map/reshape;squeeze | solution.py:278
  99.8 2.4 pad.53
  108.9 2.7 fusion.7
  114.2 2.2 copy-done.7
  116.5 8.4 %project_tokens.5.refs_1_.refs_3_.refs_7_.refs_11_ = bf16[1920,1024]{1,0:T(8,128)(2,1)S(1)} custom-call(bf16[1024,1152]{1,0:T(8,128)(2,1)} %bitcast.12.x_ref.resid_b_ref, f32[1,1152]{1,0:T(1,128)S(1)} %broadcast_in_dim.24.gain_ref, f32[1,1152]{1,0:T(1,128)S(1)} %broadcast_in_dim.25.shift_ref, bf16[1920,1152]{1,0:T(8,128)(2,1)S(1)} %copy-done.7, ...), custom_call_target="tpu_custom_call" | custom-call | flops 4529848320 | bytes 10715136 | tf_op jit(solution)/shard_map/project_tokens/pallas_call | solution.py:139
  125.1 8.2 %collective-permute-done.1.refs_5_.refs_9_.refs_13_ = bf16[1920,1024]{1,0:T(8,128)(2,1)S(1)} collective-permute-done((bf16[1920,1024]{1,0:T(8,128)(2,1)S(1)}, bf16[1920,1024]{1,0:T(8,128)(2,1)S(1)}, u32[]{:S(2)}, u32[]{:S(2)}) %collective-permute-start.1) | collective-permute-done | bytes 3932192 | tf_op jit(solution)/shard_map/ppermute | solution.py:289
  135.1 37.5 %heads_attention.3.refs_14_ = bf16[2,1024,2048]{2,1,0:T(8,128)(2,1)} custom-call(bf16[1920,1024]{1,0:T(8,128)(2,1)} %project_tokens.4.refs_0_.refs_2_.refs_6_.refs_10_, bf16[1920,1024]{1,0:T(8,128)(2,1)S(1)} %project_tokens.5.refs_1_.refs_3_.refs_7_.refs_11_, bf16[1920,1024]{1,0:T(8,128)(2,1)} %project_tokens.4.refs_0_.refs_2_.refs_6_.refs_10_, ...), custom_call_target="tpu_custom_call" | custom-call | flops 17179869184 | bytes 8388608 | tf_op jit(solution)/shard_map/heads_attention/pallas_call | solution.py:108
  176.1 2.2 copy-done.8
  178.3 9.4 %project_tokens.7.refs_1_.refs_3_.refs_7_.refs_11_ = bf16[1920,1024]{1,0:T(8,128)(2,1)} custom-call(bf16[1024,1152]{1,0:T(8,128)(2,1)} %bitcast.12.x_ref.resid_b_ref, f32[1,1152]{1,0:T(1,128)S(1)} %broadcast_in_dim.24.gain_ref, f32[1,1152]{1,0:T(1,128)S(1)} %broadcast_in_dim.25.shift_ref, bf16[1920,1152]{1,0:T(8,128)(2,1)S(1)} %copy-done.8, ...), custom_call_target="tpu_custom_call" | custom-call | flops 4529848320 | bytes 10715136 | tf_op jit(solution)/shard_map/project_tokens/pallas_call | solution.py:139
  187.9 9.8 %project_tokens.6.refs_0_.refs_2_.refs_6_.refs_10_ = bf16[1920,1024]{1,0:T(8,128)(2,1)} custom-call(bf16[1024,1152]{1,0:T(8,128)(2,1)} %bitcast.2.x_ref.resid_a_ref, f32[1,1152]{1,0:T(1,128)S(1)} %broadcast_in_dim.24.gain_ref, f32[1,1152]{1,0:T(1,128)S(1)} %broadcast_in_dim.25.shift_ref, bf16[1920,1152]{1,0:T(8,128)(2,1)S(1)} %copy-done.8, ...), custom_call_target="tpu_custom_call" | custom-call | flops 4529848320 | bytes 10715136 | tf_op jit(solution)/shard_map/project_tokens/pallas_call | solution.py:139
  198.7 2.1 copy-done.3
  200.8 37.5 %heads_attention.4.refs_14_ = bf16[2,1024,2048]{2,1,0:T(8,128)(2,1)} custom-call(bf16[1920,1024]{1,0:T(8,128)(2,1)} %project_tokens.4.refs_0_.refs_2_.refs_6_.refs_10_, bf16[1920,1024]{1,0:T(8,128)(2,1)S(1)} %copy-done.3, bf16[1920,1024]{1,0:T(8,128)(2,1)} %project_tokens.4.refs_0_.refs_2_.refs_6_.refs_10_, ...), custom_call_target="tpu_custom_call", output_to_operand_aliasing={{}: (14, {})} | custom-call | flops 17179869184 | bytes 8388608 | tf_op jit(solution)/shard_map/heads_attention/pallas_call | solution.py:108
  238.3 70.4 %heads_attention.5 = bf16[2,1024,2048]{2,1,0:T(8,128)(2,1)} custom-call(bf16[1920,1024]{1,0:T(8,128)(2,1)} %project_tokens.6.refs_0_.refs_2_.refs_6_.refs_10_, bf16[1920,1024]{1,0:T(8,128)(2,1)} %project_tokens.7.refs_1_.refs_3_.refs_7_.refs_11_, bf16[1920,1024]{1,0:T(8,128)(2,1)} %project_tokens.6.refs_0_.refs_2_.refs_6_.refs_10_, ...), custom_call_target="tpu_custom_call", output_to_operand_aliasing={{}: (14, {})} | custom-call | flops 34359738368 | bytes 8388608 | tf_op jit(solution)/shard_map/heads_attention/pallas_call | solution.py:108
  310.7 94.1 %finish_tokens.1 = (f32[16,1152]{1,0:T(8,128)}, f32[16,1]{1,0:T(8,128)}, f32[16,1]{1,0:T(8,128)}) custom-call(bf16[2048,2048]{1,0:T(8,128)(2,1)} %bitcast.82, bf16[1024,1152]{1,0:T(8,128)(2,1)} %bitcast.2.x_ref.resid_a_ref, bf16[1024,1152]{1,0:T(8,128)(2,1)} %bitcast.12.x_ref.resid_b_ref, f32[6,1152]{1,0:T(8,128)} %stack.35.vec_ref, ...), custom_call_target="tpu_custom_call" | custom-call | flops 61605937152 | bytes 41943040 | tf_op jit(solution)/shard_map/finish_tokens/pallas_call | solution.py:217
  406.7 12.2 %all-gather = f32[128,74]{1,0:T(8,128)S(1)} all-gather(f32[16,74]{1,0:T(8,128)S(1)} %pad_maximum_fusion), channel_id=2, replica_groups=mesh['dp'=1,'tp'=8] {'tp'}, dimensions={0}, use_global_device_ids=true | all-gather | bytes 42624 | tf_op jit(solution)/shard_map/all_gather | solution.py:316
  420.6 11.4 %fusion.5 = bf16[4,1152]{1,0:T(4,128)(2,1)} fusion(f32[4,1152]{1,0:T(4,128)S(1)} %get-tuple-element.61, bf16[4304,1152]{1,0:T(8,128)(2,1)} %param.54, bf16[1152,4304]{0,1:T(8,128)(2,1)} %param.52, f32[4304]{0:T(1024)S(1)} %copy-done.16, f32[1152]{0:T(1024)S(1)} %copy-done.19, f32[1152]{0:T(1024)S(1)} %copy-done.20, f32[1152]{0:T(1024)S(1)} %copy-done.21, ...), kind=kOutput, calls=%fused_computation.11 | convolution fusion | flops 79540352 | bytes 19891552 | tf_op jit(solution)/shard_map/dot_general | solution.py:236
  (147 shorter events, 28.7 us)
Async XLA Ops:
  6.5 101.4 %copy-start = (bf16[1152,16,72]{0,2,1:T(8,128)(2,1)S(1)}, bf16[1152,16,72]{0,2,1:T(8,128)(2,1)}, u32[]{:S(2)}) copy-start(bf16[1152,16,72]{0,2,1:T(8,128)(2,1)} %param.44) | copy-start | bytes 7962628
  6.5 58.5 %all-gather.7.cloned.1.call-start = ((), (), s32[]{:S(2)}) async-start(), calls=%async_computation.2 | async-start | bytes 4976640 | tf_op jit(solution)/shard_map/all_gather | solution.py:273
  14.8 52.7 %all-to-all-start = ((bf16[8,128,1152]{2,1,0:T(8,128)(2,1)}), bf16[8,128,1152]{2,1,0:T(8,128)(2,1)}, u32[]{:S(2)}, u32[]{:S(2)}) async-start(bf16[8,128,1152]{2,1,0:T(8,128)(2,1)} %get-tuple-element.48), calls=%async_computation | async-start | bytes 4718592 | tf_op jit(solution)/shard_map/all_to_all | solution.py:254
  67.5 44.8 %all-to-all-start.1 = ((bf16[8,128,1152]{2,1,0:T(8,128)(2,1)}), bf16[8,128,1152]{2,1,0:T(8,128)(2,1)}, u32[]{:S(2)}, u32[]{:S(2)}) async-start(bf16[8,128,1152]{2,1,0:T(8,128)(2,1)} %get-tuple-element.47), calls=%async_computation.1 | async-start | bytes 4718592 | tf_op jit(solution)/shard_map/all_to_all | solution.py:254
  70.6 103.9 %all-gather.9.cloned.1.call-start = ((), (), s32[]{:S(2)}) async-start(), calls=%async_computation.3 | async-start | bytes 4976640 | tf_op jit(solution)/shard_map/all_gather | solution.py:296
  83.5 28.7 %collective-permute-start = (bf16[1920,1024]{1,0:T(8,128)(2,1)}, bf16[1920,1024]{1,0:T(8,128)(2,1)}, u32[]{:S(2)}, u32[]{:S(2)}) collective-permute-start(bf16[1920,1024]{1,0:T(8,128)(2,1)} %project_tokens.4.refs_0_.refs_2_.refs_6_.refs_10_), channel_id=1, source_target_pairs={{0,1},{1,0},{2,3},{3,2},{4,5},{5,4},{6,7},{7,6}} | collective-permute-start | bytes 11796488 | tf_op jit(solution)/shard_map/ppermute | solution.py:289
  94.4 5.3 %copy-start.26 = (bf16[1152]{0:T(1024)(128)(2,1)S(1)}, bf16[1152]{0:T(1024)(128)(2,1)}, u32[]{:S(2)}) copy-start(bf16[1152]{0:T(1024)(128)(2,1)} %param.43) | copy-start | bytes 6916
  94.4 5.3 %copy-start.24 = (f32[16,72]{1,0:T(8,128)S(1)}, f32[16,72]{1,0:T(8,128)}, u32[]{:S(2)}) copy-start(f32[16,72]{1,0:T(8,128)} %param.45) | copy-start | bytes 13828
  94.4 7.8 %copy-start.13 = (bf16[2,72,1152]{2,1,0:T(8,128)(2,1)S(1)}, bf16[2,72,1152]{2,1,0:T(8,128)(2,1)}, u32[]{:S(2)}) copy-start(bf16[2,72,1152]{2,1,0:T(8,128)(2,1)} %param.33) | copy-start | bytes 995332
  112.3 196.5 %all-gather.11.cloned.1.call-start = ((), (), s32[]{:S(2)}) async-start(), calls=%async_computation.4 | async-start | bytes 11280384 | tf_op jit(solution)/shard_map/all_gather | solution.py:299
  113.0 197.6 %all-gather.13.cloned.1.call-start = ((), (), s32[]{:S(2)}) async-start(), calls=%async_computation.5 | async-start | bytes 5308416 | tf_op jit(solution)/shard_map/all_gather | solution.py:297
  113.6 197.1 %all-gather.15.cloned.1.call-start = ((), (), s32[]{:S(2)}) async-start(), calls=%async_computation.6 | async-start | bytes 11280384 | tf_op jit(solution)/shard_map/all_gather | solution.py:298
  124.9 8.4 %collective-permute-start.1 = (bf16[1920,1024]{1,0:T(8,128)(2,1)S(1)}, bf16[1920,1024]{1,0:T(8,128)(2,1)S(1)}, u32[]{:S(2)}, u32[]{:S(2)}) collective-permute-start(bf16[1920,1024]{1,0:T(8,128)(2,1)S(1)} %project_tokens.5.refs_1_.refs_3_.refs_7_.refs_11_), channel_id=1, source_target_pairs={{0,1},{1,0},{2,3},{3,2},{4,5},{5,4},{6,7},{7,6}} | collective-permute-start | bytes 11796488 | tf_op jit(solution)/shard_map/ppermute | solution.py:289
  187.7 10.3 %copy-start.17 = (f32[2,16,72]{2,1,0:T(8,128)S(1)}, f32[2,16,72]{2,1,0:T(8,128)}, u32[]{:S(2)}) copy-start(f32[2,16,72]{2,1,0:T(8,128)} %param.47) | copy-start | bytes 27652
  187.7 50.6 %collective-permute-start.3 = (bf16[1920,1024]{1,0:T(8,128)(2,1)}, bf16[1920,1024]{1,0:T(8,128)(2,1)}, u32[]{:S(2)}, u32[]{:S(2)}) collective-permute-start(bf16[1920,1024]{1,0:T(8,128)(2,1)} %project_tokens.7.refs_1_.refs_3_.refs_7_.refs_11_), channel_id=1, source_target_pairs={{0,1},{1,0},{2,3},{3,2},{4,5},{5,4},{6,7},{7,6}} | collective-permute-start | bytes 11796488 | tf_op jit(solution)/shard_map/ppermute | solution.py:289
  197.7 40.7 %collective-permute-start.2 = (bf16[1920,1024]{1,0:T(8,128)(2,1)}, bf16[1920,1024]{1,0:T(8,128)(2,1)}, u32[]{:S(2)}, u32[]{:S(2)}) collective-permute-start(bf16[1920,1024]{1,0:T(8,128)(2,1)} %project_tokens.6.refs_0_.refs_2_.refs_6_.refs_10_), channel_id=1, source_target_pairs={{0,1},{1,0},{2,3},{3,2},{4,5},{5,4},{6,7},{7,6}} | collective-permute-start | bytes 11796488 | tf_op jit(solution)/shard_map/ppermute | solution.py:289
  310.7 94.2 %copy-start.15 = (s32[1152]{0:T(1024)S(1)}, s32[1152]{0:T(1024)}, u32[]{:S(2)}) copy-start(s32[1152]{0:T(1024)} %copy-done.14) | copy-start | bytes 13828
  310.7 108.9 %copy-start.10 = (bf16[16,72,1152]{2,1,0:T(8,128)(2,1)S(1)}, bf16[16,72,1152]{2,1,0:T(8,128)(2,1)}, u32[]{:S(2)}) copy-start(bf16[16,72,1152]{2,1,0:T(8,128)(2,1)} %param.48) | copy-start | bytes 7962628
  310.7 108.9 %copy-start.18 = (f32[1152]{0:T(1024)S(1)}, f32[1152]{0:T(1024)}, u32[]{:S(2)}) copy-start(f32[1152]{0:T(1024)} %param.49) | copy-start | bytes 13828
  404.8 15.8 %copy-start.16 = (f32[4304]{0:T(1024)S(1)}, f32[4304]{0:T(1024)}, u32[]{:S(2)}) copy-start(f32[4304]{0:T(1024)} %param.53) | copy-start | bytes 51652
  404.8 15.8 %copy-start.19 = (f32[1152]{0:T(1024)S(1)}, f32[1152]{0:T(1024)}, u32[]{:S(2)}) copy-start(f32[1152]{0:T(1024)} %param.55) | copy-start | bytes 13828
  404.8 15.8 %copy-start.20 = (f32[1152]{0:T(1024)S(1)}, f32[1152]{0:T(1024)}, u32[]{:S(2)}) copy-start(f32[1152]{0:T(1024)} %param.51) | copy-start | bytes 13828
  404.9 15.8 %copy-start.21 = (f32[1152]{0:T(1024)S(1)}, f32[1152]{0:T(1024)}, u32[]{:S(2)}) copy-start(f32[1152]{0:T(1024)} %param.50) | copy-start | bytes 13828
  420.6 11.4 %copy-start.1 = (bf16[1152,16,72]{0,2,1:T(8,128)(2,1)S(1)}, bf16[1152,16,72]{0,2,1:T(8,128)(2,1)}, u32[]{:S(2)}) copy-start(bf16[1152,16,72]{0,2,1:T(8,128)(2,1)} %param.44) | copy-start | bytes 7962628
  (15 other events, 42.6 us)
Sparse Core Ops, SparseCore 0:
  9.9 55.1 all-gather.6
  112.4 32.8 all-gather.8
  147.1 56.1 all-gather.10
  204.9 32.9 all-gather.12
  239.6 55.4 all-gather.14

commit v7 on v6

--- a/solution.py
+++ b/solution.py
@@ -132,15 +132,16 @@
     out_ref[...] = (product + bias_ref[...]).astype(out_ref.dtype)
 
 
-def project_tokens(resid, gain, shift, weight, bias, block=512):
-    n_own, width = resid.shape
+def project_tokens(resid, part, gain, shift, weight, bias, block=512):
+    n_own, width = resid.shape[0] // 2, resid.shape[1]
+    first = part * (n_own // block)
     rows = weight.shape[0]
     fixed = lambda shape: pl.BlockSpec(shape, lambda i: (0, 0))
     return pl.pallas_call(
         project_kernel,
         grid=(n_own // block,),
         out_shape=jax.ShapeDtypeStruct((rows, n_own), jnp.bfloat16),
-        in_specs=[pl.BlockSpec((block, width), lambda i: (i, 0)), fixed((1, width)), fixed((1, width)), fixed((rows, width)), fixed((rows, 1))],
+        in_specs=[pl.BlockSpec((block, width), lambda i: (first + i, 0)), fixed((1, width)), fixed((1, width)), fixed((rows, width)), fixed((rows, 1))],
         out_specs=pl.BlockSpec((rows, block), lambda i: (0, i)),
         compiler_params=pltpu.CompilerParams(dimension_semantics=('arbitrary',), vmem_limit_bytes=32 * 1024 * 1024),
         cost_estimate=pl.CostEstimate(flops=2 * n_own * width * rows, bytes_accessed=2 * (n_own * width + rows * width + rows * n_own), transcendentals=n_own),
@@ -159,7 +160,7 @@
     return high + middle + low
 
 
-def finish_kernel(head_dim, up_chunk, mixed_ref, resid_a_ref, resid_b_ref, vec_ref, up_bias_ref, pool_bias_ref, probe_ref, w_out_hbm, w_up_hbm, w_down_hbm, wk_hbm, wv_hbm,
+def finish_kernel(head_dim, up_chunk, mixed_ref, resid_ref, vec_ref, up_bias_ref, pool_bias_ref, probe_ref, w_out_hbm, w_up_hbm, w_down_hbm, wk_hbm, wv_hbm,
                   pooled_ref, total_ref, peak_ref, w_out, w_up, w_down, wk, wv, units, sems):
     step = pl.program_id(0)
     copies = [pltpu.make_async_copy(src, dst, sems.at[index]) for index, (src, dst) in enumerate(
@@ -181,8 +182,7 @@
     b_out, ln2_gain, ln2_bias, b_down, lnf_gain, lnf_bias = (vec_ref[index:index + 1, :] for index in range(6))
     arrive(0)
     attn_local = jnp.dot(mixed_ref[...], w_out[...], preferred_element_type=jnp.float32)
-    resid = jnp.where(step < pl.num_programs(0) // 2, resid_a_ref[...].astype(jnp.float32), resid_b_ref[...].astype(jnp.float32))
-    resid_one = (resid + attn_local + b_out).astype(jnp.bfloat16)
+    resid_one = (resid_ref[...].astype(jnp.float32) + attn_local + b_out).astype(jnp.bfloat16)
     hidden_two = layer_norm(resid_one.astype(jnp.float32), ln2_gain, ln2_bias).astype(jnp.bfloat16)
     arrive(1)
     n_units = w_up.shape[0]
@@ -207,10 +207,9 @@
     peak_ref[...] = peak
 
 
-def finish_tokens(mixed, resid_parts, vectors, up_bias, pool_bias, probe, weights, head_dim, block=512):
-    n_own, width = mixed.shape[0], resid_parts[0].shape[1]
+def finish_tokens(mixed, resid, vectors, up_bias, pool_bias, probe, weights, head_dim, block=512):
+    n_own, width = resid.shape
     n_heads = probe.shape[0]
-    per_part = n_own // 2 // block
     n_units = up_bias.shape[1]
     fixed = lambda shape: pl.BlockSpec(shape, lambda i: (0, 0))
     small = [vectors, up_bias, pool_bias, probe]
@@ -218,7 +217,7 @@
         functools.partial(finish_kernel, head_dim, 512),
         grid=(n_own // block,),
         out_shape=[jax.ShapeDtypeStruct((n_heads, columns), jnp.float32) for columns in (width, 1, 1)],
-        in_specs=[pl.BlockSpec((block, mixed.shape[1]), lambda i: (i, 0)), pl.BlockSpec((block, width), lambda i: (jnp.minimum(i, per_part - 1), 0)), pl.BlockSpec((block, width), lambda i: (jnp.maximum(i - per_part, 0), 0))]
+        in_specs=[pl.BlockSpec((block, mixed.shape[1]), lambda i: (i, 0)), pl.BlockSpec((block, width), lambda i: (i, 0))]
         + [fixed(array.shape) for array in small] + [pl.BlockSpec(memory_space=pl.ANY)] * len(weights),
         out_specs=[fixed((n_heads, columns)) for columns in (width, 1, 1)],
         scratch_shapes=[pltpu.VMEM(weight.shape, jnp.bfloat16) for weight in weights]
@@ -226,7 +225,7 @@
         compiler_params=pltpu.CompilerParams(dimension_semantics=('arbitrary',), vmem_limit_bytes=60 * 1024 * 1024),
         cost_estimate=pl.CostEstimate(flops=2 * n_own * sum(weight.size for weight in weights), bytes_accessed=40 * 1024 * 1024, transcendentals=n_own * n_units),
         name='finish_tokens',
-    )(mixed, *resid_parts, *small, *weights)
+    )(mixed, resid, *small, *weights)
 
 
 def map_tail(pooled_heads, map_wo, map_bo, map_ln_gain, map_ln_bias, map_w_up, map_b_up, map_w_down, map_b_down):
@@ -248,12 +247,7 @@
         hidden_units = w_up.shape[1]
         own = n_images * run
 
-        pieces = tokens.reshape(tp_size, 2, own // tp_size // 2, width)
-
-        def send(piece):
-            return row_major(lax.all_to_all(row_major(pieces[:, piece]), 'tp', split_axis=0, concat_axis=0, tiled=True).reshape(own // 2, width))
-
-        resid_a, resid_b = send(0), send(1)
+        resid = row_major(lax.all_to_all(row_major(tokens.reshape(tp_size, own // tp_size, width)), 'tp', split_axis=0, concat_axis=0, tiled=True).reshape(own, width))
 
         rows_padded = round_up(head_dim, 16)
         shards = []
@@ -278,40 +272,35 @@
         pool_wk, pool_wv = (row_major(map_wkv[:, index].reshape(width, width)) for index in range(2))
         vectors = jnp.stack([b_out, ln2_gain, ln2_bias, b_down, lnf_gain, lnf_bias])
         w_out_p = jnp.pad(w_out, ((0, 0), (0, LANES - head_dim), (0, 0))).reshape(groups * LANES, width)
-        def project(group_rows, part):
+        resid, later, w_out_p, w_up_t, w_down_p, probe_cols, pool_wk, pool_wv, vectors, pool_bias = lax.optimization_barrier(
+            (resid, shards[1:], w_out_p, w_up_t, w_down_p, probe_cols, pool_wk, pool_wv, vectors, map_bkv.reshape(2, width)))
+        gathered += [lax.all_gather(shard, 'tp', axis=0, tiled=True) for shard in later]
+        w_out_all = lax.all_gather(w_out_p, 'tp', axis=0, tiled=True)
+        w_up_all = lax.all_gather(w_up_t, 'tp', axis=0, tiled=True)
+        w_down_all = lax.all_gather(w_down_p, 'tp', axis=0, tiled=True)
+
+        def projections(group_rows, resid):
             bias_row = group_rows.reshape(tp_size, 3 * rows_padded, width)[:, 2 * rows_padded + head_dim, :9 * head_dim]
             bias_row = bias_row.reshape(tp_size, 3, 3, head_dim)
             bias = join_three([bias_row[:, term] for term in range(3)])
             bias = jnp.pad(bias, ((0, 0), (0, 0), (0, rows_padded - head_dim))).reshape(-1, 1)
-            return project_tokens(part, ln1_gain, ln1_bias, group_rows, bias)
-
-        def swap(part):
-            return lax.ppermute(part, 'tp', partner)
-
-        first_a = project(gathered[0], resid_a)
-        far_a = swap(first_a)
-        first_b = project(gathered[0], resid_b)
-        far_a_later, later_parts, later, w_out_p, w_up_t, w_down_p, probe_cols, pool_wk, pool_wv, vectors = lax.optimization_barrier(
-            (far_a, (resid_a, resid_b), shards[1:], w_out_p, w_up_t, w_down_p, probe_cols, pool_wk, pool_wv, vectors))
-        gathered += [lax.all_gather(shard, 'tp', axis=0, tiled=True) for shard in later]
-        w_out_all = lax.all_gather(w_out_p, 'tp', axis=0, tiled=True)
-        w_up_all = lax.all_gather(w_up_t, 'tp', axis=0, tiled=True)
-        w_down_all = lax.all_gather(w_down_p, 'tp', axis=0, tiled=True)
+            first = project_tokens(resid, 0, ln1_gain, ln1_bias, group_rows, bias)
+            second = project_tokens(resid, 1, ln1_gain, ln1_bias, group_rows, bias)
+            return [first, second, lax.ppermute(first, 'tp', partner), lax.ppermute(second, 'tp', partner)]
 
         half = tp_size // 2
-        first_group = [first_a, first_b, far_a, swap(first_b)]
+        first_group = projections(gathered[0], resid)
         mixed = heads_attention(first_group, head_dim, (0, half), 0, groups, None, n_heads)
-        mixed, later_parts, gathered[1] = lax.optimization_barrier((mixed, later_parts, gathered[1]))
-        second_group = [project(gathered[1], part) for part in later_parts]
-        second_group += [swap(part) for part in second_group]
-        mixed = heads_attention([first_a, first_b, far_a_later, first_group[3]], head_dim, (half, half), 0, groups, mixed, n_heads)
+        mixed, resid, gathered[1] = lax.optimization_barrier((mixed, resid, gathered[1]))
+        second_group = projections(gathered[1], resid)
+        mixed = heads_attention(first_group, head_dim, (half, half), 0, groups, mixed, n_heads)
         mixed = heads_attention(second_group, head_dim, (0, tp_size), 1, groups, mixed, n_heads)
 
         bias_rows = w_down_all.reshape(tp_size, padded, width)[:, hidden_units:hidden_units + 2]
         b_up_all = join_three([bias_rows[:, 0, :hidden_units], bias_rows[:, 0, hidden_units:2 * hidden_units], bias_rows[:, 1, :hidden_units]])
         b_up_all = jnp.pad(b_up_all, ((0, 0), (0, padded - hidden_units))).reshape(tp_size * padded)
         every_head, total, peak = finish_tokens(
-            mixed.reshape(own, n_heads * LANES), later_parts, vectors, b_up_all[None], map_bkv.reshape(2, width), probe_cols, (w_out_all, w_up_all, w_down_all, pool_wk, pool_wv), head_dim)
+            mixed.reshape(own, n_heads * LANES), resid, vectors, b_up_all[None], pool_bias, probe_cols, (w_out_all, w_up_all, w_down_all, pool_wk, pool_wv), head_dim)
         pooled = jnp.sum(jnp.where(on_head.T, every_head, 0.0).reshape(n_heads, n_heads, head_dim), axis=1)
         parts = lax.all_gather(jnp.concatenate([pooled, total, peak], axis=-1), 'tp', axis=0, tiled=False)
         parts = parts.reshape(n_images, tp_size // n_images, n_heads, head_dim + 2)

time: 446 us -> 426 us (0.955)
  local copies, waits for them, and re-layouts: 51.7 us -> 45 us
    all_gather x1, waiting for transfers between devices: 45.5 us -> 0.02 us  [local_program(): gathered = [lax.all_gather(shards[0], 'tp', axis=0, tiled=True)]]
    all_to_all x2 -> x1, waiting for transfers between devices: 0.01 us -> 43.1 us  [local_program(): lax.all_to_all(row_major(tokens.reshape(tp_size, own // tp_size, width)),...]
    squeeze x1 -> x0, local copies, waits for them, and re-layouts: 5.06 us -> none  [send(): pieces[:, piece]]
    unnamed x70 -> x80, local copies, waits for them, and re-layouts: 14.9 us -> 13.6 us
  transfers between devices with their start and end apart: 11 -> 10, of which waited for: 2 -> 2; matrix products, arithmetic and copies ran while one was open for 9% -> 8% of each run, Pallas kernels for 42% -> 43%
where the time goes in v7:
time: 426 us; the launch traced here: 422 us
  Pallas kernels  274 us (64%)
  waiting for transfers between devices  52.4 us (12%)
  local copies, waits for them, and re-layouts  45 us (11%)
  between operations  14.2 us (3%)
  matrix products  13 us (3%)
  blocking collectives  11 us (3%)
  other arithmetic  7.18 us (2%)
  starting transfers between devices  5.05 us (1%)
    pallas_call x3, Pallas kernels, heads_attention(): pl.pallas_call(functools.partial(attention_kernel, head_dim, 256), grid=(...  145 us
    pallas_call x1, Pallas kernels, finish_tokens(): pl.pallas_call(functools.partial(finish_kernel, head_dim, 512), grid=(n_o...  93.9 us
    all_to_all x1, waiting for transfers between devices, local_program(): lax.all_to_all(row_major(tokens.reshape(tp_size, own // tp_size, width)),...  43.1 us
    pallas_call x4, Pallas kernels, project_tokens(): pl.pallas_call(project_kernel, grid=(n_own // block,), out_shape=jax.Shap...  35.4 us
    unnamed x80, local copies, waits for them, and re-layouts  13.6 us
    dot_general x1, matrix products, map_tail(): jnp.dot(map_act, map_w_down, preferred_element_type=jnp.float32)  11.4 us
    all_gather x1, blocking collectives, local_program(): lax.all_gather(jnp.concatenate([pooled, total, peak], axis=-1), 'tp', axi...  11 us
    another operation x2, local copies, waits for them, and re-layouts, local_program(): map_wkv[:, index].reshape(width, width)  10.5 us
  transfers between devices with their start and end apart: 10, of which 2 were waited for; matrix products, arithmetic and copies ran while one was open for 8% of the time, Pallas kernels for 43%

profile of v7, /device:TPU:0, one launch (start us, length us, event | category | flops | bytes accessed | tf_op | source)
XLA Modules:
  0.0 422.1 jit_solution(14058978821322431285)
XLA Ops:
  10.5 4.3 %all-to-all-start = ((bf16[8,256,1152]{2,1,0:T(8,128)(2,1)}), bf16[8,256,1152]{2,1,0:T(8,128)(2,1)}, u32[]{:S(2)}, u32[]{:S(2)}) async-start(bf16[8,256,1152]{2,1,0:T(8,128)(2,1)} %bitcast.76), calls=%async_computation | async-start | bytes 9437184 | tf_op jit(solution)/shard_map/all_to_all | solution.py:250
  15.2 5.3 %fusion.72 = (bf16[1152,1,16,72]{0,3,2,1:T(8,128)(2,1)}, bf16[1152,1,16,72]{0,3,2,1:T(8,128)(2,1)}) fusion(bf16[1152,2,16,72]{0,3,2,1:T(8,128)(2,1)} %param.46), kind=kLoop, calls=%fused_computation.123 | loop fusion | bytes 10616832 | tf_op jit(solution)/shard_map/slice | solution.py:272
  20.4 5.2 %copy.58.wk_hbm = bf16[1152,1152]{1,0:T(8,128)(2,1)} copy(bf16[1152,1152]{0,1:T(8,128)(2,1)} %bitcast.74) | data formatting | bytes 5308416 | tf_op jit(solution)/shard_map/reshape;squeeze | solution.py:272
  25.7 5.3 %copy.59.wv_hbm = bf16[1152,1152]{1,0:T(8,128)(2,1)} copy(bf16[1152,1152]{0,1:T(8,128)(2,1)} %bitcast.73) | data formatting | bytes 5308416 | tf_op jit(solution)/shard_map/reshape;squeeze | solution.py:272
  31.1 2.4 pad.48
  41.0 2.6 fusion.7
  44.2 43.1 %all-to-all-done = bf16[8,256,1152]{2,1,0:T(8,128)(2,1)} async-done(((bf16[8,256,1152]{2,1,0:T(8,128)(2,1)}), bf16[8,256,1152]{2,1,0:T(8,128)(2,1)}, u32[]{:S(2)}, u32[]{:S(2)}) %all-to-all-start) | async-done | bytes 4718624 | tf_op jit(solution)/shard_map/all_to_all | solution.py:250
  90.9 2.2 copy-done.8
  93.1 9.1 %project_tokens.5.refs_1_.refs_3_.refs_7_.refs_11_ = bf16[1920,1024]{1,0:T(8,128)(2,1)S(1)} custom-call(bf16[2048,1152]{1,0:T(8,128)(2,1)} %bitcast.1.x_ref.resid_ref, f32[1,1152]{1,0:T(1,128)S(1)} %broadcast_in_dim.27.gain_ref, f32[1,1152]{1,0:T(1,128)S(1)} %broadcast_in_dim.28.shift_ref, bf16[1920,1152]{1,0:T(8,128)(2,1)S(1)} %copy-done.8, ...), custom_call_target="tpu_custom_call" | custom-call | flops 4529848320 | bytes 10715136 | tf_op jit(solution)/shard_map/project_tokens/pallas_call | solution.py:140
  102.3 9.3 %project_tokens.4.refs_0_.refs_2_.refs_6_.refs_10_ = bf16[1920,1024]{1,0:T(8,128)(2,1)S(1)} custom-call(bf16[2048,1152]{1,0:T(8,128)(2,1)} %bitcast.1.x_ref.resid_ref, f32[1,1152]{1,0:T(1,128)S(1)} %broadcast_in_dim.27.gain_ref, f32[1,1152]{1,0:T(1,128)S(1)} %broadcast_in_dim.28.shift_ref, bf16[1920,1152]{1,0:T(8,128)(2,1)S(1)} %bitcast.71, ...), custom_call_target="tpu_custom_call" | custom-call | flops 4529848320 | bytes 10715136 | tf_op jit(solution)/shard_map/project_tokens/pallas_call | solution.py:140
  111.7 7.5 %collective-permute-done.refs_4_.refs_8_.refs_12_ = bf16[1920,1024]{1,0:T(8,128)(2,1)S(1)} collective-permute-done((bf16[1920,1024]{1,0:T(8,128)(2,1)S(1)}, bf16[1920,1024]{1,0:T(8,128)(2,1)S(1)}, u32[]{:S(2)}, u32[]{:S(2)}) %collective-permute-start) | collective-permute-done | bytes 3932192 | tf_op jit(solution)/shard_map/ppermute | solution.py:289
  119.2 37.2 %heads_attention.3.refs_14_ = bf16[2,1024,2048]{2,1,0:T(8,128)(2,1)} custom-call(bf16[1920,1024]{1,0:T(8,128)(2,1)S(1)} %project_tokens.4.refs_0_.refs_2_.refs_6_.refs_10_, bf16[1920,1024]{1,0:T(8,128)(2,1)S(1)} %project_tokens.5.refs_1_.refs_3_.refs_7_.refs_11_, bf16[1920,1024]{1,0:T(8,128)(2,1)S(1)} %project_tokens.4.refs_0_.refs_2_.refs_6_.refs_10_, ...), custom_call_target="tpu_custom_call" | custom-call | flops 17179869184 | bytes 8388608 | tf_op jit(solution)/shard_map/heads_attention/pallas_call | solution.py:108
  156.4 1.8 copy-done.4
  158.2 1.9 copy-done.6
  161.6 2.2 copy-done.9
  163.8 8.5 %project_tokens.7.refs_1_.refs_3_.refs_7_.refs_11_ = bf16[1920,1024]{1,0:T(8,128)(2,1)S(1)} custom-call(bf16[2048,1152]{1,0:T(8,128)(2,1)} %bitcast.1.x_ref.resid_ref, f32[1,1152]{1,0:T(1,128)S(1)} %broadcast_in_dim.27.gain_ref, f32[1,1152]{1,0:T(1,128)S(1)} %broadcast_in_dim.28.shift_ref, bf16[1920,1152]{1,0:T(8,128)(2,1)S(1)} %copy-done.9, ...), custom_call_target="tpu_custom_call" | custom-call | flops 4529848320 | bytes 10715136 | tf_op jit(solution)/shard_map/project_tokens/pallas_call | solution.py:140
  172.4 2.0 copy-done.11
  174.4 2.3 copy-done.10
  176.6 8.5 %project_tokens.6.refs_0_.refs_2_.refs_6_.refs_10_ = bf16[1920,1024]{1,0:T(8,128)(2,1)S(1)} custom-call(bf16[2048,1152]{1,0:T(8,128)(2,1)} %bitcast.1.x_ref.resid_ref, f32[1,1152]{1,0:T(1,128)S(1)} %broadcast_in_dim.27.gain_ref, f32[1,1152]{1,0:T(1,128)S(1)} %broadcast_in_dim.28.shift_ref, bf16[1920,1152]{1,0:T(8,128)(2,1)S(1)} %copy-done.10, ...), custom_call_target="tpu_custom_call" | custom-call | flops 4529848320 | bytes 10715136 | tf_op jit(solution)/shard_map/project_tokens/pallas_call | solution.py:140
  185.7 37.5 %heads_attention.4.refs_14_ = bf16[2,1024,2048]{2,1,0:T(8,128)(2,1)} custom-call(bf16[1920,1024]{1,0:T(8,128)(2,1)S(1)} %copy-done.5, bf16[1920,1024]{1,0:T(8,128)(2,1)S(1)} %copy-done.3, bf16[1920,1024]{1,0:T(8,128)(2,1)S(1)} %copy-done.5, bf16[1920,1024]{1,0:T(8,128)(2,1)S(1)} %copy-done.3, ...), custom_call_target="tpu_custom_call", output_to_operand_aliasing={{}: (14, {})} | custom-call | flops 17179869184 | bytes 8388608 | tf_op jit(solution)/shard_map/heads_attention/pallas_call | solution.py:108
  223.2 70.2 %heads_attention.5 = bf16[2,1024,2048]{2,1,0:T(8,128)(2,1)} custom-call(bf16[1920,1024]{1,0:T(8,128)(2,1)S(1)} %project_tokens.6.refs_0_.refs_2_.refs_6_.refs_10_, bf16[1920,1024]{1,0:T(8,128)(2,1)S(1)} %copy-done.12, bf16[1920,1024]{1,0:T(8,128)(2,1)S(1)} %project_tokens.6.refs_0_.refs_2_.refs_6_.refs_10_, ...), custom_call_target="tpu_custom_call", output_to_operand_aliasing={{}: (14, {})} | custom-call | flops 34359738368 | bytes 8388608 | tf_op jit(solution)/shard_map/heads_attention/pallas_call | solution.py:108
  295.3 93.9 %finish_tokens.1 = (f32[16,1152]{1,0:T(8,128)}, f32[16,1]{1,0:T(8,128)}, f32[16,1]{1,0:T(8,128)}) custom-call(bf16[2048,2048]{1,0:T(8,128)(2,1)} %bitcast.75, bf16[2048,1152]{1,0:T(8,128)(2,1)} %bitcast.1.x_ref.resid_ref, f32[6,1152]{1,0:T(8,128)} %stack.35.vec_ref, f32[1,4352]{1,0:T(1,128)} %broadcast_in_dim_reshape.3.up_bias_ref, ...), custom_call_target="tpu_custom_call" | custom-call | flops 61605937152 | bytes 41943040 | tf_op jit(solution)/shard_map/finish_tokens/pallas_call | solution.py:216
  391.1 11.0 %all-gather = f32[128,74]{1,0:T(8,128)S(1)} all-gather(f32[16,74]{1,0:T(8,128)S(1)} %pad_maximum_fusion), channel_id=2, replica_groups=mesh['dp'=1,'tp'=8] {'tp'}, dimensions={0}, use_global_device_ids=true | all-gather | bytes 42624 | tf_op jit(solution)/shard_map/all_gather | solution.py:305
  403.8 11.4 %fusion.5 = bf16[4,1152]{1,0:T(4,128)(2,1)} fusion(f32[4,1152]{1,0:T(4,128)S(1)} %get-tuple-element.55, bf16[4304,1152]{1,0:T(8,128)(2,1)} %param.54, bf16[1152,4304]{0,1:T(8,128)(2,1)} %param.52, f32[4304]{0:T(1024)S(1)} %copy-done.20, f32[1152]{0:T(1024)S(1)} %copy-done.23, f32[1152]{0:T(1024)S(1)} %copy-done.24, f32[1152]{0:T(1024)S(1)} %copy-done.25, ...), kind=kOutput, calls=%fused_computation.9 | convolution fusion | flops 79540352 | bytes 19891552 | tf_op jit(solution)/shard_map/dot_general | solution.py:235
  (155 shorter events, 23.0 us)
Async XLA Ops:
  6.5 33.4 %copy-start = (bf16[1152,16,72]{0,2,1:T(8,128)(2,1)S(1)}, bf16[1152,16,72]{0,2,1:T(8,128)(2,1)}, u32[]{:S(2)}) copy-start(bf16[1152,16,72]{0,2,1:T(8,128)(2,1)} %param.44) | copy-start | bytes 7962628
  6.5 82.8 %all-gather.7.cloned.1.call-start = ((), (), s32[]{:S(2)}) async-start(), calls=%async_computation.1 | async-start | bytes 4976640 | tf_op jit(solution)/shard_map/all_gather | solution.py:267
  10.5 76.8 %all-to-all-start = ((bf16[8,256,1152]{2,1,0:T(8,128)(2,1)}), bf16[8,256,1152]{2,1,0:T(8,128)(2,1)}, u32[]{:S(2)}, u32[]{:S(2)}) async-start(bf16[8,256,1152]{2,1,0:T(8,128)(2,1)} %bitcast.76), calls=%async_computation | async-start | bytes 9437184 | tf_op jit(solution)/shard_map/all_to_all | solution.py:250
  14.8 145.3 %all-gather.9.cloned.1.call-start = ((), (), s32[]{:S(2)}) async-start(), calls=%async_computation.2 | async-start | bytes 4976640 | tf_op jit(solution)/shard_map/all_gather | solution.py:277
  40.9 46.4 %copy-start.16 = (bf16[240,1152]{1,0:T(8,128)(2,1)}, bf16[240,1152]{1,0:T(8,128)(2,1)S(1)}, u32[]{:S(2)}) copy-start(bf16[240,1152]{1,0:T(8,128)(2,1)S(1)} %constant_dynamic-update-slice_fusion) | copy-start | bytes 1658884
  40.9 48.3 %copy-start.27 = (f32[1152]{0:T(1024)S(1)}, f32[1152]{0:T(1024)}, u32[]{:S(2)}) copy-start(f32[1152]{0:T(1024)} %param.29) | copy-start | bytes 13828
  41.0 48.3 %copy-start.28 = (f32[1152]{0:T(1024)S(1)}, f32[1152]{0:T(1024)}, u32[]{:S(2)}) copy-start(f32[1152]{0:T(1024)} %param.30) | copy-start | bytes 13828
  87.4 206.1 %all-gather.11.cloned.1.call-start = ((), (), s32[]{:S(2)}) async-start(), calls=%async_computation.3 | async-start | bytes 11280384 | tf_op jit(solution)/shard_map/all_gather | solution.py:280
  88.1 207.2 %all-gather.13.cloned.1.call-start = ((), (), s32[]{:S(2)}) async-start(), calls=%async_computation.4 | async-start | bytes 5308416 | tf_op jit(solution)/shard_map/all_gather | solution.py:278
  88.7 206.6 %all-gather.15.cloned.1.call-start = ((), (), s32[]{:S(2)}) async-start(), calls=%async_computation.5 | async-start | bytes 11280384 | tf_op jit(solution)/shard_map/all_gather | solution.py:279
  90.4 11.9 %slice-start = ((s8[4423680]{0:T(1024)(128)(4,1)}), s8[229376]{0:T(1024)(128)(4,1)S(1)}, s32[]{:S(2)}) async-start(s8[4423680]{0:T(1024)(128)(4,1)} %bitcast.70), calls=%async_computation.6 | async-start | bytes 458752
  102.3 16.9 %copy-start.2 = (bf16[1920,1024]{1,0:T(8,128)(2,1)}, bf16[1920,1024]{1,0:T(8,128)(2,1)S(1)}, u32[]{:S(2)}) copy-start(bf16[1920,1024]{1,0:T(8,128)(2,1)S(1)} %project_tokens.5.refs_1_.refs_3_.refs_7_.refs_11_) | copy-start | bytes 11796484
  102.3 9.4 %collective-permute-start.1 = (bf16[1920,1024]{1,0:T(8,128)(2,1)S(1)}, bf16[1920,1024]{1,0:T(8,128)(2,1)S(1)}, u32[]{:S(2)}, u32[]{:S(2)}) collective-permute-start(bf16[1920,1024]{1,0:T(8,128)(2,1)S(1)} %project_tokens.5.refs_1_.refs_3_.refs_7_.refs_11_), channel_id=1, source_target_pairs={{0,1},{1,0},{2,3},{3,2},{4,5},{5,4},{6,7},{7,6}} | collective-permute-start | bytes 11796488 | tf_op jit(solution)/shard_map/ppermute | solution.py:289
  111.6 7.6 %collective-permute-start = (bf16[1920,1024]{1,0:T(8,128)(2,1)S(1)}, bf16[1920,1024]{1,0:T(8,128)(2,1)S(1)}, u32[]{:S(2)}, u32[]{:S(2)}) collective-permute-start(bf16[1920,1024]{1,0:T(8,128)(2,1)S(1)} %project_tokens.4.refs_0_.refs_2_.refs_6_.refs_10_), channel_id=1, source_target_pairs={{0,1},{1,0},{2,3},{3,2},{4,5},{5,4},{6,7},{7,6}} | collective-permute-start | bytes 11796488 | tf_op jit(solution)/shard_map/ppermute | solution.py:289
  185.1 38.0 %copy-start.12 = (bf16[1920,1024]{1,0:T(8,128)(2,1)S(1)}, bf16[1920,1024]{1,0:T(8,128)(2,1)}, u32[]{:S(2)}) copy-start(bf16[1920,1024]{1,0:T(8,128)(2,1)} %copy-done.11) | copy-start | bytes 11796484
  185.2 38.0 %collective-permute-start.3 = (bf16[1920,1024]{1,0:T(8,128)(2,1)}, bf16[1920,1024]{1,0:T(8,128)(2,1)}, u32[]{:S(2)}, u32[]{:S(2)}) collective-permute-start(bf16[1920,1024]{1,0:T(8,128)(2,1)} %copy-done.11), channel_id=1, source_target_pairs={{0,1},{1,0},{2,3},{3,2},{4,5},{5,4},{6,7},{7,6}} | collective-permute-start | bytes 11796488 | tf_op jit(solution)/shard_map/ppermute | solution.py:289
  185.3 37.9 %collective-permute-start.2 = (bf16[1920,1024]{1,0:T(8,128)(2,1)S(1)}, bf16[1920,1024]{1,0:T(8,128)(2,1)}, u32[]{:S(2)}, u32[]{:S(2)}) collective-permute-start(bf16[1920,1024]{1,0:T(8,128)(2,1)S(1)} %project_tokens.6.refs_0_.refs_2_.refs_6_.refs_10_), channel_id=1, source_target_pairs={{0,1},{1,0},{2,3},{3,2},{4,5},{5,4},{6,7},{7,6}} | collective-permute-start | bytes 11796488 | tf_op jit(solution)/shard_map/ppermute | solution.py:289
  295.3 94.0 %copy-start.19 = (s32[1152]{0:T(1024)S(1)}, s32[1152]{0:T(1024)}, u32[]{:S(2)}) copy-start(s32[1152]{0:T(1024)} %copy-done.18) | copy-start | bytes 13828
  295.3 107.4 %copy-start.14 = (bf16[16,72,1152]{2,1,0:T(8,128)(2,1)S(1)}, bf16[16,72,1152]{2,1,0:T(8,128)(2,1)}, u32[]{:S(2)}) copy-start(bf16[16,72,1152]{2,1,0:T(8,128)(2,1)} %param.48) | copy-start | bytes 7962628
  295.3 107.4 %copy-start.22 = (f32[1152]{0:T(1024)S(1)}, f32[1152]{0:T(1024)}, u32[]{:S(2)}) copy-start(f32[1152]{0:T(1024)} %param.49) | copy-start | bytes 13828
  389.2 14.5 %copy-start.20 = (f32[4304]{0:T(1024)S(1)}, f32[4304]{0:T(1024)}, u32[]{:S(2)}) copy-start(f32[4304]{0:T(1024)} %param.53) | copy-start | bytes 51652
  389.2 14.5 %copy-start.23 = (f32[1152]{0:T(1024)S(1)}, f32[1152]{0:T(1024)}, u32[]{:S(2)}) copy-start(f32[1152]{0:T(1024)} %param.55) | copy-start | bytes 13828
  389.2 14.5 %copy-start.24 = (f32[1152]{0:T(1024)S(1)}, f32[1152]{0:T(1024)}, u32[]{:S(2)}) copy-start(f32[1152]{0:T(1024)} %param.51) | copy-start | bytes 13828
  389.2 14.5 %copy-start.25 = (f32[1152]{0:T(1024)S(1)}, f32[1152]{0:T(1024)}, u32[]{:S(2)}) copy-start(f32[1152]{0:T(1024)} %param.50) | copy-start | bytes 13828
  (19 other events, 103.0 us)
Sparse Core Ops, SparseCore 0:
  10.6 64.0 all-gather.6
  87.5 31.8 all-gather.8
  121.2 55.3 all-gather.10
  178.2 32.9 all-gather.12
  212.8 55.4 all-gather.14

commit v8 on v7

--- a/solution.py
+++ b/solution.py
@@ -69,7 +69,6 @@
     @pl.when(step == 0)
     def _():
         apart[0] = 0
-        scores_b[...] = jnp.zeros_like(scores_b)
         max_b[...] = jnp.zeros_like(max_b)
         first_out[...] = jnp.zeros_like(first_out)
 
@@ -120,7 +119,7 @@
             pltpu.SMEM((1,), jnp.int32),
         ],
         input_output_aliases=aliases,
-        compiler_params=pltpu.CompilerParams(dimension_semantics=('arbitrary',), vmem_limit_bytes=40 * 1024 * 1024),
+        compiler_params=pltpu.CompilerParams(dimension_semantics=('arbitrary',), vmem_limit_bytes=60 * 1024 * 1024),
         cost_estimate=pl.CostEstimate(flops=4 * scored * LANES, bytes_accessed=8 * 1024 * 1024, transcendentals=scored),
         name='heads_attention',
     )(*operands)
@@ -143,7 +142,7 @@
         out_shape=jax.ShapeDtypeStruct((rows, n_own), jnp.bfloat16),
         in_specs=[pl.BlockSpec((block, width), lambda i: (first + i, 0)), fixed((1, width)), fixed((1, width)), fixed((rows, width)), fixed((rows, 1))],
         out_specs=pl.BlockSpec((rows, block), lambda i: (0, i)),
-        compiler_params=pltpu.CompilerParams(dimension_semantics=('arbitrary',), vmem_limit_bytes=32 * 1024 * 1024),
+        compiler_params=pltpu.CompilerParams(dimension_semantics=('arbitrary',), vmem_limit_bytes=60 * 1024 * 1024),
         cost_estimate=pl.CostEstimate(flops=2 * n_own * width * rows, bytes_accessed=2 * (n_own * width + rows * width + rows * n_own), transcendentals=n_own),
         name='project_tokens',
     )(resid, gain[None], shift[None], weight, bias)

time: 426 us -> 425 us (level)
  local copies, waits for them, and re-layouts: 45 us -> 35.9 us
  Pallas kernels: 274 us -> 283 us
    unnamed x80 -> x52, local copies, waits for them, and re-layouts: 13.6 us -> 1.09 us
    pallas_call x4, Pallas kernels: 35.4 us -> 44.5 us  [project_tokens(): pl.pallas_call(project_kernel, grid=(n_own // block,), out_shape=jax.Shap...]
  transfers between devices with their start and end apart: 10 -> 10, of which waited for: 2 -> 2; matrix products, arithmetic and copies ran while one was open for 8% -> 9% of each run, Pallas kernels for 43% -> 45%
where the time goes in v8:
time: 425 us; the launch traced here: 421 us
  Pallas kernels  283 us (67%)
  waiting for transfers between devices  51.1 us (12%)
  local copies, waits for them, and re-layouts  35.9 us (8%)
  between operations  14.1 us (3%)
  matrix products  13 us (3%)
  blocking collectives  11 us (3%)
  other arithmetic  7.22 us (2%)
  starting transfers between devices  5.99 us (1%)
    pallas_call x3, Pallas kernels, heads_attention(): pl.pallas_call(functools.partial(attention_kernel, head_dim, 256), grid=(...  144 us
    pallas_call x1, Pallas kernels, finish_tokens(): pl.pallas_call(functools.partial(finish_kernel, head_dim, 512), grid=(n_o...  93.9 us
    pallas_call x4, Pallas kernels, project_tokens(): pl.pallas_call(project_kernel, grid=(n_own // block,), out_shape=jax.Shap...  44.5 us
    all_to_all x1, waiting for transfers between devices, local_program(): lax.all_to_all(row_major(tokens.reshape(tp_size, own // tp_size, width)),...  43 us
    dot_general x1, matrix products, map_tail(): jnp.dot(map_act, map_w_down, preferred_element_type=jnp.float32)  11.4 us
    all_gather x1, blocking collectives, local_program(): lax.all_gather(jnp.concatenate([pooled, total, peak], axis=-1), 'tp', axi...  11 us
    another operation x2, local copies, waits for them, and re-layouts, local_program(): map_wkv[:, index].reshape(width, width)  10.6 us
  transfers between devices with their start and end apart: 10, of which 2 were waited for; matrix products, arithmetic and copies ran while one was open for 9% of the time, Pallas kernels for 45%

profile of v8, /device:TPU:0, one launch (start us, length us, event | category | flops | bytes accessed | tf_op | source)
XLA Modules:
  0.0 420.9 jit_solution(4730987506107047081)
XLA Ops:
  6.5 1.4 slice_bitcast_fusion
  10.5 4.3 %all-to-all-start = ((bf16[8,256,1152]{2,1,0:T(8,128)(2,1)}), bf16[8,256,1152]{2,1,0:T(8,128)(2,1)}, u32[]{:S(2)}, u32[]{:S(2)}) async-start(bf16[8,256,1152]{2,1,0:T(8,128)(2,1)} %bitcast.72), calls=%async_computation | async-start | bytes 9437184 | tf_op jit(solution)/shard_map/all_to_all | solution.py:249
  15.2 5.3 %fusion.72 = (bf16[1152,1,16,72]{0,3,2,1:T(8,128)(2,1)}, bf16[1152,1,16,72]{0,3,2,1:T(8,128)(2,1)}) fusion(bf16[1152,2,16,72]{0,3,2,1:T(8,128)(2,1)} %param.46), kind=kLoop, calls=%fused_computation.123 | loop fusion | bytes 10616832 | tf_op jit(solution)/shard_map/slice | solution.py:271
  20.5 5.2 %copy.58.wk_hbm = bf16[1152,1152]{1,0:T(8,128)(2,1)} copy(bf16[1152,1152]{0,1:T(8,128)(2,1)} %bitcast.70) | data formatting | bytes 5308416 | tf_op jit(solution)/shard_map/reshape;squeeze | solution.py:271
  25.7 5.3 %copy.59.wv_hbm = bf16[1152,1152]{1,0:T(8,128)(2,1)} copy(bf16[1152,1152]{0,1:T(8,128)(2,1)} %bitcast.69) | data formatting | bytes 5308416 | tf_op jit(solution)/shard_map/reshape;squeeze | solution.py:271
  31.1 2.5 pad.48
  41.1 2.7 fusion.7
  44.4 43.0 %all-to-all-done = bf16[8,256,1152]{2,1,0:T(8,128)(2,1)} async-done(((bf16[8,256,1152]{2,1,0:T(8,128)(2,1)}), bf16[8,256,1152]{2,1,0:T(8,128)(2,1)}, u32[]{:S(2)}, u32[]{:S(2)}) %all-to-all-start) | async-done | bytes 4718624 | tf_op jit(solution)/shard_map/all_to_all | solution.py:249
  90.5 0.9 slice.114
  91.6 1.5 reshape.123.bias_ref
  93.1 11.1 %project_tokens.5.refs_1_.refs_3_.refs_7_.refs_11_ = bf16[1920,1024]{1,0:T(8,128)(2,1)} custom-call(bf16[2048,1152]{1,0:T(8,128)(2,1)} %bitcast.1.x_ref.resid_ref, f32[1,1152]{1,0:T(1,128)} %broadcast_in_dim.27.gain_ref, f32[1,1152]{1,0:T(1,128)} %broadcast_in_dim.28.shift_ref, bf16[1920,1152]{1,0:T(8,128)(2,1)} %all-gather.7.cloned.1.call-done.weight_ref, ...), custom_call_target="tpu_custom_call" | custom-call | flops 4529848320 | bytes 10715136 | tf_op jit(solution)/shard_map/project_tokens/pallas_call | solution.py:139
  104.1 11.1 %project_tokens.4.refs_0_.refs_2_.refs_6_.refs_10_ = bf16[1920,1024]{1,0:T(8,128)(2,1)} custom-call(bf16[2048,1152]{1,0:T(8,128)(2,1)} %bitcast.1.x_ref.resid_ref, f32[1,1152]{1,0:T(1,128)} %broadcast_in_dim.27.gain_ref, f32[1,1152]{1,0:T(1,128)} %broadcast_in_dim.28.shift_ref, bf16[1920,1152]{1,0:T(8,128)(2,1)} %all-gather.7.cloned.1.call-done.weight_ref, ...), custom_call_target="tpu_custom_call" | custom-call | flops 4529848320 | bytes 10715136 | tf_op jit(solution)/shard_map/project_tokens/pallas_call | solution.py:139
  115.7 6.8 %collective-permute-done.refs_4_.refs_8_.refs_12_ = bf16[1920,1024]{1,0:T(8,128)(2,1)} collective-permute-done((bf16[1920,1024]{1,0:T(8,128)(2,1)}, bf16[1920,1024]{1,0:T(8,128)(2,1)}, u32[]{:S(2)}, u32[]{:S(2)}) %collective-permute-start) | collective-permute-done | bytes 3932192 | tf_op jit(solution)/shard_map/ppermute | solution.py:288
  122.6 37.2 %heads_attention.3.refs_14_ = bf16[2,1024,2048]{2,1,0:T(8,128)(2,1)} custom-call(bf16[1920,1024]{1,0:T(8,128)(2,1)} %project_tokens.4.refs_0_.refs_2_.refs_6_.refs_10_, bf16[1920,1024]{1,0:T(8,128)(2,1)} %project_tokens.5.refs_1_.refs_3_.refs_7_.refs_11_, bf16[1920,1024]{1,0:T(8,128)(2,1)} %project_tokens.4.refs_0_.refs_2_.refs_6_.refs_10_, ...), custom_call_target="tpu_custom_call" | custom-call | flops 17179869184 | bytes 8388608 | tf_op jit(solution)/shard_map/heads_attention/pallas_call | solution.py:107
  159.8 0.9 slice.118
  160.9 1.4 reshape.124.bias_ref
  162.3 11.2 %project_tokens.7.refs_1_.refs_3_.refs_7_.refs_11_ = bf16[1920,1024]{1,0:T(8,128)(2,1)} custom-call(bf16[2048,1152]{1,0:T(8,128)(2,1)} %bitcast.1.x_ref.resid_ref, f32[1,1152]{1,0:T(1,128)} %broadcast_in_dim.27.gain_ref, f32[1,1152]{1,0:T(1,128)} %broadcast_in_dim.28.shift_ref, bf16[1920,1152]{1,0:T(8,128)(2,1)} %all-gather.9.cloned.1.call-done.weight_ref, ...), custom_call_target="tpu_custom_call" | custom-call | flops 4529848320 | bytes 10715136 | tf_op jit(solution)/shard_map/project_tokens/pallas_call | solution.py:139
  173.5 11.1 %project_tokens.6.refs_0_.refs_2_.refs_6_.refs_10_ = bf16[1920,1024]{1,0:T(8,128)(2,1)} custom-call(bf16[2048,1152]{1,0:T(8,128)(2,1)} %bitcast.1.x_ref.resid_ref, f32[1,1152]{1,0:T(1,128)} %broadcast_in_dim.27.gain_ref, f32[1,1152]{1,0:T(1,128)} %broadcast_in_dim.28.shift_ref, bf16[1920,1152]{1,0:T(8,128)(2,1)} %all-gather.9.cloned.1.call-done.weight_ref, ...), custom_call_target="tpu_custom_call" | custom-call | flops 4529848320 | bytes 10715136 | tf_op jit(solution)/shard_map/project_tokens/pallas_call | solution.py:139
  185.1 37.2 %heads_attention.4.refs_14_ = bf16[2,1024,2048]{2,1,0:T(8,128)(2,1)} custom-call(bf16[1920,1024]{1,0:T(8,128)(2,1)} %project_tokens.4.refs_0_.refs_2_.refs_6_.refs_10_, bf16[1920,1024]{1,0:T(8,128)(2,1)} %project_tokens.5.refs_1_.refs_3_.refs_7_.refs_11_, ...), custom_call_target="tpu_custom_call", output_to_operand_aliasing={{}: (14, {})} | custom-call | flops 17179869184 | bytes 8388608 | tf_op jit(solution)/shard_map/heads_attention/pallas_call | solution.py:107
  222.3 69.9 %heads_attention.5 = bf16[2,1024,2048]{2,1,0:T(8,128)(2,1)} custom-call(bf16[1920,1024]{1,0:T(8,128)(2,1)} %project_tokens.6.refs_0_.refs_2_.refs_6_.refs_10_, bf16[1920,1024]{1,0:T(8,128)(2,1)} %project_tokens.7.refs_1_.refs_3_.refs_7_.refs_11_, bf16[1920,1024]{1,0:T(8,128)(2,1)} %project_tokens.6.refs_0_.refs_2_.refs_6_.refs_10_, ...), custom_call_target="tpu_custom_call", output_to_operand_aliasing={{}: (14, {})} | custom-call | flops 34359738368 | bytes 8388608 | tf_op jit(solution)/shard_map/heads_attention/pallas_call | solution.py:107
  292.2 1.1 fusion.32
  294.1 93.9 %finish_tokens.1 = (f32[16,1152]{1,0:T(8,128)}, f32[16,1]{1,0:T(8,128)}, f32[16,1]{1,0:T(8,128)}) custom-call(bf16[2048,2048]{1,0:T(8,128)(2,1)} %bitcast.71, bf16[2048,1152]{1,0:T(8,128)(2,1)} %bitcast.1.x_ref.resid_ref, f32[6,1152]{1,0:T(8,128)} %stack.35.vec_ref, f32[1,4352]{1,0:T(1,128)} %broadcast_in_dim_reshape.3.up_bias_ref, ...), custom_call_target="tpu_custom_call" | custom-call | flops 61605937152 | bytes 41943040 | tf_op jit(solution)/shard_map/finish_tokens/pallas_call | solution.py:215
  389.9 11.0 %all-gather = f32[128,74]{1,0:T(8,128)S(1)} all-gather(f32[16,74]{1,0:T(8,128)S(1)} %pad_maximum_fusion), channel_id=2, replica_groups=mesh['dp'=1,'tp'=8] {'tp'}, dimensions={0}, use_global_device_ids=true | all-gather | bytes 42624 | tf_op jit(solution)/shard_map/all_gather | solution.py:304
  402.6 11.4 %fusion.5 = bf16[4,1152]{1,0:T(4,128)(2,1)} fusion(f32[4,1152]{1,0:T(4,128)S(1)} %get-tuple-element.55, bf16[4304,1152]{1,0:T(8,128)(2,1)} %param.54, bf16[1152,4304]{0,1:T(8,128)(2,1)} %param.52, f32[4304]{0:T(1024)S(1)} %copy-done.8, f32[1152]{0:T(1024)S(1)} %copy-done.11, f32[1152]{0:T(1024)S(1)} %copy-done.12, f32[1152]{0:T(1024)S(1)} %copy-done.13, ...), kind=kOutput, calls=%fused_computation.9 | convolution fusion | flops 79540352 | bytes 19891552 | tf_op jit(solution)/shard_map/dot_general | solution.py:234
  (126 shorter events, 19.4 us)
Async XLA Ops:
  6.5 33.6 %copy-start = (bf16[1152,16,72]{0,2,1:T(8,128)(2,1)S(1)}, bf16[1152,16,72]{0,2,1:T(8,128)(2,1)}, u32[]{:S(2)}) copy-start(bf16[1152,16,72]{0,2,1:T(8,128)(2,1)} %param.44) | copy-start | bytes 7962628
  6.5 84.0 %all-gather.7.cloned.1.call-start = ((), (), s32[]{:S(2)}) async-start(), calls=%async_computation.1 | async-start | bytes 4976640 | tf_op jit(solution)/shard_map/all_gather | solution.py:266
  10.5 76.8 %all-to-all-start = ((bf16[8,256,1152]{2,1,0:T(8,128)(2,1)}), bf16[8,256,1152]{2,1,0:T(8,128)(2,1)}, u32[]{:S(2)}, u32[]{:S(2)}) async-start(bf16[8,256,1152]{2,1,0:T(8,128)(2,1)} %bitcast.72), calls=%async_computation | async-start | bytes 9437184 | tf_op jit(solution)/shard_map/all_to_all | solution.py:249
  14.8 145.0 %all-gather.9.cloned.1.call-start = ((), (), s32[]{:S(2)}) async-start(), calls=%async_computation.2 | async-start | bytes 4976640 | tf_op jit(solution)/shard_map/all_gather | solution.py:276
  25.7 8.0 %copy-start.5 = (bf16[2,72,1152]{2,1,0:T(8,128)(2,1)S(1)}, bf16[2,72,1152]{2,1,0:T(8,128)(2,1)}, u32[]{:S(2)}) copy-start(bf16[2,72,1152]{2,1,0:T(8,128)(2,1)} %param.33) | copy-start | bytes 995332
  31.0 7.7 %copy-start.9 = (f32[2,16,72]{2,1,0:T(8,128)S(1)}, f32[2,16,72]{2,1,0:T(8,128)}, u32[]{:S(2)}) copy-start(f32[2,16,72]{2,1,0:T(8,128)} %param.47) | copy-start | bytes 27652
  41.1 46.3 %copy-start.4 = (bf16[240,1152]{1,0:T(8,128)(2,1)}, bf16[240,1152]{1,0:T(8,128)(2,1)S(1)}, u32[]{:S(2)}) copy-start(bf16[240,1152]{1,0:T(8,128)(2,1)S(1)} %constant_dynamic-update-slice_fusion) | copy-start | bytes 1658884
  41.1 48.2 %copy-start.15 = (f32[1152]{0:T(1024)S(1)}, f32[1152]{0:T(1024)}, u32[]{:S(2)}) copy-start(f32[1152]{0:T(1024)} %param.29) | copy-start | bytes 13828
  41.1 48.8 %copy-start.16 = (f32[1152]{0:T(1024)S(1)}, f32[1152]{0:T(1024)}, u32[]{:S(2)}) copy-start(f32[1152]{0:T(1024)} %param.30) | copy-start | bytes 13828
  87.4 204.8 %all-gather.11.cloned.1.call-start = ((), (), s32[]{:S(2)}) async-start(), calls=%async_computation.3 | async-start | bytes 11280384 | tf_op jit(solution)/shard_map/all_gather | solution.py:279
  88.1 206.0 %all-gather.13.cloned.1.call-start = ((), (), s32[]{:S(2)}) async-start(), calls=%async_computation.4 | async-start | bytes 5308416 | tf_op jit(solution)/shard_map/all_gather | solution.py:277
  88.7 205.4 %all-gather.15.cloned.1.call-start = ((), (), s32[]{:S(2)}) async-start(), calls=%async_computation.5 | async-start | bytes 11280384 | tf_op jit(solution)/shard_map/all_gather | solution.py:278
  104.1 11.6 %collective-permute-start.1 = (bf16[1920,1024]{1,0:T(8,128)(2,1)}, bf16[1920,1024]{1,0:T(8,128)(2,1)}, u32[]{:S(2)}, u32[]{:S(2)}) collective-permute-start(bf16[1920,1024]{1,0:T(8,128)(2,1)} %project_tokens.5.refs_1_.refs_3_.refs_7_.refs_11_), channel_id=1, source_target_pairs={{0,1},{1,0},{2,3},{3,2},{4,5},{5,4},{6,7},{7,6}} | collective-permute-start | bytes 11796488 | tf_op jit(solution)/shard_map/ppermute | solution.py:288
  115.2 7.3 %collective-permute-start = (bf16[1920,1024]{1,0:T(8,128)(2,1)}, bf16[1920,1024]{1,0:T(8,128)(2,1)}, u32[]{:S(2)}, u32[]{:S(2)}) collective-permute-start(bf16[1920,1024]{1,0:T(8,128)(2,1)} %project_tokens.4.refs_0_.refs_2_.refs_6_.refs_10_), channel_id=1, source_target_pairs={{0,1},{1,0},{2,3},{3,2},{4,5},{5,4},{6,7},{7,6}} | collective-permute-start | bytes 11796488 | tf_op jit(solution)/shard_map/ppermute | solution.py:288
  184.6 37.7 %collective-permute-start.3 = (bf16[1920,1024]{1,0:T(8,128)(2,1)}, bf16[1920,1024]{1,0:T(8,128)(2,1)}, u32[]{:S(2)}, u32[]{:S(2)}) collective-permute-start(bf16[1920,1024]{1,0:T(8,128)(2,1)} %project_tokens.7.refs_1_.refs_3_.refs_7_.refs_11_), channel_id=1, source_target_pairs={{0,1},{1,0},{2,3},{3,2},{4,5},{5,4},{6,7},{7,6}} | collective-permute-start | bytes 11796488 | tf_op jit(solution)/shard_map/ppermute | solution.py:288
  184.9 37.4 %collective-permute-start.2 = (bf16[1920,1024]{1,0:T(8,128)(2,1)}, bf16[1920,1024]{1,0:T(8,128)(2,1)}, u32[]{:S(2)}, u32[]{:S(2)}) collective-permute-start(bf16[1920,1024]{1,0:T(8,128)(2,1)} %project_tokens.6.refs_0_.refs_2_.refs_6_.refs_10_), channel_id=1, source_target_pairs={{0,1},{1,0},{2,3},{3,2},{4,5},{5,4},{6,7},{7,6}} | collective-permute-start | bytes 11796488 | tf_op jit(solution)/shard_map/ppermute | solution.py:288
  294.1 94.0 %copy-start.7 = (s32[1152]{0:T(1024)S(1)}, s32[1152]{0:T(1024)}, u32[]{:S(2)}) copy-start(s32[1152]{0:T(1024)} %copy-done.6) | copy-start | bytes 13828
  294.1 107.4 %copy-start.2 = (bf16[16,72,1152]{2,1,0:T(8,128)(2,1)S(1)}, bf16[16,72,1152]{2,1,0:T(8,128)(2,1)}, u32[]{:S(2)}) copy-start(bf16[16,72,1152]{2,1,0:T(8,128)(2,1)} %param.48) | copy-start | bytes 7962628
  294.1 107.4 %copy-start.10 = (f32[1152]{0:T(1024)S(1)}, f32[1152]{0:T(1024)}, u32[]{:S(2)}) copy-start(f32[1152]{0:T(1024)} %param.49) | copy-start | bytes 13828
  388.0 14.5 %copy-start.8 = (f32[4304]{0:T(1024)S(1)}, f32[4304]{0:T(1024)}, u32[]{:S(2)}) copy-start(f32[4304]{0:T(1024)} %param.53) | copy-start | bytes 51652
  388.0 14.5 %copy-start.11 = (f32[1152]{0:T(1024)S(1)}, f32[1152]{0:T(1024)}, u32[]{:S(2)}) copy-start(f32[1152]{0:T(1024)} %param.55) | copy-start | bytes 13828
  388.0 14.5 %copy-start.12 = (f32[1152]{0:T(1024)S(1)}, f32[1152]{0:T(1024)}, u32[]{:S(2)}) copy-start(f32[1152]{0:T(1024)} %param.51) | copy-start | bytes 13828
  388.0 14.5 %copy-start.13 = (f32[1152]{0:T(1024)S(1)}, f32[1152]{0:T(1024)}, u32[]{:S(2)}) copy-start(f32[1152]{0:T(1024)} %param.50) | copy-start | bytes 13828
  402.6 11.4 %copy-start.1 = (bf16[1152,16,72]{0,2,1:T(8,128)(2,1)S(1)}, bf16[1152,16,72]{0,2,1:T(8,128)(2,1)}, u32[]{:S(2)}) copy-start(bf16[1152,16,72]{0,2,1:T(8,128)(2,1)} %param.44) | copy-start | bytes 7962628
  (5 other events, 19.7 us)
Sparse Core Ops, SparseCore 0:
  10.6 64.0 all-gather.6
  87.5 31.9 all-gather.8
  121.3 55.4 all-gather.10
  178.5 32.9 all-gather.12
  213.1 55.4 all-gather.14

commit v9 on v8

--- a/solution.py
+++ b/solution.py
@@ -125,23 +125,28 @@
     )(*operands)
 
 
-def project_kernel(x_ref, gain_ref, shift_ref, weight_ref, bias_ref, out_ref):
+def project_kernel(per_out, x_ref, gain_ref, shift_ref, weight_ref, bias_ref, *out_refs):
     hidden = layer_norm(x_ref[...].astype(jnp.float32), gain_ref[...], shift_ref[...]).astype(jnp.bfloat16)
     product = lax.dot_general(weight_ref[...], hidden, (((1,), (1,)), ((), ())), preferred_element_type=jnp.float32)
-    out_ref[...] = (product + bias_ref[...]).astype(out_ref.dtype)
-
-
-def project_tokens(resid, part, gain, shift, weight, bias, block=512):
+    for index, out_ref in enumerate(out_refs):
+        @pl.when(pl.program_id(0) // per_out == index)
+        def _():
+            out_ref[...] = (product + bias_ref[...]).astype(out_ref.dtype)
+
+
+def project_tokens(resid, parts, gain, shift, weight, bias, block=512):
     n_own, width = resid.shape[0] // 2, resid.shape[1]
-    first = part * (n_own // block)
+    per_out = n_own // block
+    first = parts[0] * per_out
+    out_spec = lambda index: pl.BlockSpec((rows, block), lambda i: (0, jnp.clip(i - index * per_out, 0, per_out - 1)))
     rows = weight.shape[0]
     fixed = lambda shape: pl.BlockSpec(shape, lambda i: (0, 0))
     return pl.pallas_call(
-        project_kernel,
-        grid=(n_own // block,),
-        out_shape=jax.ShapeDtypeStruct((rows, n_own), jnp.bfloat16),
+        functools.partial(project_kernel, per_out),
+        grid=(len(parts) * per_out,),
+        out_shape=[jax.ShapeDtypeStruct((rows, n_own), jnp.bfloat16)] * len(parts),
         in_specs=[pl.BlockSpec((block, width), lambda i: (first + i, 0)), fixed((1, width)), fixed((1, width)), fixed((rows, width)), fixed((rows, 1))],
-        out_specs=pl.BlockSpec((rows, block), lambda i: (0, i)),
+        out_specs=[out_spec(index) for index in range(len(parts))],
         compiler_params=pltpu.CompilerParams(dimension_semantics=('arbitrary',), vmem_limit_bytes=60 * 1024 * 1024),
         cost_estimate=pl.CostEstimate(flops=2 * n_own * width * rows, bytes_accessed=2 * (n_own * width + rows * width + rows * n_own), transcendentals=n_own),
         name='project_tokens',
@@ -278,20 +283,19 @@
         w_up_all = lax.all_gather(w_up_t, 'tp', axis=0, tiled=True)
         w_down_all = lax.all_gather(w_down_p, 'tp', axis=0, tiled=True)
 
-        def projections(group_rows, resid):
+        def projections(group_rows, resid, calls):
             bias_row = group_rows.reshape(tp_size, 3 * rows_padded, width)[:, 2 * rows_padded + head_dim, :9 * head_dim]
             bias_row = bias_row.reshape(tp_size, 3, 3, head_dim)
             bias = join_three([bias_row[:, term] for term in range(3)])
             bias = jnp.pad(bias, ((0, 0), (0, 0), (0, rows_padded - head_dim))).reshape(-1, 1)
-            first = project_tokens(resid, 0, ln1_gain, ln1_bias, group_rows, bias)
-            second = project_tokens(resid, 1, ln1_gain, ln1_bias, group_rows, bias)
+            first, second = (part for parts in calls for part in project_tokens(resid, parts, ln1_gain, ln1_bias, group_rows, bias))
             return [first, second, lax.ppermute(first, 'tp', partner), lax.ppermute(second, 'tp', partner)]
 
         half = tp_size // 2
-        first_group = projections(gathered[0], resid)
+        first_group = projections(gathered[0], resid, [(0,), (1,)])
         mixed = heads_attention(first_group, head_dim, (0, half), 0, groups, None, n_heads)
         mixed, resid, gathered[1] = lax.optimization_barrier((mixed, resid, gathered[1]))
-        second_group = projections(gathered[1], resid)
+        second_group = projections(gathered[1], resid, [(0, 1)])
         mixed = heads_attention(first_group, head_dim, (half, half), 0, groups, mixed, n_heads)
         mixed = heads_attention(second_group, head_dim, (0, tp_size), 1, groups, mixed, n_heads)
 

time: 425 us -> 425 us (level)
    pallas_call x4 -> x3, Pallas kernels: 44.5 us -> 44.6 us  [project_tokens(): pl.pallas_call(functools.partial(project_kernel, per_out), grid=(len(part...]
where the time goes in v9:
time: 425 us; the launch traced here: 421 us
  Pallas kernels  283 us (67%)
  waiting for transfers between devices  51.2 us (12%)
  local copies, waits for them, and re-layouts  35.9 us (8%)
  between operations  13.9 us (3%)
  matrix products  13 us (3%)
  blocking collectives  11 us (3%)
  other arithmetic  7.21 us (2%)
  starting transfers between devices  5.46 us (1%)
    pallas_call x3, Pallas kernels, heads_attention(): pl.pallas_call(functools.partial(attention_kernel, head_dim, 256), grid=(...  144 us
    pallas_call x1, Pallas kernels, finish_tokens(): pl.pallas_call(functools.partial(finish_kernel, head_dim, 512), grid=(n_o...  93.9 us
    pallas_call x3, Pallas kernels, project_tokens(): pl.pallas_call(functools.partial(project_kernel, per_out), grid=(len(part...  44.6 us
    all_to_all x1, waiting for transfers between devices, local_program(): lax.all_to_all(row_major(tokens.reshape(tp_size, own // tp_size, width)),...  42.9 us
    dot_general x1, matrix products, map_tail(): jnp.dot(map_act, map_w_down, preferred_element_type=jnp.float32)  11.4 us
    all_gather x1, blocking collectives, local_program(): lax.all_gather(jnp.concatenate([pooled, total, peak], axis=-1), 'tp', axi...  11 us
    another operation x2, local copies, waits for them, and re-layouts, local_program(): map_wkv[:, index].reshape(width, width)  10.6 us
  transfers between devices with their start and end apart: 10, of which 2 were waited for; matrix products, arithmetic and copies ran while one was open for 9% of the time, Pallas kernels for 45%

profile of v9, /device:TPU:0, one launch (start us, length us, event | category | flops | bytes accessed | tf_op | source)
XLA Modules:
  0.0 420.5 jit_solution(6599905567938023198)
XLA Ops:
  6.5 1.4 slice_bitcast_fusion
  10.5 4.3 %all-to-all-start = ((bf16[8,256,1152]{2,1,0:T(8,128)(2,1)}), bf16[8,256,1152]{2,1,0:T(8,128)(2,1)}, u32[]{:S(2)}, u32[]{:S(2)}) async-start(bf16[8,256,1152]{2,1,0:T(8,128)(2,1)} %bitcast.72), calls=%async_computation | async-start | bytes 9437184 | tf_op jit(solution)/shard_map/all_to_all | solution.py:254
  15.2 5.3 %fusion.72 = (bf16[1152,1,16,72]{0,3,2,1:T(8,128)(2,1)}, bf16[1152,1,16,72]{0,3,2,1:T(8,128)(2,1)}) fusion(bf16[1152,2,16,72]{0,3,2,1:T(8,128)(2,1)} %param.46), kind=kLoop, calls=%fused_computation.123 | loop fusion | bytes 10616832 | tf_op jit(solution)/shard_map/slice | solution.py:276
  20.4 5.3 %copy.56.wk_hbm = bf16[1152,1152]{1,0:T(8,128)(2,1)} copy(bf16[1152,1152]{0,1:T(8,128)(2,1)} %bitcast.70) | data formatting | bytes 5308416 | tf_op jit(solution)/shard_map/reshape;squeeze | solution.py:276
  25.7 5.3 %copy.57.wv_hbm = bf16[1152,1152]{1,0:T(8,128)(2,1)} copy(bf16[1152,1152]{0,1:T(8,128)(2,1)} %bitcast.69) | data formatting | bytes 5308416 | tf_op jit(solution)/shard_map/reshape;squeeze | solution.py:276
  31.1 2.5 pad.48
  41.1 2.7 fusion.7
  44.4 42.9 %all-to-all-done = bf16[8,256,1152]{2,1,0:T(8,128)(2,1)} async-done(((bf16[8,256,1152]{2,1,0:T(8,128)(2,1)}), bf16[8,256,1152]{2,1,0:T(8,128)(2,1)}, u32[]{:S(2)}, u32[]{:S(2)}) %all-to-all-start) | async-done | bytes 4718624 | tf_op jit(solution)/shard_map/all_to_all | solution.py:254
  90.5 0.9 slice.114
  91.5 1.5 reshape.124.bias_ref
  93.0 12.6 %project_tokens.4.refs_1_.refs_3_.refs_7_.refs_11_ = bf16[1920,1024]{1,0:T(8,128)(2,1)} custom-call(bf16[2048,1152]{1,0:T(8,128)(2,1)} %bitcast.1.x_ref.resid_ref, f32[1,1152]{1,0:T(1,128)} %broadcast_in_dim.27.gain_ref, f32[1,1152]{1,0:T(1,128)} %broadcast_in_dim.28.shift_ref, bf16[1920,1152]{1,0:T(8,128)(2,1)} %all-gather.7.cloned.1.call-done.weight_ref, ...), custom_call_target="tpu_custom_call" | custom-call | flops 4529848320 | bytes 10715136 | tf_op jit(solution)/shard_map/project_tokens/pallas_call | solution.py:144
  105.6 12.1 %project_tokens.3.refs_0_.refs_2_.refs_6_.refs_10_ = bf16[1920,1024]{1,0:T(8,128)(2,1)} custom-call(bf16[2048,1152]{1,0:T(8,128)(2,1)} %bitcast.1.x_ref.resid_ref, f32[1,1152]{1,0:T(1,128)} %broadcast_in_dim.27.gain_ref, f32[1,1152]{1,0:T(1,128)} %broadcast_in_dim.28.shift_ref, bf16[1920,1152]{1,0:T(8,128)(2,1)} %all-gather.7.cloned.1.call-done.weight_ref, ...), custom_call_target="tpu_custom_call" | custom-call | flops 4529848320 | bytes 10715136 | tf_op jit(solution)/shard_map/project_tokens/pallas_call | solution.py:144
  118.2 6.4 %collective-permute-done.refs_4_.refs_8_.refs_12_ = bf16[1920,1024]{1,0:T(8,128)(2,1)} collective-permute-done((bf16[1920,1024]{1,0:T(8,128)(2,1)}, bf16[1920,1024]{1,0:T(8,128)(2,1)}, u32[]{:S(2)}, u32[]{:S(2)}) %collective-permute-start) | collective-permute-done | bytes 3932192 | tf_op jit(solution)/shard_map/ppermute | solution.py:292
  124.6 37.2 %heads_attention.3.refs_14_ = bf16[2,1024,2048]{2,1,0:T(8,128)(2,1)} custom-call(bf16[1920,1024]{1,0:T(8,128)(2,1)} %project_tokens.3.refs_0_.refs_2_.refs_6_.refs_10_, bf16[1920,1024]{1,0:T(8,128)(2,1)} %project_tokens.4.refs_1_.refs_3_.refs_7_.refs_11_, bf16[1920,1024]{1,0:T(8,128)(2,1)} %project_tokens.3.refs_0_.refs_2_.refs_6_.refs_10_, ...), custom_call_target="tpu_custom_call" | custom-call | flops 17179869184 | bytes 8388608 | tf_op jit(solution)/shard_map/heads_attention/pallas_call | solution.py:107
  161.8 0.9 slice.118
  162.9 1.4 reshape.123.bias_ref
  164.3 20.0 %project_tokens.5 = (bf16[1920,1024]{1,0:T(8,128)(2,1)}, bf16[1920,1024]{1,0:T(8,128)(2,1)}) custom-call(bf16[2048,1152]{1,0:T(8,128)(2,1)} %bitcast.1.x_ref.resid_ref, f32[1,1152]{1,0:T(1,128)} %broadcast_in_dim.27.gain_ref, f32[1,1152]{1,0:T(1,128)} %broadcast_in_dim.28.shift_ref, bf16[1920,1152]{1,0:T(8,128)(2,1)} %all-gather.9.cloned.1.call-done.weight_ref, ...), custom_call_target="tpu_custom_call" | custom-call | flops 4529848320 | bytes 10715136 | tf_op jit(solution)/shard_map/project_tokens/pallas_call | solution.py:144
  184.8 37.2 %heads_attention.4.refs_14_ = bf16[2,1024,2048]{2,1,0:T(8,128)(2,1)} custom-call(bf16[1920,1024]{1,0:T(8,128)(2,1)} %project_tokens.3.refs_0_.refs_2_.refs_6_.refs_10_, bf16[1920,1024]{1,0:T(8,128)(2,1)} %project_tokens.4.refs_1_.refs_3_.refs_7_.refs_11_, ...), custom_call_target="tpu_custom_call", output_to_operand_aliasing={{}: (14, {})} | custom-call | flops 17179869184 | bytes 8388608 | tf_op jit(solution)/shard_map/heads_attention/pallas_call | solution.py:107
  222.0 69.9 %heads_attention.5 = bf16[2,1024,2048]{2,1,0:T(8,128)(2,1)} custom-call(bf16[1920,1024]{1,0:T(8,128)(2,1)} %get-tuple-element.27.refs_0_.refs_2_.refs_6_.refs_10_, bf16[1920,1024]{1,0:T(8,128)(2,1)} %get-tuple-element.28.refs_1_.refs_3_.refs_7_.refs_11_, ...), custom_call_target="tpu_custom_call", output_to_operand_aliasing={{}: (14, {})} | custom-call | flops 34359738368 | bytes 8388608 | tf_op jit(solution)/shard_map/heads_attention/pallas_call | solution.py:107
  292.0 1.1 fusion.32
  293.9 93.9 %finish_tokens.1 = (f32[16,1152]{1,0:T(8,128)}, f32[16,1]{1,0:T(8,128)}, f32[16,1]{1,0:T(8,128)}) custom-call(bf16[2048,2048]{1,0:T(8,128)(2,1)} %bitcast.71, bf16[2048,1152]{1,0:T(8,128)(2,1)} %bitcast.1.x_ref.resid_ref, f32[6,1152]{1,0:T(8,128)} %stack.35.vec_ref, f32[1,4352]{1,0:T(1,128)} %broadcast_in_dim_reshape.3.up_bias_ref, ...), custom_call_target="tpu_custom_call" | custom-call | flops 61605937152 | bytes 41943040 | tf_op jit(solution)/shard_map/finish_tokens/pallas_call | solution.py:220
  387.8 0.9 fusion.14
  389.7 11.0 %all-gather = f32[128,74]{1,0:T(8,128)S(1)} all-gather(f32[16,74]{1,0:T(8,128)S(1)} %pad_maximum_fusion), channel_id=2, replica_groups=mesh['dp'=1,'tp'=8] {'tp'}, dimensions={0}, use_global_device_ids=true | all-gather | bytes 42624 | tf_op jit(solution)/shard_map/all_gather | solution.py:308
  402.3 11.4 %fusion.5 = bf16[4,1152]{1,0:T(4,128)(2,1)} fusion(f32[4,1152]{1,0:T(4,128)S(1)} %get-tuple-element.59, bf16[4304,1152]{1,0:T(8,128)(2,1)} %param.54, bf16[1152,4304]{0,1:T(8,128)(2,1)} %param.52, f32[4304]{0:T(1024)S(1)} %copy-done.8, f32[1152]{0:T(1024)S(1)} %copy-done.11, f32[1152]{0:T(1024)S(1)} %copy-done.12, f32[1152]{0:T(1024)S(1)} %copy-done.13, ...), kind=kOutput, calls=%fused_computation.9 | convolution fusion | flops 79540352 | bytes 19891552 | tf_op jit(solution)/shard_map/dot_general | solution.py:239
  (125 shorter events, 18.5 us)
Async XLA Ops:
  6.5 33.6 %copy-start = (bf16[1152,16,72]{0,2,1:T(8,128)(2,1)S(1)}, bf16[1152,16,72]{0,2,1:T(8,128)(2,1)}, u32[]{:S(2)}) copy-start(bf16[1152,16,72]{0,2,1:T(8,128)(2,1)} %param.44) | copy-start | bytes 7962628
  6.5 83.9 %all-gather.7.cloned.1.call-start = ((), (), s32[]{:S(2)}) async-start(), calls=%async_computation.1 | async-start | bytes 4976640 | tf_op jit(solution)/shard_map/all_gather | solution.py:271
  10.5 76.8 %all-to-all-start = ((bf16[8,256,1152]{2,1,0:T(8,128)(2,1)}), bf16[8,256,1152]{2,1,0:T(8,128)(2,1)}, u32[]{:S(2)}, u32[]{:S(2)}) async-start(bf16[8,256,1152]{2,1,0:T(8,128)(2,1)} %bitcast.72), calls=%async_computation | async-start | bytes 9437184 | tf_op jit(solution)/shard_map/all_to_all | solution.py:254
  14.8 147.0 %all-gather.9.cloned.1.call-start = ((), (), s32[]{:S(2)}) async-start(), calls=%async_computation.2 | async-start | bytes 4976640 | tf_op jit(solution)/shard_map/all_gather | solution.py:281
  25.7 8.0 %copy-start.5 = (bf16[2,72,1152]{2,1,0:T(8,128)(2,1)S(1)}, bf16[2,72,1152]{2,1,0:T(8,128)(2,1)}, u32[]{:S(2)}) copy-start(bf16[2,72,1152]{2,1,0:T(8,128)(2,1)} %param.33) | copy-start | bytes 995332
  31.0 7.7 %copy-start.9 = (f32[2,16,72]{2,1,0:T(8,128)S(1)}, f32[2,16,72]{2,1,0:T(8,128)}, u32[]{:S(2)}) copy-start(f32[2,16,72]{2,1,0:T(8,128)} %param.47) | copy-start | bytes 27652
  41.1 46.3 %copy-start.4 = (bf16[240,1152]{1,0:T(8,128)(2,1)}, bf16[240,1152]{1,0:T(8,128)(2,1)S(1)}, u32[]{:S(2)}) copy-start(bf16[240,1152]{1,0:T(8,128)(2,1)S(1)} %constant_dynamic-update-slice_fusion) | copy-start | bytes 1658884
  41.1 48.2 %copy-start.15 = (f32[1152]{0:T(1024)S(1)}, f32[1152]{0:T(1024)}, u32[]{:S(2)}) copy-start(f32[1152]{0:T(1024)} %param.29) | copy-start | bytes 13828
  41.1 48.8 %copy-start.16 = (f32[1152]{0:T(1024)S(1)}, f32[1152]{0:T(1024)}, u32[]{:S(2)}) copy-start(f32[1152]{0:T(1024)} %param.30) | copy-start | bytes 13828
  87.4 204.6 %all-gather.11.cloned.1.call-start = ((), (), s32[]{:S(2)}) async-start(), calls=%async_computation.3 | async-start | bytes 11280384 | tf_op jit(solution)/shard_map/all_gather | solution.py:284
  88.1 205.7 %all-gather.13.cloned.1.call-start = ((), (), s32[]{:S(2)}) async-start(), calls=%async_computation.4 | async-start | bytes 5308416 | tf_op jit(solution)/shard_map/all_gather | solution.py:282
  88.7 205.2 %all-gather.15.cloned.1.call-start = ((), (), s32[]{:S(2)}) async-start(), calls=%async_computation.5 | async-start | bytes 11280384 | tf_op jit(solution)/shard_map/all_gather | solution.py:283
  105.6 12.5 %collective-permute-start.1 = (bf16[1920,1024]{1,0:T(8,128)(2,1)}, bf16[1920,1024]{1,0:T(8,128)(2,1)}, u32[]{:S(2)}, u32[]{:S(2)}) collective-permute-start(bf16[1920,1024]{1,0:T(8,128)(2,1)} %project_tokens.4.refs_1_.refs_3_.refs_7_.refs_11_), channel_id=1, source_target_pairs={{0,1},{1,0},{2,3},{3,2},{4,5},{5,4},{6,7},{7,6}} | collective-permute-start | bytes 11796488 | tf_op jit(solution)/shard_map/ppermute | solution.py:292
  117.7 6.9 %collective-permute-start = (bf16[1920,1024]{1,0:T(8,128)(2,1)}, bf16[1920,1024]{1,0:T(8,128)(2,1)}, u32[]{:S(2)}, u32[]{:S(2)}) collective-permute-start(bf16[1920,1024]{1,0:T(8,128)(2,1)} %project_tokens.3.refs_0_.refs_2_.refs_6_.refs_10_), channel_id=1, source_target_pairs={{0,1},{1,0},{2,3},{3,2},{4,5},{5,4},{6,7},{7,6}} | collective-permute-start | bytes 11796488 | tf_op jit(solution)/shard_map/ppermute | solution.py:292
  184.3 37.7 %collective-permute-start.2 = (bf16[1920,1024]{1,0:T(8,128)(2,1)}, bf16[1920,1024]{1,0:T(8,128)(2,1)}, u32[]{:S(2)}, u32[]{:S(2)}) collective-permute-start(bf16[1920,1024]{1,0:T(8,128)(2,1)} %get-tuple-element.27.refs_0_.refs_2_.refs_6_.refs_10_), channel_id=1, source_target_pairs={{0,1},{1,0},{2,3},{3,2},{4,5},{5,4},{6,7},{7,6}} | collective-permute-start | bytes 11796488 | tf_op jit(solution)/shard_map/ppermute | solution.py:292
  184.6 37.4 %collective-permute-start.3 = (bf16[1920,1024]{1,0:T(8,128)(2,1)}, bf16[1920,1024]{1,0:T(8,128)(2,1)}, u32[]{:S(2)}, u32[]{:S(2)}) collective-permute-start(bf16[1920,1024]{1,0:T(8,128)(2,1)} %get-tuple-element.28.refs_1_.refs_3_.refs_7_.refs_11_), channel_id=1, source_target_pairs={{0,1},{1,0},{2,3},{3,2},{4,5},{5,4},{6,7},{7,6}} | collective-permute-start | bytes 11796488 | tf_op jit(solution)/shard_map/ppermute | solution.py:292
  293.8 94.0 %copy-start.7 = (s32[1152]{0:T(1024)S(1)}, s32[1152]{0:T(1024)}, u32[]{:S(2)}) copy-start(s32[1152]{0:T(1024)} %copy-done.6) | copy-start | bytes 13828
  293.8 107.4 %copy-start.2 = (bf16[16,72,1152]{2,1,0:T(8,128)(2,1)S(1)}, bf16[16,72,1152]{2,1,0:T(8,128)(2,1)}, u32[]{:S(2)}) copy-start(bf16[16,72,1152]{2,1,0:T(8,128)(2,1)} %param.48) | copy-start | bytes 7962628
  293.9 107.4 %copy-start.10 = (f32[1152]{0:T(1024)S(1)}, f32[1152]{0:T(1024)}, u32[]{:S(2)}) copy-start(f32[1152]{0:T(1024)} %param.49) | copy-start | bytes 13828
  387.8 14.5 %copy-start.8 = (f32[4304]{0:T(1024)S(1)}, f32[4304]{0:T(1024)}, u32[]{:S(2)}) copy-start(f32[4304]{0:T(1024)} %param.53) | copy-start | bytes 51652
  387.8 14.5 %copy-start.11 = (f32[1152]{0:T(1024)S(1)}, f32[1152]{0:T(1024)}, u32[]{:S(2)}) copy-start(f32[1152]{0:T(1024)} %param.55) | copy-start | bytes 13828
  387.8 14.5 %copy-start.12 = (f32[1152]{0:T(1024)S(1)}, f32[1152]{0:T(1024)}, u32[]{:S(2)}) copy-start(f32[1152]{0:T(1024)} %param.51) | copy-start | bytes 13828
  387.8 14.5 %copy-start.13 = (f32[1152]{0:T(1024)S(1)}, f32[1152]{0:T(1024)}, u32[]{:S(2)}) copy-start(f32[1152]{0:T(1024)} %param.50) | copy-start | bytes 13828
  402.3 11.4 %copy-start.1 = (bf16[1152,16,72]{0,2,1:T(8,128)(2,1)S(1)}, bf16[1152,16,72]{0,2,1:T(8,128)(2,1)}, u32[]{:S(2)}) copy-start(bf16[1152,16,72]{0,2,1:T(8,128)(2,1)} %param.44) | copy-start | bytes 7962628
  (5 other events, 19.7 us)
Sparse Core Ops, SparseCore 0:
  10.6 64.0 all-gather.6
  87.5 31.6 all-gather.8
  121.0 55.7 all-gather.10
  178.4 32.9 all-gather.12
  213.1 55.5 all-gather.14
